TPU v7x, 32 devices: a whole 2x2x4 slice. The times are simulated.
32 devices in a mesh: rows: 4 (over z), cols: 8 (over y, x, core).
Axes of the slice: x: 2, y: 2, z: 4, core: 2. Of those that a mesh axis runs over, the one named last changes fastest.
Arguments:
- features: bfloat16 [65536, 440], P(('rows', 'cols')), may hold values from -12 to 12
- residual: float32 [65536, 147], P(('rows', 'cols')), may hold values from -6 to 6
- coeffs: float32 [65536, 147], P(('rows', 'cols')), may hold values from -3 to 3
- block_inverse: float32 [2, 2048, 2048], P(None, ('rows', 'cols')), may hold values from -0.0234375 to 0.0234375
- block_index: int32 [2, 2048], P(None, 'cols'), may hold values from 0 to 2047, as said below
- owners: int32 [2], replicated, may hold values from 0 to 3
Outputs:
- new_coeffs: float32 [65536, 147], P(('rows', 'cols'))
- new_residual: float32 [65536, 147], P(('rows', 'cols'))
Inputs may be any that keep to these rules, and one draw needn't show every extreme that they name: `block_index`: for each step and each aligned run of 256 positions, the indices are distinct.
All inputs are finite; a program needn't handle non-finite values.
Results may differ from a plain program's by a relative error of at most 0.0028.
Values may be sent and summed in bfloat16 or wider, within the bound.
No kernel may reach another device: no remote copies, remote signals or barrier semaphores. Data moves between devices by JAX's collectives and lax.ppermute only.
A program may use at most 64 MiB of HBM per device.

v0:
```python
import jax
import jax.numpy as jnp
from jax import lax
from jax.experimental import pallas as pl
from jax.experimental.pallas import tpu as pltpu
from jax.sharding import PartitionSpec as P


penalty = 0.5
LANES = 128
VMEM = pltpu.MemorySpace.VMEM
SMEM = pltpu.MemorySpace.SMEM
f32 = jnp.float32
bf16 = jnp.bfloat16
f16 = jnp.float16
MM = dict(preferred_element_type=f32)


def up(value, unit):
    return -(-value // unit) * unit


def params(megabytes=20):
    return pltpu.CompilerParams(vmem_limit_bytes=megabytes * 1024 * 1024)


def split(value, parts):
    pieces = []
    for _ in range(parts - 1):
        high = value.astype(bf16)
        pieces.append(high)
        value = value - high.astype(f32)
    pieces.append(value.astype(bf16))
    return pieces


def matmul(a, b):
    return lax.dot_general(a, b, (((1,), (0,)), ((), ())), **MM)


def matmul_nt(a, b):
    return lax.dot_general(a, b, (((1,), (1,)), ((), ())), **MM)


def one_hot(frames, index_row):
    rows = lax.broadcasted_iota(jnp.int32, (frames, index_row.shape[1]), 0)
    return jnp.where(rows == index_row, 1.0, 0.0).astype(bf16)


def turn(row):
    square = jnp.broadcast_to(row.astype(f32), (LANES, row.shape[1]))
    return jnp.transpose(square)[:, 0:1].astype(jnp.int32)


def padded(value, rows):
    return jnp.pad(value, ((0, rows - value.shape[0]), (0, 0)))


vmem = pl.BlockSpec(memory_space=VMEM)
smem = pl.BlockSpec(memory_space=SMEM)


def pick_residual(index, residual_t):
    outputs, frames = residual_t.shape
    rows = up(outputs, 16)
    picks = index.shape[1]

    def body(index_ref, residual_ref, first_ref):
        high, low = split(padded(residual_ref[...], rows), 2)
        first = matmul(jnp.concatenate([high, low], 0), one_hot(frames, index_ref[0:1, :]))
        first_ref[...] = first[:rows] + first[rows:]

    return pl.pallas_call(
        body,
        in_specs=[vmem, vmem],
        out_specs=vmem,
        out_shape=jax.ShapeDtypeStruct((rows, picks), f32),
        compiler_params=params(),
        name="pick_residual",
    )(index, residual_t)


def norm_rows(squares, kinds):
    width = squares.shape[1]
    norm = split(-0.5 * squares, 3)
    ones = jnp.ones((3, width), bf16)
    zeros = jnp.zeros((6, width), bf16)
    norm = jnp.concatenate(norm, 0)
    pieces = []
    for kind in kinds:
        if kind == 0:
            pieces.append(zeros)
        elif kind == 1:
            pieces.append(jnp.concatenate([norm, ones], 0))
        else:
            pieces.append(jnp.concatenate([ones, norm], 0))
    return jnp.concatenate(pieces, 0)


def pick_features(owners, index, features_t, residual_t):
    width, frames = features_t.shape
    outputs = residual_t.shape[0]
    depth = up(width + 20, 16)
    picks = index.shape[1]
    rows = up(outputs, 16)
    tail = depth - width

    def body(owners_ref, index_ref, features_ref, residual_ref, local_ref, first_ref, second_ref):
        features = features_ref[...]
        hot = one_hot(frames, index_ref[0:1, :])
        picked = matmul(features, hot)
        picked_squares = jnp.sum(picked * picked, axis=0, keepdims=True)
        first_ref[0:width, :] = picked.astype(bf16)
        rest = jnp.zeros((tail - 18, picks), bf16)
        first_ref[width:depth, :] = jnp.concatenate([norm_rows(picked_squares, (2, 0, 1)), rest], 0)

        hot = one_hot(frames, index_ref[1:2, :])
        picked = matmul(features, hot)
        picked_squares = jnp.sum(picked * picked, axis=0, keepdims=True)
        second_ref[0:width, :] = picked.astype(bf16)
        places = lax.broadcasted_iota(jnp.int32, (picks, picks), 0) + 1
        meet = jnp.where(turn(index_ref[0:1, :]) == index_ref[1:2, :], places, 0)
        place = jnp.max(meet, axis=0, keepdims=True)
        place = jnp.where(owners_ref[0] == owners_ref[1], place, 0)
        place = jnp.concatenate([place // LANES, place % LANES], 0).astype(f32).astype(bf16)
        rest = jnp.zeros((tail - 20, picks), bf16)
        second_ref[width:depth, :] = jnp.concatenate([norm_rows(picked_squares, (0, 2, 2)), place, rest], 0)
        high, low = split(padded(residual_ref[...], rows), 2)
        second_ref[depth:, :] = matmul(jnp.concatenate([high, low], 0), hot).astype(bf16)

        wide = features.astype(f32)
        squares = jnp.sum(wide * wide, axis=0, keepdims=True)
        local_ref[0:width, :] = features
        rest = jnp.zeros((tail - 18, frames), bf16)
        local_ref[width:depth, :] = jnp.concatenate([norm_rows(squares, (1, 1, 0)), rest], 0)

    return pl.pallas_call(
        body,
        in_specs=[smem, vmem, vmem, vmem],
        out_specs=(vmem, vmem, vmem),
        out_shape=(
            jax.ShapeDtypeStruct((depth, frames), bf16),
            jax.ShapeDtypeStruct((depth, picks), bf16),
            jax.ShapeDtypeStruct((depth + 2 * rows, picks), bf16),
        ),
        compiler_params=params(),
        name="pick_features",
    )(owners, index, features_t, residual_t)


def lane_start(value, unit):
    return pl.ds(pl.multiple_of(value * unit, unit), unit)


def piece_col(piece):
    mine = lax.axis_index("cols")
    return ((mine // 2) ^ (piece // 2)) * 2 + ((mine % 2) ^ (piece % 2))


def fold(update):
    half = update.shape[0] // 2
    return jnp.concatenate([update[:half], update[half:]], 1).astype(bf16)


def stack_inverse(inverse_ref, picks, stacked):
    for k in range(stacked.shape[1] // picks):
        high, low = split(inverse_ref[0, :, lane_start(piece_col(k), picks)], 2)
        stacked[:, k * picks : (k + 1) * picks] = jnp.concatenate([high, low], 0)


def first_update(picked, inverse, step, picks):
    rows, block = picked.shape
    mine = inverse.shape[1]

    def body(inverse_ref, picked_ref, out_ref, stacked):
        stack_inverse(inverse_ref, picks, stacked)
        product = matmul_nt(jnp.concatenate(split(picked_ref[...], 2), 0), stacked[...])
        product = product[:rows] + product[rows:]
        out_ref[...] = fold(product[:, :mine] + product[:, mine:])

    return pl.pallas_call(
        body,
        grid=(1,),
        in_specs=[pl.BlockSpec((1, mine, block), lambda i: (step, 0, 0)), vmem],
        out_specs=vmem,
        out_shape=jax.ShapeDtypeStruct((rows // 2, 2 * mine), bf16),
        scratch_shapes=[pltpu.VMEM((2 * mine, block), bf16)],
        compiler_params=params(),
        name="first_update",
    )(inverse, picked)


def second_operator(first, second, inverse, step, width, scale):
    depth, picks = first[0].shape
    count = len(first)
    block = picks * count
    mine = inverse.shape[1]
    rows = (second[0].shape[0] - depth) // 2
    wide = 2 * picks

    def body(inverse_ref, *refs):
        first_ref, second_ref = refs[:count], refs[count : 2 * count]
        operator_ref, base_ref, turned, stacked, kernel, meet = refs[2 * count :]
        stack_inverse(inverse_ref, picks, stacked)
        for k in range(count):
            turned[k * picks : (k + 1) * picks, :] = jnp.transpose(second_ref[k][0:depth, :])
        base = jnp.zeros((2 * rows, 2 * mine), f32)
        lanes = lax.broadcasted_iota(jnp.int32, (picks, picks), 1) + 1
        for k in range(count):
            base = base + matmul_nt(second_ref[k][depth:, :], stacked[:, k * picks : (k + 1) * picks])
            place = turned[k * picks : (k + 1) * picks, width + 18 : width + 20].astype(f32)
            place = (place[:, 0:1] * LANES + place[:, 1:2]).astype(jnp.int32)
            meet[k * picks : (k + 1) * picks, :] = jnp.where(place == lanes, penalty, 0.0).astype(bf16)
        for n in range(0, count, 2):
            columns = jnp.concatenate([first_ref[n][...], first_ref[n + 1][...]], 1)
            for k in range(count):
                here = slice(k * picks, (k + 1) * picks)
                inner = matmul(turned[here, :], columns)
                kernel[here, :] = jnp.exp2(inner * scale).astype(bf16)
            for k in (n, n + 1):
                here = slice(k * picks, (k + 1) * picks)
                there = slice((k - n) * picks, (k - n + 1) * picks)
                kernel[here, there] = kernel[here, there] + meet[here, :]
            product = matmul(stacked[...], kernel[...])
            high, low = split(product[0:mine, :] + product[mine:, :], 2)
            operator_ref[0:mine, n * picks : n * picks + wide] = high
            operator_ref[mine:, n * picks : n * picks + wide] = low
        base = base[:rows] + base[rows:]
        base_ref[...] = base[:, :mine] + base[:, mine:]

    flops = 2 * block * block * (depth + 2 * mine)
    return pl.pallas_call(
        body,
        grid=(1,),
        in_specs=[pl.BlockSpec((1, mine, block), lambda i: (step, 0, 0))] + [vmem] * (2 * count),
        out_specs=(vmem, vmem),
        out_shape=(
            jax.ShapeDtypeStruct((2 * mine, block), bf16),
            jax.ShapeDtypeStruct((rows, mine), f32),
        ),
        scratch_shapes=[
            pltpu.VMEM((block, depth), bf16),
            pltpu.VMEM((2 * mine, block), bf16),
            pltpu.VMEM((block, wide), bf16),
            pltpu.VMEM((block, picks), bf16),
        ],
        cost_estimate=pl.CostEstimate(flops=flops, transcendentals=block * block, bytes_accessed=10**7),
        compiler_params=params(),
        name="second_operator",
    )(inverse, *first, *second)


def block_kernel(pieces, local, scale):
    depth, frames = local.shape
    picks = pieces[0].shape[1]
    count = len(pieces)
    block = picks * count
    tile = min(512, frames)

    def body(local_ref, *refs):
        pieces_ref, out_ref, turned = refs[:count], refs[-2], refs[-1]

        @pl.when(pl.program_id(0) == 0)
        def _():
            for k in range(count):
                turned[k * picks : (k + 1) * picks, :] = jnp.transpose(pieces_ref[k][0:depth, :])

        for k in range(count):
            here = slice(k * picks, (k + 1) * picks)
            inner = matmul(turned[here, :], local_ref[...])
            out_ref[here, :] = jnp.exp2(inner * scale).astype(bf16)

    return pl.pallas_call(
        body,
        grid=(frames // tile,),
        in_specs=[pl.BlockSpec((depth, tile), lambda i: (0, i))] + [vmem] * count,
        out_specs=pl.BlockSpec((block, tile), lambda i: (0, i)),
        out_shape=jax.ShapeDtypeStruct((block, frames), bf16),
        scratch_shapes=[pltpu.VMEM((block, depth), bf16)],
        cost_estimate=pl.CostEstimate(
            flops=2 * block * frames * depth, transcendentals=block * frames, bytes_accessed=10**7
        ),
        compiler_params=params(),
    )(local, *pieces)


def unfold(pieces_ref, parts, picks, canon):
    half, width = pieces_ref[0].shape[0] // parts, pieces_ref[0].shape[1]
    mine = width // 2
    count = len(pieces_ref)
    lanes = lax.broadcasted_iota(jnp.int32, (half, width), 1)
    low = lanes < mine
    row, col = lax.axis_index("rows"), lax.axis_index("cols")
    core = col % 2
    for k in range(0, count, 2):
        for r in range(parts):
            here = pieces_ref[k][r * half : (r + 1) * half, :].astype(f32)
            other = pieces_ref[k + 1][r * half : (r + 1) * half, :].astype(f32)
            a = jnp.where(core == 0, here, other)
            b = jnp.where(core == 0, other, here)
            upper = jnp.where(low, a, pltpu.roll(b, mine, 1))
            lower = jnp.where(low, pltpu.roll(a, mine, 1), b)
            pair = (row ^ r) * (count // 2) + ((col // 2) ^ (k // 2))
            from_col = pair * width // picks
            place = ((from_col // 2) ^ (col // 2)) * 2 + ((from_col % 2) ^ core)
            place = pl.ds(pl.multiple_of(place * picks + pair * width % picks, width), width)
            canon[0:half, place] = upper.astype(bf16)
            canon[half:, place] = lower.astype(bf16)


def second_update(pieces, operator, base, picks):
    rows, mine = base.shape
    block = operator.shape[1]
    count = len(pieces)

    def body(operator_ref, base_ref, *refs):
        pieces_ref, out_ref, canon = refs[:count], refs[-2], refs[-1]
        unfold(pieces_ref, pieces[0].shape[0] * 2 // rows, picks, canon)
        product = matmul_nt(canon[...], operator_ref[...])
        out_ref[...] = fold(base_ref[...] - (product[:, :mine] + product[:, mine:]))

    return pl.pallas_call(
        body,
        in_specs=[vmem] * (2 + count),
        out_specs=vmem,
        out_shape=jax.ShapeDtypeStruct((rows // 2, 2 * mine), bf16),
        scratch_shapes=[pltpu.VMEM((rows, block), bf16)],
        compiler_params=params(),
        name="second_update",
    )(operator, base, *pieces)


def apply_update(owners, pieces, kernel, index, step, residual_t, coeffs_t):
    outputs, frames = residual_t.shape
    block = kernel.shape[0]
    picks = index.shape[1]
    count = len(pieces)
    rows = up(outputs, 16)
    tile = min(512, frames)

    def body(owners_ref, index_ref, kernel_ref, residual_ref, coeffs_ref, *refs):
        pieces_ref = refs[:count]
        new_residual_ref, new_coeffs_ref, canon, own = refs[count:]
        here = pl.program_id(0)

        @pl.when(here == 0)
        def _():
            unfold(pieces_ref, pieces[0].shape[0] * 2 // rows, picks, canon)
            mine = canon[:, 0:picks]
            own[...] = jnp.where(lax.axis_index("rows") == owners_ref[step], mine, jnp.zeros_like(mine))

        change = matmul(canon[...], kernel_ref[...])
        frame = lax.broadcasted_iota(jnp.int32, (tile, picks), 0) + here * tile
        hot = jnp.where(frame == index_ref[step : step + 1, :], 1.0, 0.0).astype(bf16)
        put = matmul_nt(own[...], hot)
        new_residual_ref[...] = residual_ref[...] - (change + penalty * put)[:outputs]
        new_coeffs_ref[...] = coeffs_ref[...] + put[:outputs]

    strip = pl.BlockSpec((outputs, tile), lambda i: (0, i))
    return pl.pallas_call(
        body,
        grid=(frames // tile,),
        in_specs=[smem, vmem, pl.BlockSpec((block, tile), lambda i: (0, i)), strip, strip] + [vmem] * count,
        out_specs=(strip, strip),
        out_shape=(
            jax.ShapeDtypeStruct((outputs, frames), f32),
            jax.ShapeDtypeStruct((outputs, frames), f32),
        ),
        scratch_shapes=[pltpu.VMEM((rows, block), bf16), pltpu.VMEM((rows, picks), bf16)],
        cost_estimate=pl.CostEstimate(
            flops=2 * rows * block * frames, transcendentals=0, bytes_accessed=2 * block * frames
        ),
        compiler_params=params(),
    )(owners, index, kernel, residual_t, coeffs_t, *pieces)


class Sender:
    def __init__(self, rows, cols):
        self.rows, self.cols, self.chips = rows, cols, cols // 2
        self.row = lax.axis_index("rows")

    def send(self, value, row=None, chip_step=0, core_step=0):
        pairs = []
        for i in range(self.rows * self.cols):
            at, col = i // self.cols, i % self.cols
            to = at if row is None else row(at)
            if to is None:
                continue
            col = ((col // 2) ^ chip_step) * 2 + ((col % 2) ^ core_step)
            pairs.append((i, to * self.cols + col))
        return lax.ppermute(value, ("rows", "cols"), pairs)

    def doubling(self, value, owner):
        step = 1
        while step < self.rows:
            other = self.send(value, row=lambda at, step=step: at ^ step)
            value = jnp.where(((owner ^ self.row) & step) != 0, other, value)
            step *= 2
        return value

    def along(self, value, owner):
        count, row = self.rows, self.row
        half = count // 2
        lower = row < half
        moves = []
        for s in range(half - 1):
            moves.append((s, {s: s + 1, count - 1 - s: count - 2 - s}))
        moves.append((None, {half - 1: half, half: half - 1}))
        for s in reversed(range(half - 1)):
            moves.append((~s, {s + 1: s, count - 2 - s: count - 1 - s}))
        for s, move in moves:
            other = self.send(value, row=move.get)
            if s is None:
                take = ((row == half - 1) & (owner >= half)) | ((row == half) & (owner < half))
            elif s >= 0:
                take = ((row == s + 1) & (owner <= s)) | ((row == count - 2 - s) & (owner >= count - 1 - s))
            else:
                s = ~s
                take = ((row == s) & (owner > s)) | ((row == count - 1 - s) & (owner < count - 1 - s))
            value = jnp.where(take, other, value)
        return value

    def over_rows(self, value):
        steps = sorted(range(1, self.rows), key=lambda k: -k)
        got = {k: self.send(value, row=lambda at, k=k: at ^ k) for k in steps}
        return [value] + [got[k] for k in range(1, self.rows)]

    def over_cols(self, value):
        found = []
        for k in range(self.chips):
            mine = value if k == 0 else self.send(value, chip_step=k)
            found += [mine, self.send(mine, core_step=1)]
        return found


def per_device_pieces(rows, cols, features, residual, coeffs, block_inverse, block_index, owners):
    scale = 2.0 / features.shape[1] * 1.4426950408889634
    sender = Sender(rows, cols)
    width, picks = features.shape[1], block_index.shape[1]
    features_t, residual_t, coeffs_t = features.T, residual.T, coeffs.T
    first = pick_residual(block_index, residual_t)
    first = sender.over_cols(sender.doubling(first.astype(f16), owners[0]))
    local, first_block, second_block = pick_features(owners, block_index, features_t, residual_t)
    first_block = sender.over_cols(sender.along(first_block, owners[0]))
    second_block = sender.over_cols(sender.along(second_block, owners[1]))
    update = first_update(jnp.concatenate(first, 1).astype(f32), block_inverse, 0, picks)
    update = sender.over_cols(jnp.concatenate(sender.over_rows(update), 0))
    first_kernel = block_kernel(first_block, local, scale)
    operator, base = second_operator(first_block, second_block, block_inverse, 1, width, scale)
    later = second_update(update, operator, base, picks)
    later = sender.over_cols(jnp.concatenate(sender.over_rows(later), 0))
    second_kernel = block_kernel(second_block, local, scale)
    residual_t, coeffs_t = apply_update(
        owners, update, first_kernel, block_index, 0, residual_t, coeffs_t
    )
    residual_t, coeffs_t = apply_update(
        owners, later, second_kernel, block_index, 1, residual_t, coeffs_t
    )
    return (coeffs_t.T, residual_t.T)


def from_root(value, axis, source):
    kept = jnp.where(lax.axis_index(axis) == source, value, 0).astype(value.dtype)
    return lax.psum(kept, axis)


def per_device_plain(features, residual, coeffs, block_inverse, block_index, owners):
    frame_count = features.shape[0]
    feature_width = features.shape[1]
    per_col = block_index.shape[1]
    row_block = min(512, frame_count)
    exponent = -1.0 / feature_width
    my_row = lax.axis_index("rows")
    my_col = lax.axis_index("cols")
    squares = jnp.sum(jnp.square(features.astype(jnp.float32)), axis=1)
    feature_blocks = features.reshape(frame_count // row_block, row_block, feature_width)
    norm_blocks = squares.reshape(frame_count // row_block, row_block)
    for step_id in range(block_index.shape[0]):
        chosen_rows = block_index[step_id]
        owner_row = owners[step_id]
        mine_feat = jnp.take(features, chosen_rows, axis=0)
        mine_res = jnp.take(residual, chosen_rows, axis=0)
        row_piece = from_root(mine_feat, "rows", owner_row)
        chosen = lax.all_gather(row_piece, "cols", axis=0, tiled=True)
        res_piece = from_root(mine_res, "rows", owner_row)
        picked_res = lax.all_gather(res_piece, "cols", axis=0, tiled=True)
        my_update = jnp.dot(
            block_inverse[step_id],
            picked_res,
            precision=lax.Precision.HIGHEST,
            preferred_element_type=jnp.float32,
        ).astype(jnp.bfloat16)
        update = lax.all_gather(my_update, ("rows", "cols"), axis=0, tiled=True)
        chosen_norms = jnp.sum(jnp.square(chosen.astype(jnp.float32)), axis=1)

        def kernel_rows(operands):
            block_rows, block_norms = operands
            inner = lax.dot_general(
                block_rows, chosen, (((1,), (1,)), ((), ())), preferred_element_type=jnp.float32
            )
            distance = block_norms[:, None] + chosen_norms[None, :] - 2.0 * inner
            kernel = jnp.exp(distance * exponent).astype(jnp.bfloat16)
            return jnp.dot(kernel, update, preferred_element_type=jnp.float32)

        change = lax.map(kernel_rows, (feature_blocks, norm_blocks)).reshape(frame_count, -1)
        residual = residual - change
        is_owner = jnp.where(my_row == owner_row, 1.0, 0.0).astype(jnp.float32)
        mine_update = (
            lax.dynamic_slice_in_dim(update, my_col * per_col, per_col, 0).astype(jnp.float32)
            * is_owner
        )
        residual = residual.at[chosen_rows].add(-penalty * mine_update)
        coeffs = coeffs.at[chosen_rows].add(mine_update)
    return (coeffs, residual)


def power_of_two(value):
    return value & (value - 1) == 0


def solution(mesh):
    rows, cols = mesh.shape["rows"], mesh.shape["cols"]
    in_specs = (
        P(("rows", "cols"), None),
        P(("rows", "cols"), None),
        P(("rows", "cols"), None),
        P(None, ("rows", "cols"), None),
        P(None, "cols"),
        P(),
    )
    out_specs = (P(("rows", "cols"), None), P(("rows", "cols"), None))

    def per_device(features, residual, coeffs, block_inverse, block_index, owners):
        args = (features, residual, coeffs, block_inverse, block_index, owners)
        return per_device_pieces(rows, cols, *args) if fits(*args) else per_device_plain(*args)

    def fits(features, residual, coeffs, block_inverse, block_index, owners):
        return (
            small
            and block_index.shape[0] == 2
            and block_index.shape[1] % LANES == 0
            and 2 * block_inverse.shape[1] == LANES
            and features.shape[0] % 512 == 0
        )

    small = power_of_two(rows) and power_of_two(cols) and 2 <= rows <= 8 and 4 <= cols <= 16
    return jax.shard_map(
        per_device, mesh=mesh, in_specs=in_specs, out_specs=out_specs, check_vma=False
    )
```

profile of v0, /device:TPU:0, one launch (start us, length us, event | category | flops | bytes accessed | tf_op | source)
XLA Modules:
  0.0 136.6 jit_solution(10646258506237952430)
XLA Ops:
  0.7 1.3 copy-done
  1.9 0.7 copy-done.5
  2.6 0.6 pick_residual.1
  3.2 3.1 %collective-permute-start.20 = (f16[160,256]{1,0:T(8,128)(2,1)S(1)}, f16[160,256]{1,0:T(8,128)(2,1)S(1)}, u32[]{:S(2)}, u32[]{:S(2)}) collective-permute-start(f16[160,256]{1,0:T(8,128)(2,1)S(1)} %convert_element_type.6), channel_id=1, source_target_pairs={{0,8},{1,9},{2,10},{3,11},{4,12},{5,13},{6,14},{7,15},{8,0},{9,1},... | collective-permute-start | bytes 245768 | tf_op jit(solution)/shard_map/ppermute | solution.py:391
  6.3 0.6 fusion
  7.6 1.2 collective-permute-done.20
  8.8 3.1 %collective-permute-start.21 = (f16[160,256]{1,0:T(8,128)(2,1)S(1)}, f16[160,256]{1,0:T(8,128)(2,1)S(1)}, u32[]{:S(2)}, u32[]{:S(2)}) collective-permute-start(f16[160,256]{1,0:T(8,128)(2,1)S(1)} %broadcast_select_fusion.6), channel_id=1, source_target_pairs={{0,16},{1,17},{2,18},{3,19},{4,20},{5,21},{6,22},{7,23},{8,24},{9,... | collective-permute-start | bytes 245768 | tf_op jit(solution)/shard_map/ppermute | solution.py:391
  11.9 1.5 %copy-done.2 = bf16[2048,440]{0,1:T(8,128)(2,1)S(1)} copy-done((bf16[2048,440]{0,1:T(8,128)(2,1)S(1)}, bf16[2048,440]{0,1:T(8,128)(2,1)}, u32[]{:S(2)}) %copy-start.2) | copy-done | bytes 1802264
  13.4 2.1 %pick_features.1 = (bf16[464,2048]{1,0:T(8,128)(2,1)S(1)}, bf16[464,256]{1,0:T(8,128)(2,1)S(1)}, bf16[784,256]{1,0:T(8,128)(2,1)S(1)}) custom-call(s32[2]{0:T(128)S(1)} %copy-done.7, s32[2,256]{1,0:T(2,128)S(1)} %copy-done.6, bf16[440,2048]{1,0:T(8,128)(2,1)S(1)} %bitcast.15, f32[147,2048]{1,0:T(8,128)S(1)} %bitcast.13), custom_call_target="tpu_custom_call" | custom-call | tf_op jit(solution)/shard_map/pick_features/pallas_call | solution.py:137
  15.5 1.3 copy-done.8
  16.8 3.5 %collective-permute-start.10 = (bf16[464,256]{1,0:T(8,128)(2,1)S(1)}, bf16[464,256]{1,0:T(8,128)(2,1)S(1)}, u32[]{:S(2)}, u32[]{:S(2)}) collective-permute-start(bf16[464,256]{1,0:T(8,128)(2,1)S(1)} %get-tuple-element.13), channel_id=1, source_target_pairs={{0,8},{1,9},{2,10},{3,11},{4,12},{5,13},{6,14},{7,15},{24,16},{25,... | collective-permute-start | bytes 712712 | tf_op jit(solution)/shard_map/ppermute | solution.py:391
  20.3 1.3 collective-permute-start
  26.9 1.6 %collective-permute-start.23 = (f16[160,256]{1,0:T(8,128)(2,1)S(1)}, f16[160,256]{1,0:T(8,128)(2,1)S(1)}, u32[]{:S(2)}, u32[]{:S(2)}) collective-permute-start(f16[160,256]{1,0:T(8,128)(2,1)S(1)} %get-tuple-element.21), channel_id=1, source_target_pairs={{0,2},{1,3},{2,0},{3,1},{4,6},{5,7},{6,4},{7,5},{8,10},{9,11},{10,... | collective-permute-start | bytes 245768 | tf_op jit(solution)/shard_map/ppermute | solution.py:391
  28.5 1.5 %collective-permute-start.25 = (f16[160,256]{1,0:T(8,128)(2,1)S(1)}, f16[160,256]{1,0:T(8,128)(2,1)S(1)}, u32[]{:S(2)}, u32[]{:S(2)}) collective-permute-start(f16[160,256]{1,0:T(8,128)(2,1)S(1)} %get-tuple-element.21), channel_id=1, source_target_pairs={{0,4},{1,5},{2,6},{3,7},{4,0},{5,1},{6,2},{7,3},{8,12},{9,13},{10,... | collective-permute-start | bytes 245768 | tf_op jit(solution)/shard_map/ppermute | solution.py:391
  30.0 0.5 collective-permute-start.27
  30.5 0.7 collective-permute-start.11
  31.2 0.6 collective-permute-done.23
  31.8 2.0 %collective-permute-done.25 = f16[160,256]{1,0:T(8,128)(2,1)S(1)} collective-permute-done((f16[160,256]{1,0:T(8,128)(2,1)S(1)}, f16[160,256]{1,0:T(8,128)(2,1)S(1)}, u32[]{:S(2)}, u32[]{:S(2)}) %collective-permute-start.25) | collective-permute-done | bytes 81952 | tf_op jit(solution)/shard_map/ppermute | solution.py:391
  33.8 1.5 %collective-permute-done.27 = f16[160,256]{1,0:T(8,128)(2,1)S(1)} collective-permute-done((f16[160,256]{1,0:T(8,128)(2,1)S(1)}, f16[160,256]{1,0:T(8,128)(2,1)S(1)}, u32[]{:S(2)}, u32[]{:S(2)}) %collective-permute-start.27) | collective-permute-done | bytes 81952 | tf_op jit(solution)/shard_map/ppermute | solution.py:391
  35.6 0.7 collective-permute-start.1
  36.4 1.3 collective-permute-start.12
  37.7 1.6 %collective-permute-start.2 = (bf16[784,256]{1,0:T(8,128)(2,1)S(1)}, bf16[784,256]{1,0:T(8,128)(2,1)S(1)}, u32[]{:S(2)}, u32[]{:S(2)}) collective-permute-start(bf16[784,256]{1,0:T(8,128)(2,1)S(1)} %broadcast_select_fusion.1), channel_id=1, source_target_pairs={{8,0},{9,1},{10,2},{11,3},{12,4},{13,5},{14,6},{15,7},{16,24},{17,... | collective-permute-start | bytes 1204232 | tf_op jit(solution)/shard_map/ppermute | solution.py:391
  39.5 0.7 first_update.1
  40.2 10.9 %collective-permute-start.29 = (bf16[80,128]{1,0:T(8,128)(2,1)S(1)}, bf16[80,128]{1,0:T(8,128)(2,1)S(1)}, u32[]{:S(2)}, u32[]{:S(2)}) collective-permute-start(bf16[80,128]{1,0:T(8,128)(2,1)S(1)} %first_update.1), channel_id=1, source_target_pairs={{0,8},{1,9},{2,10},{3,11},{4,12},{5,13},{6,14},{7,15},{8,0},{9,1},... | collective-permute-start | bytes 61448 | tf_op jit(solution)/shard_map/ppermute | solution.py:391
  51.1 1.1 collective-permute-start.30
  52.2 1.4 %collective-permute-start.31 = (bf16[80,128]{1,0:T(8,128)(2,1)S(1)}, bf16[80,128]{1,0:T(8,128)(2,1)S(1)}, u32[]{:S(2)}, u32[]{:S(2)}) collective-permute-start(bf16[80,128]{1,0:T(8,128)(2,1)S(1)} %first_update.1), channel_id=1, source_target_pairs={{0,24},{1,25},{2,26},{3,27},{4,28},{5,29},{6,30},{7,31},{8,16},{9,... | collective-permute-start | bytes 61448 | tf_op jit(solution)/shard_map/ppermute | solution.py:391
  56.2 4.1 %collective-permute-done.29 = bf16[80,128]{1,0:T(8,128)(2,1)S(1)} collective-permute-done((bf16[80,128]{1,0:T(8,128)(2,1)S(1)}, bf16[80,128]{1,0:T(8,128)(2,1)S(1)}, u32[]{:S(2)}, u32[]{:S(2)}) %collective-permute-start.29) | collective-permute-done | bytes 20512 | tf_op jit(solution)/shard_map/ppermute | solution.py:391
  60.3 0.6 collective-permute-start.33
  60.9 1.5 %collective-permute-start.35 = (bf16[320,128]{1,0:T(8,128)(2,1)S(1)}, bf16[320,128]{1,0:T(8,128)(2,1)S(1)}, u32[]{:S(2)}, u32[]{:S(2)}) collective-permute-start(bf16[320,128]{1,0:T(8,128)(2,1)S(1)} %pad_maximum_fusion.refs_0_), channel_id=1, source_target_pairs={{0,4},{1,5},{2,6},{3,7},{4,0},{5,1},{6,2},{7,3},{8,12},{9,13},{10,... | collective-permute-start | bytes 245768 | tf_op jit(solution)/shard_map/ppermute | solution.py:391
  62.5 1.4 %collective-permute-start.37 = (bf16[320,128]{1,0:T(8,128)(2,1)S(1)}, bf16[320,128]{1,0:T(8,128)(2,1)S(1)}, u32[]{:S(2)}, u32[]{:S(2)}) collective-permute-start(bf16[320,128]{1,0:T(8,128)(2,1)S(1)} %pad_maximum_fusion.refs_0_), channel_id=1, source_target_pairs={{0,6},{1,7},{2,4},{3,5},{4,2},{5,3},{6,0},{7,1},{8,14},{9,15},{10,... | collective-permute-start | bytes 245768 | tf_op jit(solution)/shard_map/ppermute | solution.py:391
  63.9 1.0 broadcast_select_fusion.5.refs_0_
  64.9 0.6 collective-permute-start.14
  65.5 1.5 %collective-permute-start.16 = (bf16[464,256]{1,0:T(8,128)(2,1)S(1)}, bf16[464,256]{1,0:T(8,128)(2,1)S(1)}, u32[]{:S(2)}, u32[]{:S(2)}) collective-permute-start(bf16[464,256]{1,0:T(8,128)(2,1)S(1)} %broadcast_select_fusion.5.refs_0_), channel_id=1, source_target_pairs={{0,4},{1,5},{2,6},{3,7},{4,0},{5,1},{6,2},{7,3},{8,12},{9,13},{10,... | collective-permute-start | bytes 712712 | tf_op jit(solution)/shard_map/ppermute | solution.py:391
  67.0 1.4 %collective-permute-start.18 = (bf16[464,256]{1,0:T(8,128)(2,1)S(1)}, bf16[464,256]{1,0:T(8,128)(2,1)S(1)}, u32[]{:S(2)}, u32[]{:S(2)}) collective-permute-start(bf16[464,256]{1,0:T(8,128)(2,1)S(1)} %broadcast_select_fusion.5.refs_0_), channel_id=1, source_target_pairs={{0,6},{1,7},{2,4},{3,5},{4,2},{5,3},{6,0},{7,1},{8,14},{9,15},{10,... | collective-permute-start | bytes 712712 | tf_op jit(solution)/shard_map/ppermute | solution.py:391
  68.5 0.6 collective-permute-start.4
  69.1 1.5 %collective-permute-start.6 = (bf16[784,256]{1,0:T(8,128)(2,1)S(1)}, bf16[784,256]{1,0:T(8,128)(2,1)S(1)}, u32[]{:S(2)}, u32[]{:S(2)}) collective-permute-start(bf16[784,256]{1,0:T(8,128)(2,1)S(1)} %broadcast_select_fusion.2.refs_0_.refs_8_), channel_id=1, source_target_pairs={{0,4},{1,5},{2,6},{3,7},{4,0},{5,1},{6,2},{7,3},{8,12},{9,13},{10,... | collective-permute-start | bytes 1204232 | tf_op jit(solution)/shard_map/ppermute | solution.py:391
  70.6 2.9 %collective-permute-done.14.refs_2_ = bf16[464,256]{1,0:T(8,128)(2,1)S(1)} collective-permute-done((bf16[464,256]{1,0:T(8,128)(2,1)S(1)}, bf16[464,256]{1,0:T(8,128)(2,1)S(1)}, u32[]{:S(2)}, u32[]{:S(2)}) %collective-permute-start.14) | collective-permute-done | bytes 237600 | tf_op jit(solution)/shard_map/ppermute | solution.py:391
  73.6 1.5 %collective-permute-start.8 = (bf16[784,256]{1,0:T(8,128)(2,1)S(1)}, bf16[784,256]{1,0:T(8,128)(2,1)S(1)}, u32[]{:S(2)}, u32[]{:S(2)}) collective-permute-start(bf16[784,256]{1,0:T(8,128)(2,1)S(1)} %broadcast_select_fusion.2.refs_0_.refs_8_), channel_id=1, source_target_pairs={{0,6},{1,7},{2,4},{3,5},{4,2},{5,3},{6,0},{7,1},{8,14},{9,15},{10,... | collective-permute-start | bytes 1204232 | tf_op jit(solution)/shard_map/ppermute | solution.py:391
  75.1 4.1 %collective-permute-done.16.refs_4_ = bf16[464,256]{1,0:T(8,128)(2,1)S(1)} collective-permute-done((bf16[464,256]{1,0:T(8,128)(2,1)S(1)}, bf16[464,256]{1,0:T(8,128)(2,1)S(1)}, u32[]{:S(2)}, u32[]{:S(2)}) %collective-permute-start.16) | collective-permute-done | bytes 237600 | tf_op jit(solution)/shard_map/ppermute | solution.py:391
  79.2 0.5 collective-permute-start.15
  79.7 1.0 collective-permute-done.13.refs_1_
  80.7 0.1 collective-permute-start.17
  80.8 0.2 collective-permute-done.15.refs_3_
  81.0 0.2 collective-permute-start.3
  81.2 6.1 %collective-permute-done.4.refs_2_.refs_10_ = bf16[784,256]{1,0:T(8,128)(2,1)S(1)} collective-permute-done((bf16[784,256]{1,0:T(8,128)(2,1)S(1)}, bf16[784,256]{1,0:T(8,128)(2,1)S(1)}, u32[]{:S(2)}, u32[]{:S(2)}) %collective-permute-start.4) | collective-permute-done | bytes 401440 | tf_op jit(solution)/shard_map/ppermute | solution.py:391
  87.3 6.9 %collective-permute-done.6.refs_4_.refs_12_ = bf16[784,256]{1,0:T(8,128)(2,1)S(1)} collective-permute-done((bf16[784,256]{1,0:T(8,128)(2,1)S(1)}, bf16[784,256]{1,0:T(8,128)(2,1)S(1)}, u32[]{:S(2)}, u32[]{:S(2)}) %collective-permute-start.6) | collective-permute-done | bytes 401440 | tf_op jit(solution)/shard_map/ppermute | solution.py:391
  94.2 0.5 collective-permute-start.9
  94.8 2.1 %collective-permute-done.19.refs_7_ = bf16[464,256]{1,0:T(8,128)(2,1)S(1)} collective-permute-done((bf16[464,256]{1,0:T(8,128)(2,1)S(1)}, bf16[464,256]{1,0:T(8,128)(2,1)S(1)}, u32[]{:S(2)}, u32[]{:S(2)}) %collective-permute-start.19) | collective-permute-done | bytes 237600 | tf_op jit(solution)/shard_map/ppermute | solution.py:391
  97.0 0.4 collective-permute-start.34
  97.3 0.1 collective-permute-start.36
  97.5 0.4 collective-permute-start.38
  97.9 6.6 %second_operator.1 = (bf16[128,2048]{1,0:T(8,128)(2,1)S(1)}, f32[160,64]{1,0:T(8,128)S(1)}) custom-call(f32[2,64,2048]{2,1,0:T(8,128)S(1)} %copy-done.4, bf16[464,256]{1,0:T(8,128)(2,1)S(1)} %broadcast_select_fusion.5.refs_0_, bf16[464,256]{1,0:T(8,128)(2,1)S(1)} %collective-permute-done.13.refs_1_, bf16[464,256]{1,0:T(8,128)(2,1)S(1)} %collective-permute-done.14.refs_2_, ...), custom_call_target="tpu_custom_call" | custom-call | flops 4966055936 | bytes 10000000 | tf_op jit(solution)/shard_map/second_operator/pallas_call | solution.py:232
  104.5 0.8 second_update.1
  105.4 2.5 %collective-permute-start.40 = (bf16[80,128]{1,0:T(8,128)(2,1)S(1)}, bf16[80,128]{1,0:T(8,128)(2,1)S(1)}, u32[]{:S(2)}, u32[]{:S(2)}) collective-permute-start(bf16[80,128]{1,0:T(8,128)(2,1)S(1)} %second_update.1), channel_id=1, source_target_pairs={{0,16},{1,17},{2,18},{3,19},{4,20},{5,21},{6,22},{7,23},{8,24},{9,... | collective-permute-start | bytes 61448 | tf_op jit(solution)/shard_map/ppermute | solution.py:391
  107.9 1.9 %collective-permute-start.41 = (bf16[80,128]{1,0:T(8,128)(2,1)S(1)}, bf16[80,128]{1,0:T(8,128)(2,1)S(1)}, u32[]{:S(2)}, u32[]{:S(2)}) collective-permute-start(bf16[80,128]{1,0:T(8,128)(2,1)S(1)} %second_update.1), channel_id=1, source_target_pairs={{0,24},{1,25},{2,26},{3,27},{4,28},{5,29},{6,30},{7,31},{8,16},{9,... | collective-permute-start | bytes 61448 | tf_op jit(solution)/shard_map/ppermute | solution.py:391
  109.8 6.5 %shard_map.78.kernel_ref = bf16[2048,2048]{1,0:T(8,128)(2,1)S(1)} custom-call(bf16[464,2048]{1,0:T(8,128)(2,1)S(1)} %copy-done.9, bf16[464,256]{1,0:T(8,128)(2,1)S(1)} %broadcast_select_fusion.5.refs_0_, bf16[464,256]{1,0:T(8,128)(2,1)S(1)} %collective-permute-done.13.refs_1_, bf16[464,256]{1,0:T(8,128)(2,1)S(1)} %collective-permute-done.14.refs_2_, ...), custom_call_target="tpu_custom_call" | custom-call | flops 3892314112 | bytes 10000000 | tf_op jit(solution)/shard_map/pallas_call | solution.py:273
  116.3 1.6 %collective-permute-start.43 = (bf16[320,128]{1,0:T(8,128)(2,1)S(1)}, bf16[320,128]{1,0:T(8,128)(2,1)S(1)}, u32[]{:S(2)}, u32[]{:S(2)}) collective-permute-start(bf16[320,128]{1,0:T(8,128)(2,1)S(1)} %pad_maximum_fusion.1.refs_0_), channel_id=1, source_target_pairs={{0,2},{1,3},{2,0},{3,1},{4,6},{5,7},{6,4},{7,5},{8,10},{9,11},{10,... | collective-permute-start | bytes 245768 | tf_op jit(solution)/shard_map/ppermute | solution.py:391
  117.9 0.8 collective-permute-start.45
  118.7 1.2 collective-permute-start.47
  119.9 4.2 %shard_map.79 = (f32[147,2048]{1,0:T(8,128)S(1)}, f32[147,2048]{1,0:T(8,128)S(1)}) custom-call(s32[2]{0:T(128)S(1)} %copy-done.7, s32[2,256]{1,0:T(2,128)S(1)} %copy-done.6, bf16[2048,2048]{1,0:T(8,128)(2,1)S(1)} %shard_map.78.kernel_ref, f32[147,2048]{1,0:T(8,128)S(1)} %bitcast.14, f32[147,2048]{1,0:T(8,128)S(1)} %bitcast.16, ...), custom_call_target="tpu_custom_call" | custom-call | flops 1342177280 | bytes 8388608 | tf_op jit(solution)/shard_map/pallas_call | solution.py:360
  124.2 0.5 collective-permute-start.44
  124.8 0.4 collective-permute-start.48
  125.2 6.5 %shard_map.77.kernel_ref = bf16[2048,2048]{1,0:T(8,128)(2,1)S(1)} custom-call(bf16[464,2048]{1,0:T(8,128)(2,1)S(1)} %copy-done.9, bf16[784,256]{1,0:T(8,128)(2,1)S(1)} %broadcast_select_fusion.2.refs_0_.refs_8_, bf16[784,256]{1,0:T(8,128)(2,1)S(1)} %collective-permute-done.3.refs_1_.refs_9_, bf16[784,256]{1,0:T(8,128)(2,1)S(1)} %collective-permute-done.4.refs_2_.refs_10_, ...), custom_call_target="tpu_custom_call" | custom-call | flops 3892314112 | bytes 10000000 | tf_op jit(solution)/shard_map/pallas_call | solution.py:273
  131.8 4.8 %shard_map.80 = (f32[147,2048]{1,0:T(8,128)}, f32[147,2048]{1,0:T(8,128)}) custom-call(s32[2]{0:T(128)S(1)} %copy-done.7, s32[2,256]{1,0:T(2,128)S(1)} %copy-done.6, bf16[2048,2048]{1,0:T(8,128)(2,1)S(1)} %shard_map.77.kernel_ref, f32[147,2048]{1,0:T(8,128)S(1)} %get-tuple-element.14.residual_ref, f32[147,2048]{1,0:T(8,128)S(1)} %get-tuple-element.15.coeffs_ref, ...), custom_call_target="tpu_custom_call" | custom-call | flops 1342177280 | bytes 8388608 | tf_op jit(solution)/shard_map/pallas_call | solution.py:360
  (83 shorter events, 1.2 us)
Async XLA Ops:
  0.6 5.7 %copy-start.7 = (s32[2]{0:T(128)S(1)}, s32[2]{0:T(128)}, u32[]{:S(2)}) copy-start(s32[2]{0:T(128)} %owners_ref.5) | copy-start | bytes 28
  0.6 1.3 copy-start
  1.9 0.7 copy-start.5
  2.6 9.3 %copy-start.1 = (f32[2048,147]{0,1:T(8,128)S(1)}, f32[2048,147]{0,1:T(8,128)}, u32[]{:S(2)}) copy-start(f32[2048,147]{0,1:T(8,128)} %param.7) | copy-start | bytes 3612676
  2.6 9.3 %copy-start.6 = (s32[2,256]{1,0:T(2,128)S(1)}, s32[2,256]{1,0:T(2,128)}, u32[]{:S(2)}) copy-start(s32[2,256]{1,0:T(2,128)} %index_ref.7) | copy-start | bytes 6148
  3.2 5.6 %collective-permute-start.20 = (f16[160,256]{1,0:T(8,128)(2,1)S(1)}, f16[160,256]{1,0:T(8,128)(2,1)S(1)}, u32[]{:S(2)}, u32[]{:S(2)}) collective-permute-start(f16[160,256]{1,0:T(8,128)(2,1)S(1)} %convert_element_type.6), channel_id=1, source_target_pairs={{0,8},{1,9},{2,10},{3,11},{4,12},{5,13},{6,14},{7,15},{8,0},{9,1},... | collective-permute-start | bytes 245768 | tf_op jit(solution)/shard_map/ppermute | solution.py:391
  8.8 18.0 %collective-permute-start.21 = (f16[160,256]{1,0:T(8,128)(2,1)S(1)}, f16[160,256]{1,0:T(8,128)(2,1)S(1)}, u32[]{:S(2)}, u32[]{:S(2)}) collective-permute-start(f16[160,256]{1,0:T(8,128)(2,1)S(1)} %broadcast_select_fusion.6), channel_id=1, source_target_pairs={{0,16},{1,17},{2,18},{3,19},{4,20},{5,21},{6,22},{7,23},{8,24},{9,... | collective-permute-start | bytes 245768 | tf_op jit(solution)/shard_map/ppermute | solution.py:391
  11.9 1.5 %copy-start.2 = (bf16[2048,440]{0,1:T(8,128)(2,1)S(1)}, bf16[2048,440]{0,1:T(8,128)(2,1)}, u32[]{:S(2)}) copy-start(bf16[2048,440]{0,1:T(8,128)(2,1)} %param.6) | copy-start | bytes 5406724
  15.5 1.3 copy-start.8
  16.8 13.2 %collective-permute-start.10 = (bf16[464,256]{1,0:T(8,128)(2,1)S(1)}, bf16[464,256]{1,0:T(8,128)(2,1)S(1)}, u32[]{:S(2)}, u32[]{:S(2)}) collective-permute-start(bf16[464,256]{1,0:T(8,128)(2,1)S(1)} %get-tuple-element.13), channel_id=1, source_target_pairs={{0,8},{1,9},{2,10},{3,11},{4,12},{5,13},{6,14},{7,15},{24,16},{25,... | collective-permute-start | bytes 712712 | tf_op jit(solution)/shard_map/ppermute | solution.py:391
  20.3 15.2 %collective-permute-start = (bf16[784,256]{1,0:T(8,128)(2,1)S(1)}, bf16[784,256]{1,0:T(8,128)(2,1)S(1)}, u32[]{:S(2)}, u32[]{:S(2)}) collective-permute-start(bf16[784,256]{1,0:T(8,128)(2,1)S(1)} %get-tuple-element.12), channel_id=1, source_target_pairs={{0,8},{1,9},{2,10},{3,11},{4,12},{5,13},{6,14},{7,15},{24,16},{25,... | collective-permute-start | bytes 1204232 | tf_op jit(solution)/shard_map/ppermute | solution.py:391
  26.9 3.7 %collective-permute-start.22 = (f16[160,256]{1,0:T(8,128)(2,1)S(1)}, f16[160,256]{1,0:T(8,128)(2,1)S(1)}, u32[]{:S(2)}, u32[]{:S(2)}) collective-permute-start(f16[160,256]{1,0:T(8,128)(2,1)S(1)} %get-tuple-element.21), channel_id=1, source_target_pairs={{0,1},{1,0},{2,3},{3,2},{4,5},{5,4},{6,7},{7,6},{8,9},{9,8},{10,11... | collective-permute-start | bytes 245768 | tf_op jit(solution)/shard_map/ppermute | solution.py:391
  26.9 4.8 %collective-permute-start.23 = (f16[160,256]{1,0:T(8,128)(2,1)S(1)}, f16[160,256]{1,0:T(8,128)(2,1)S(1)}, u32[]{:S(2)}, u32[]{:S(2)}) collective-permute-start(f16[160,256]{1,0:T(8,128)(2,1)S(1)} %get-tuple-element.21), channel_id=1, source_target_pairs={{0,2},{1,3},{2,0},{3,1},{4,6},{5,7},{6,4},{7,5},{8,10},{9,11},{10,... | collective-permute-start | bytes 245768 | tf_op jit(solution)/shard_map/ppermute | solution.py:391
  28.5 5.3 %collective-permute-start.25 = (f16[160,256]{1,0:T(8,128)(2,1)S(1)}, f16[160,256]{1,0:T(8,128)(2,1)S(1)}, u32[]{:S(2)}, u32[]{:S(2)}) collective-permute-start(f16[160,256]{1,0:T(8,128)(2,1)S(1)} %get-tuple-element.21), channel_id=1, source_target_pairs={{0,4},{1,5},{2,6},{3,7},{4,0},{5,1},{6,2},{7,3},{8,12},{9,13},{10,... | collective-permute-start | bytes 245768 | tf_op jit(solution)/shard_map/ppermute | solution.py:391
  30.0 5.3 %collective-permute-start.27 = (f16[160,256]{1,0:T(8,128)(2,1)S(1)}, f16[160,256]{1,0:T(8,128)(2,1)S(1)}, u32[]{:S(2)}, u32[]{:S(2)}) collective-permute-start(f16[160,256]{1,0:T(8,128)(2,1)S(1)} %get-tuple-element.21), channel_id=1, source_target_pairs={{0,6},{1,7},{2,4},{3,5},{4,2},{5,3},{6,0},{7,1},{8,14},{9,15},{10,... | collective-permute-start | bytes 245768 | tf_op jit(solution)/shard_map/ppermute | solution.py:391
  30.5 5.8 %collective-permute-start.11 = (bf16[464,256]{1,0:T(8,128)(2,1)S(1)}, bf16[464,256]{1,0:T(8,128)(2,1)S(1)}, u32[]{:S(2)}, u32[]{:S(2)}) collective-permute-start(bf16[464,256]{1,0:T(8,128)(2,1)S(1)} %broadcast_select_fusion.3), channel_id=1, source_target_pairs={{8,16},{9,17},{10,18},{11,19},{12,20},{13,21},{14,22},{15,23},{16,... | collective-permute-start | bytes 712712 | tf_op jit(solution)/shard_map/ppermute | solution.py:391
  31.8 3.6 %collective-permute-start.24 = (f16[160,256]{1,0:T(8,128)(2,1)S(1)}, f16[160,256]{1,0:T(8,128)(2,1)S(1)}, u32[]{:S(2)}, u32[]{:S(2)}) collective-permute-start(f16[160,256]{1,0:T(8,128)(2,1)S(1)} %collective-permute-done.23), channel_id=1, source_target_pairs={{0,1},{1,0},{2,3},{3,2},{4,5},{5,4},{6,7},{7,6},{8,9},{9,8},{10,11... | collective-permute-start | bytes 245768 | tf_op jit(solution)/shard_map/ppermute | solution.py:391
  33.8 2.4 %collective-permute-start.26 = (f16[160,256]{1,0:T(8,128)(2,1)S(1)}, f16[160,256]{1,0:T(8,128)(2,1)S(1)}, u32[]{:S(2)}, u32[]{:S(2)}) collective-permute-start(f16[160,256]{1,0:T(8,128)(2,1)S(1)} %collective-permute-done.25), channel_id=1, source_target_pairs={{0,1},{1,0},{2,3},{3,2},{4,5},{5,4},{6,7},{7,6},{8,9},{9,8},{10,11... | collective-permute-start | bytes 245768 | tf_op jit(solution)/shard_map/ppermute | solution.py:391
  35.4 4.0 %collective-permute-start.28 = (f16[160,256]{1,0:T(8,128)(2,1)S(1)}, f16[160,256]{1,0:T(8,128)(2,1)S(1)}, u32[]{:S(2)}, u32[]{:S(2)}) collective-permute-start(f16[160,256]{1,0:T(8,128)(2,1)S(1)} %collective-permute-done.27), channel_id=1, source_target_pairs={{0,1},{1,0},{2,3},{3,2},{4,5},{5,4},{6,7},{7,6},{8,9},{9,8},{10,11... | collective-permute-start | bytes 245768 | tf_op jit(solution)/shard_map/ppermute | solution.py:391
  35.6 2.1 %collective-permute-start.1 = (bf16[784,256]{1,0:T(8,128)(2,1)S(1)}, bf16[784,256]{1,0:T(8,128)(2,1)S(1)}, u32[]{:S(2)}, u32[]{:S(2)}) collective-permute-start(bf16[784,256]{1,0:T(8,128)(2,1)S(1)} %broadcast_select_fusion), channel_id=1, source_target_pairs={{8,16},{9,17},{10,18},{11,19},{12,20},{13,21},{14,22},{15,23},{16,... | collective-permute-start | bytes 1204232 | tf_op jit(solution)/shard_map/ppermute | solution.py:391
  36.4 27.5 %collective-permute-start.12 = (bf16[464,256]{1,0:T(8,128)(2,1)S(1)}, bf16[464,256]{1,0:T(8,128)(2,1)}, u32[]{:S(2)}, u32[]{:S(2)}) collective-permute-start(bf16[464,256]{1,0:T(8,128)(2,1)S(1)} %broadcast_select_fusion.4), channel_id=1, source_target_pairs={{8,0},{9,1},{10,2},{11,3},{12,4},{13,5},{14,6},{15,7},{16,24},{17,... | collective-permute-start | bytes 712712 | tf_op jit(solution)/shard_map/ppermute | solution.py:391
  37.7 1.8 %copy-start.4 = (f32[2,64,2048]{2,1,0:T(8,128)S(1)}, f32[2,64,2048]{2,1,0:T(8,128)}, u32[]{:S(2)}) copy-start(f32[2,64,2048]{2,1,0:T(8,128)} %inverse_ref.3) | copy-start | bytes 3145732
  37.7 29.3 %collective-permute-start.2 = (bf16[784,256]{1,0:T(8,128)(2,1)S(1)}, bf16[784,256]{1,0:T(8,128)(2,1)S(1)}, u32[]{:S(2)}, u32[]{:S(2)}) collective-permute-start(bf16[784,256]{1,0:T(8,128)(2,1)S(1)} %broadcast_select_fusion.1), channel_id=1, source_target_pairs={{8,0},{9,1},{10,2},{11,3},{12,4},{13,5},{14,6},{15,7},{16,24},{17,... | collective-permute-start | bytes 1204232 | tf_op jit(solution)/shard_map/ppermute | solution.py:391
  40.2 20.1 %collective-permute-start.29 = (bf16[80,128]{1,0:T(8,128)(2,1)S(1)}, bf16[80,128]{1,0:T(8,128)(2,1)S(1)}, u32[]{:S(2)}, u32[]{:S(2)}) collective-permute-start(bf16[80,128]{1,0:T(8,128)(2,1)S(1)} %first_update.1), channel_id=1, source_target_pairs={{0,8},{1,9},{2,10},{3,11},{4,12},{5,13},{6,14},{7,15},{8,0},{9,1},... | collective-permute-start | bytes 61448 | tf_op jit(solution)/shard_map/ppermute | solution.py:391
  51.1 9.2 %collective-permute-start.30 = (bf16[80,128]{1,0:T(8,128)(2,1)S(1)}, bf16[80,128]{1,0:T(8,128)(2,1)S(1)}, u32[]{:S(2)}, u32[]{:S(2)}) collective-permute-start(bf16[80,128]{1,0:T(8,128)(2,1)S(1)} %first_update.1), channel_id=1, source_target_pairs={{0,16},{1,17},{2,18},{3,19},{4,20},{5,21},{6,22},{7,23},{8,24},{9,... | collective-permute-start | bytes 61448 | tf_op jit(solution)/shard_map/ppermute | solution.py:391
  52.2 8.1 %collective-permute-start.31 = (bf16[80,128]{1,0:T(8,128)(2,1)S(1)}, bf16[80,128]{1,0:T(8,128)(2,1)S(1)}, u32[]{:S(2)}, u32[]{:S(2)}) collective-permute-start(bf16[80,128]{1,0:T(8,128)(2,1)S(1)} %first_update.1), channel_id=1, source_target_pairs={{0,24},{1,25},{2,26},{3,27},{4,28},{5,29},{6,30},{7,31},{8,16},{9,... | collective-permute-start | bytes 61448 | tf_op jit(solution)/shard_map/ppermute | solution.py:391
  60.3 5.1 %collective-permute-start.33 = (bf16[320,128]{1,0:T(8,128)(2,1)S(1)}, bf16[320,128]{1,0:T(8,128)(2,1)S(1)}, u32[]{:S(2)}, u32[]{:S(2)}) collective-permute-start(bf16[320,128]{1,0:T(8,128)(2,1)S(1)} %pad_maximum_fusion.refs_0_), channel_id=1, source_target_pairs={{0,2},{1,3},{2,0},{3,1},{4,6},{5,7},{6,4},{7,5},{8,10},{9,11},{10,... | collective-permute-start | bytes 245768 | tf_op jit(solution)/shard_map/ppermute | solution.py:391
  60.9 7.6 %collective-permute-start.35 = (bf16[320,128]{1,0:T(8,128)(2,1)S(1)}, bf16[320,128]{1,0:T(8,128)(2,1)S(1)}, u32[]{:S(2)}, u32[]{:S(2)}) collective-permute-start(bf16[320,128]{1,0:T(8,128)(2,1)S(1)} %pad_maximum_fusion.refs_0_), channel_id=1, source_target_pairs={{0,4},{1,5},{2,6},{3,7},{4,0},{5,1},{6,2},{7,3},{8,12},{9,13},{10,... | collective-permute-start | bytes 245768 | tf_op jit(solution)/shard_map/ppermute | solution.py:391
  62.5 6.6 %collective-permute-start.37 = (bf16[320,128]{1,0:T(8,128)(2,1)S(1)}, bf16[320,128]{1,0:T(8,128)(2,1)S(1)}, u32[]{:S(2)}, u32[]{:S(2)}) collective-permute-start(bf16[320,128]{1,0:T(8,128)(2,1)S(1)} %pad_maximum_fusion.refs_0_), channel_id=1, source_target_pairs={{0,6},{1,7},{2,4},{3,5},{4,2},{5,3},{6,0},{7,1},{8,14},{9,15},{10,... | collective-permute-start | bytes 245768 | tf_op jit(solution)/shard_map/ppermute | solution.py:391
  64.9 8.7 %collective-permute-start.14 = (bf16[464,256]{1,0:T(8,128)(2,1)S(1)}, bf16[464,256]{1,0:T(8,128)(2,1)S(1)}, u32[]{:S(2)}, u32[]{:S(2)}) collective-permute-start(bf16[464,256]{1,0:T(8,128)(2,1)S(1)} %broadcast_select_fusion.5.refs_0_), channel_id=1, source_target_pairs={{0,2},{1,3},{2,0},{3,1},{4,6},{5,7},{6,4},{7,5},{8,10},{9,11},{10,... | collective-permute-start | bytes 712712 | tf_op jit(solution)/shard_map/ppermute | solution.py:391
  65.5 13.7 %collective-permute-start.16 = (bf16[464,256]{1,0:T(8,128)(2,1)S(1)}, bf16[464,256]{1,0:T(8,128)(2,1)S(1)}, u32[]{:S(2)}, u32[]{:S(2)}) collective-permute-start(bf16[464,256]{1,0:T(8,128)(2,1)S(1)} %broadcast_select_fusion.5.refs_0_), channel_id=1, source_target_pairs={{0,4},{1,5},{2,6},{3,7},{4,0},{5,1},{6,2},{7,3},{8,12},{9,13},{10,... | collective-permute-start | bytes 712712 | tf_op jit(solution)/shard_map/ppermute | solution.py:391
  67.0 12.2 %collective-permute-start.18 = (bf16[464,256]{1,0:T(8,128)(2,1)S(1)}, bf16[464,256]{1,0:T(8,128)(2,1)S(1)}, u32[]{:S(2)}, u32[]{:S(2)}) collective-permute-start(bf16[464,256]{1,0:T(8,128)(2,1)S(1)} %broadcast_select_fusion.5.refs_0_), channel_id=1, source_target_pairs={{0,6},{1,7},{2,4},{3,5},{4,2},{5,3},{6,0},{7,1},{8,14},{9,15},{10,... | collective-permute-start | bytes 712712 | tf_op jit(solution)/shard_map/ppermute | solution.py:391
  68.5 18.8 %collective-permute-start.4 = (bf16[784,256]{1,0:T(8,128)(2,1)S(1)}, bf16[784,256]{1,0:T(8,128)(2,1)S(1)}, u32[]{:S(2)}, u32[]{:S(2)}) collective-permute-start(bf16[784,256]{1,0:T(8,128)(2,1)S(1)} %broadcast_select_fusion.2.refs_0_.refs_8_), channel_id=1, source_target_pairs={{0,2},{1,3},{2,0},{3,1},{4,6},{5,7},{6,4},{7,5},{8,10},{9,11},{10,... | collective-permute-start | bytes 1204232 | tf_op jit(solution)/shard_map/ppermute | solution.py:391
  69.1 25.1 %collective-permute-start.6 = (bf16[784,256]{1,0:T(8,128)(2,1)S(1)}, bf16[784,256]{1,0:T(8,128)(2,1)S(1)}, u32[]{:S(2)}, u32[]{:S(2)}) collective-permute-start(bf16[784,256]{1,0:T(8,128)(2,1)S(1)} %broadcast_select_fusion.2.refs_0_.refs_8_), channel_id=1, source_target_pairs={{0,4},{1,5},{2,6},{3,7},{4,0},{5,1},{6,2},{7,3},{8,12},{9,13},{10,... | collective-permute-start | bytes 1204232 | tf_op jit(solution)/shard_map/ppermute | solution.py:391
  73.6 20.6 %collective-permute-start.8 = (bf16[784,256]{1,0:T(8,128)(2,1)S(1)}, bf16[784,256]{1,0:T(8,128)(2,1)S(1)}, u32[]{:S(2)}, u32[]{:S(2)}) collective-permute-start(bf16[784,256]{1,0:T(8,128)(2,1)S(1)} %broadcast_select_fusion.2.refs_0_.refs_8_), channel_id=1, source_target_pairs={{0,6},{1,7},{2,4},{3,5},{4,2},{5,3},{6,0},{7,1},{8,14},{9,15},{10,... | collective-permute-start | bytes 1204232 | tf_op jit(solution)/shard_map/ppermute | solution.py:391
  79.2 1.5 %collective-permute-start.13 = (bf16[464,256]{1,0:T(8,128)(2,1)S(1)}, bf16[464,256]{1,0:T(8,128)(2,1)S(1)}, u32[]{:S(2)}, u32[]{:S(2)}) collective-permute-start(bf16[464,256]{1,0:T(8,128)(2,1)S(1)} %broadcast_select_fusion.5.refs_0_), channel_id=1, source_target_pairs={{0,1},{1,0},{2,3},{3,2},{4,5},{5,4},{6,7},{7,6},{8,9},{9,8},{10,11... | collective-permute-start | bytes 712712 | tf_op jit(solution)/shard_map/ppermute | solution.py:391
  79.2 1.8 %collective-permute-start.15 = (bf16[464,256]{1,0:T(8,128)(2,1)S(1)}, bf16[464,256]{1,0:T(8,128)(2,1)S(1)}, u32[]{:S(2)}, u32[]{:S(2)}) collective-permute-start(bf16[464,256]{1,0:T(8,128)(2,1)S(1)} %collective-permute-done.14.refs_2_), channel_id=1, source_target_pairs={{0,1},{1,0},{2,3},{3,2},{4,5},{5,4},{6,7},{7,6},{8,9},{9,8},{10,11... | collective-permute-start | bytes 712712 | tf_op jit(solution)/shard_map/ppermute | solution.py:391
  80.7 14.0 %collective-permute-start.17 = (bf16[464,256]{1,0:T(8,128)(2,1)S(1)}, bf16[464,256]{1,0:T(8,128)(2,1)S(1)}, u32[]{:S(2)}, u32[]{:S(2)}) collective-permute-start(bf16[464,256]{1,0:T(8,128)(2,1)S(1)} %collective-permute-done.16.refs_4_), channel_id=1, source_target_pairs={{0,1},{1,0},{2,3},{3,2},{4,5},{5,4},{6,7},{7,6},{8,9},{9,8},{10,11... | collective-permute-start | bytes 712712 | tf_op jit(solution)/shard_map/ppermute | solution.py:391
  81.0 15.9 %collective-permute-start.3 = (bf16[784,256]{1,0:T(8,128)(2,1)S(1)}, bf16[784,256]{1,0:T(8,128)(2,1)S(1)}, u32[]{:S(2)}, u32[]{:S(2)}) collective-permute-start(bf16[784,256]{1,0:T(8,128)(2,1)S(1)} %broadcast_select_fusion.2.refs_0_.refs_8_), channel_id=1, source_target_pairs={{0,1},{1,0},{2,3},{3,2},{4,5},{5,4},{6,7},{7,6},{8,9},{9,8},{10,11... | collective-permute-start | bytes 1204232 | tf_op jit(solution)/shard_map/ppermute | solution.py:391
  87.3 10.0 %collective-permute-start.5 = (bf16[784,256]{1,0:T(8,128)(2,1)S(1)}, bf16[784,256]{1,0:T(8,128)(2,1)S(1)}, u32[]{:S(2)}, u32[]{:S(2)}) collective-permute-start(bf16[784,256]{1,0:T(8,128)(2,1)S(1)} %collective-permute-done.4.refs_2_.refs_10_), channel_id=1, source_target_pairs={{0,1},{1,0},{2,3},{3,2},{4,5},{5,4},{6,7},{7,6},{8,9},{9,8},{10,11... | collective-permute-start | bytes 1204232 | tf_op jit(solution)/shard_map/ppermute | solution.py:391
  94.2 3.3 %collective-permute-start.7 = (bf16[784,256]{1,0:T(8,128)(2,1)S(1)}, bf16[784,256]{1,0:T(8,128)(2,1)S(1)}, u32[]{:S(2)}, u32[]{:S(2)}) collective-permute-start(bf16[784,256]{1,0:T(8,128)(2,1)S(1)} %collective-permute-done.6.refs_4_.refs_12_), channel_id=1, source_target_pairs={{0,1},{1,0},{2,3},{3,2},{4,5},{5,4},{6,7},{7,6},{8,9},{9,8},{10,11... | collective-permute-start | bytes 1204232 | tf_op jit(solution)/shard_map/ppermute | solution.py:391
  94.2 3.7 %collective-permute-start.9 = (bf16[784,256]{1,0:T(8,128)(2,1)S(1)}, bf16[784,256]{1,0:T(8,128)(2,1)S(1)}, u32[]{:S(2)}, u32[]{:S(2)}) collective-permute-start(bf16[784,256]{1,0:T(8,128)(2,1)S(1)} %collective-permute-done.8.refs_6_.refs_14_), channel_id=1, source_target_pairs={{0,1},{1,0},{2,3},{3,2},{4,5},{5,4},{6,7},{7,6},{8,9},{9,8},{10,11... | collective-permute-start | bytes 1204232 | tf_op jit(solution)/shard_map/ppermute | solution.py:391
  94.7 2.1 %collective-permute-start.19 = (bf16[464,256]{1,0:T(8,128)(2,1)S(1)}, bf16[464,256]{1,0:T(8,128)(2,1)S(1)}, u32[]{:S(2)}, u32[]{:S(2)}) collective-permute-start(bf16[464,256]{1,0:T(8,128)(2,1)S(1)} %collective-permute-done.18.refs_6_), channel_id=1, source_target_pairs={{0,1},{1,0},{2,3},{3,2},{4,5},{5,4},{6,7},{7,6},{8,9},{9,8},{10,11... | collective-permute-start | bytes 712712 | tf_op jit(solution)/shard_map/ppermute | solution.py:391
  96.8 7.7 %collective-permute-start.32 = (bf16[320,128]{1,0:T(8,128)(2,1)S(1)}, bf16[320,128]{1,0:T(8,128)(2,1)S(1)}, u32[]{:S(2)}, u32[]{:S(2)}) collective-permute-start(bf16[320,128]{1,0:T(8,128)(2,1)S(1)} %pad_maximum_fusion.refs_0_), channel_id=1, source_target_pairs={{0,1},{1,0},{2,3},{3,2},{4,5},{5,4},{6,7},{7,6},{8,9},{9,8},{10,11... | collective-permute-start | bytes 245768 | tf_op jit(solution)/shard_map/ppermute | solution.py:391
  97.0 7.5 %collective-permute-start.34 = (bf16[320,128]{1,0:T(8,128)(2,1)S(1)}, bf16[320,128]{1,0:T(8,128)(2,1)S(1)}, u32[]{:S(2)}, u32[]{:S(2)}) collective-permute-start(bf16[320,128]{1,0:T(8,128)(2,1)S(1)} %collective-permute-done.33.refs_2_), channel_id=1, source_target_pairs={{0,1},{1,0},{2,3},{3,2},{4,5},{5,4},{6,7},{7,6},{8,9},{9,8},{10,11... | collective-permute-start | bytes 245768 | tf_op jit(solution)/shard_map/ppermute | solution.py:391
  97.3 7.2 %collective-permute-start.36 = (bf16[320,128]{1,0:T(8,128)(2,1)S(1)}, bf16[320,128]{1,0:T(8,128)(2,1)S(1)}, u32[]{:S(2)}, u32[]{:S(2)}) collective-permute-start(bf16[320,128]{1,0:T(8,128)(2,1)S(1)} %collective-permute-done.35.refs_4_), channel_id=1, source_target_pairs={{0,1},{1,0},{2,3},{3,2},{4,5},{5,4},{6,7},{7,6},{8,9},{9,8},{10,11... | collective-permute-start | bytes 245768 | tf_op jit(solution)/shard_map/ppermute | solution.py:391
  97.5 7.0 %collective-permute-start.38 = (bf16[320,128]{1,0:T(8,128)(2,1)S(1)}, bf16[320,128]{1,0:T(8,128)(2,1)S(1)}, u32[]{:S(2)}, u32[]{:S(2)}) collective-permute-start(bf16[320,128]{1,0:T(8,128)(2,1)S(1)} %collective-permute-done.37.refs_6_), channel_id=1, source_target_pairs={{0,1},{1,0},{2,3},{3,2},{4,5},{5,4},{6,7},{7,6},{8,9},{9,8},{10,11... | collective-permute-start | bytes 245768 | tf_op jit(solution)/shard_map/ppermute | solution.py:391
  97.9 11.9 %copy-start.9 = (bf16[464,2048]{1,0:T(8,128)(2,1)S(1)}, bf16[464,2048]{1,0:T(8,128)(2,1)}, u32[]{:S(2)}) copy-start(bf16[464,2048]{1,0:T(8,128)(2,1)} %copy-done.8) | copy-start | bytes 5701636
  105.3 11.0 %collective-permute-start.39 = (bf16[80,128]{1,0:T(8,128)(2,1)S(1)}, bf16[80,128]{1,0:T(8,128)(2,1)S(1)}, u32[]{:S(2)}, u32[]{:S(2)}) collective-permute-start(bf16[80,128]{1,0:T(8,128)(2,1)S(1)} %second_update.1), channel_id=1, source_target_pairs={{0,8},{1,9},{2,10},{3,11},{4,12},{5,13},{6,14},{7,15},{8,0},{9,1},... | collective-permute-start | bytes 61448 | tf_op jit(solution)/shard_map/ppermute | solution.py:391
  105.4 10.9 %collective-permute-start.40 = (bf16[80,128]{1,0:T(8,128)(2,1)S(1)}, bf16[80,128]{1,0:T(8,128)(2,1)S(1)}, u32[]{:S(2)}, u32[]{:S(2)}) collective-permute-start(bf16[80,128]{1,0:T(8,128)(2,1)S(1)} %second_update.1), channel_id=1, source_target_pairs={{0,16},{1,17},{2,18},{3,19},{4,20},{5,21},{6,22},{7,23},{8,24},{9,... | collective-permute-start | bytes 61448 | tf_op jit(solution)/shard_map/ppermute | solution.py:391
  107.9 8.4 %collective-permute-start.41 = (bf16[80,128]{1,0:T(8,128)(2,1)S(1)}, bf16[80,128]{1,0:T(8,128)(2,1)S(1)}, u32[]{:S(2)}, u32[]{:S(2)}) collective-permute-start(bf16[80,128]{1,0:T(8,128)(2,1)S(1)} %second_update.1), channel_id=1, source_target_pairs={{0,24},{1,25},{2,26},{3,27},{4,28},{5,29},{6,30},{7,31},{8,16},{9,... | collective-permute-start | bytes 61448 | tf_op jit(solution)/shard_map/ppermute | solution.py:391
  109.8 10.1 %copy-start.3 = (f32[2048,147]{0,1:T(8,128)S(1)}, f32[2048,147]{0,1:T(8,128)}, u32[]{:S(2)}) copy-start(f32[2048,147]{0,1:T(8,128)} %param.8) | copy-start | bytes 3612676
  116.3 7.9 %collective-permute-start.43 = (bf16[320,128]{1,0:T(8,128)(2,1)S(1)}, bf16[320,128]{1,0:T(8,128)(2,1)S(1)}, u32[]{:S(2)}, u32[]{:S(2)}) collective-permute-start(bf16[320,128]{1,0:T(8,128)(2,1)S(1)} %pad_maximum_fusion.1.refs_0_), channel_id=1, source_target_pairs={{0,2},{1,3},{2,0},{3,1},{4,6},{5,7},{6,4},{7,5},{8,10},{9,11},{10,... | collective-permute-start | bytes 245768 | tf_op jit(solution)/shard_map/ppermute | solution.py:391
  117.9 6.8 %collective-permute-start.45 = (bf16[320,128]{1,0:T(8,128)(2,1)S(1)}, bf16[320,128]{1,0:T(8,128)(2,1)S(1)}, u32[]{:S(2)}, u32[]{:S(2)}) collective-permute-start(bf16[320,128]{1,0:T(8,128)(2,1)S(1)} %pad_maximum_fusion.1.refs_0_), channel_id=1, source_target_pairs={{0,4},{1,5},{2,6},{3,7},{4,0},{5,1},{6,2},{7,3},{8,12},{9,13},{10,... | collective-permute-start | bytes 245768 | tf_op jit(solution)/shard_map/ppermute | solution.py:391
  118.7 6.1 %collective-permute-start.47 = (bf16[320,128]{1,0:T(8,128)(2,1)S(1)}, bf16[320,128]{1,0:T(8,128)(2,1)S(1)}, u32[]{:S(2)}, u32[]{:S(2)}) collective-permute-start(bf16[320,128]{1,0:T(8,128)(2,1)S(1)} %pad_maximum_fusion.1.refs_0_), channel_id=1, source_target_pairs={{0,6},{1,7},{2,4},{3,5},{4,2},{5,3},{6,0},{7,1},{8,14},{9,15},{10,... | collective-permute-start | bytes 245768 | tf_op jit(solution)/shard_map/ppermute | solution.py:391
  124.1 7.6 %collective-permute-start.42 = (bf16[320,128]{1,0:T(8,128)(2,1)S(1)}, bf16[320,128]{1,0:T(8,128)(2,1)S(1)}, u32[]{:S(2)}, u32[]{:S(2)}) collective-permute-start(bf16[320,128]{1,0:T(8,128)(2,1)S(1)} %pad_maximum_fusion.1.refs_0_), channel_id=1, source_target_pairs={{0,1},{1,0},{2,3},{3,2},{4,5},{5,4},{6,7},{7,6},{8,9},{9,8},{10,11... | collective-permute-start | bytes 245768 | tf_op jit(solution)/shard_map/ppermute | solution.py:391
  124.2 7.5 %collective-permute-start.44 = (bf16[320,128]{1,0:T(8,128)(2,1)S(1)}, bf16[320,128]{1,0:T(8,128)(2,1)S(1)}, u32[]{:S(2)}, u32[]{:S(2)}) collective-permute-start(bf16[320,128]{1,0:T(8,128)(2,1)S(1)} %collective-permute-done.43.refs_2_), channel_id=1, source_target_pairs={{0,1},{1,0},{2,3},{3,2},{4,5},{5,4},{6,7},{7,6},{8,9},{9,8},{10,11... | collective-permute-start | bytes 245768 | tf_op jit(solution)/shard_map/ppermute | solution.py:391
  124.7 7.0 %collective-permute-start.46 = (bf16[320,128]{1,0:T(8,128)(2,1)S(1)}, bf16[320,128]{1,0:T(8,128)(2,1)S(1)}, u32[]{:S(2)}, u32[]{:S(2)}) collective-permute-start(bf16[320,128]{1,0:T(8,128)(2,1)S(1)} %collective-permute-done.45.refs_4_), channel_id=1, source_target_pairs={{0,1},{1,0},{2,3},{3,2},{4,5},{5,4},{6,7},{7,6},{8,9},{9,8},{10,11... | collective-permute-start | bytes 245768 | tf_op jit(solution)/shard_map/ppermute | solution.py:391
  124.8 6.9 %collective-permute-start.48 = (bf16[320,128]{1,0:T(8,128)(2,1)S(1)}, bf16[320,128]{1,0:T(8,128)(2,1)S(1)}, u32[]{:S(2)}, u32[]{:S(2)}) collective-permute-start(bf16[320,128]{1,0:T(8,128)(2,1)S(1)} %collective-permute-done.47.refs_6_), channel_id=1, source_target_pairs={{0,1},{1,0},{2,3},{3,2},{4,5},{5,4},{6,7},{7,6},{8,9},{9,8},{10,11... | collective-permute-start | bytes 245768 | tf_op jit(solution)/shard_map/ppermute | solution.py:391
where the time goes:
time: 137 us
  starting transfers between devices  54.5 us (40%)
  Pallas kernels  32.8 us (24%)
  waiting for transfers between devices  32.8 us (24%)
  between operations  9.58 us (7%)
  local copies, waits for them, and re-layouts  5.46 us (4%)
  other arithmetic  1.37 us (1%)
    ppermute x49, starting transfers between devices, send(): return lax.ppermute(value, ('rows', 'cols'), pairs)  54.5 us
    ppermute x49, waiting for transfers between devices, send(): return lax.ppermute(value, ('rows', 'cols'), pairs)  32.8 us
    pallas_call x2, Pallas kernels, block_kernel(): pl.pallas_call(body, grid=(frames // tile,), in_specs=[pl.BlockSpec((dept...  13 us
    pallas_call x2, Pallas kernels, apply_update(): pl.pallas_call(body, grid=(frames // tile,), in_specs=[smem, vmem, pl.Blo...  9.07 us
    pallas_call x1, Pallas kernels, second_operator(): pl.pallas_call(body, grid=(1,), in_specs=[pl.BlockSpec((1, mine, block),...  6.61 us
    unnamed x26, local copies, waits for them, and re-layouts  4.86 us
  transfers between devices with their start and end apart: 49, of which 12 were waited for; matrix products, arithmetic and copies ran while one was open for 1% of the time, Pallas kernels for 19%

commit v1 on v0

--- a/solution.py
+++ b/solution.py
@@ -63,18 +63,19 @@
 def pick_residual(index, residual_t):
     outputs, frames = residual_t.shape
     rows = up(outputs, 16)
-    picks = index.shape[1]
-
-    def body(index_ref, residual_ref, first_ref):
-        high, low = split(padded(residual_ref[...], rows), 2)
-        first = matmul(jnp.concatenate([high, low], 0), one_hot(frames, index_ref[0:1, :]))
-        first_ref[...] = first[:rows] + first[rows:]
+    steps, picks = index.shape
+
+    def body(index_ref, residual_ref, *out_ref):
+        both = jnp.concatenate(split(padded(residual_ref[...], rows), 2), 0)
+        for step in range(steps):
+            found = matmul(both, one_hot(frames, index_ref[step : step + 1, :]))
+            out_ref[step][...] = found[:rows] + found[rows:]
 
     return pl.pallas_call(
         body,
         in_specs=[vmem, vmem],
-        out_specs=vmem,
-        out_shape=jax.ShapeDtypeStruct((rows, picks), f32),
+        out_specs=(vmem,) * steps,
+        out_shape=(jax.ShapeDtypeStruct((rows, picks), f32),) * steps,
         compiler_params=params(),
         name="pick_residual",
     )(index, residual_t)
@@ -97,157 +98,143 @@
     return jnp.concatenate(pieces, 0)
 
 
-def pick_features(owners, index, features_t, residual_t):
+def pick_features(owners, index, features_t, rules):
     width, frames = features_t.shape
-    outputs = residual_t.shape[0]
-    depth = up(width + 20, 16)
-    picks = index.shape[1]
-    rows = up(outputs, 16)
-    tail = depth - width
-
-    def body(owners_ref, index_ref, features_ref, residual_ref, local_ref, first_ref, second_ref):
+    depth = up(width + 18, 16)
+    steps, picks = index.shape
+    kinds = ((2, 0, 1), (0, 2, 2))
+
+    def body(owners_ref, index_ref, features_ref, *out_ref):
         features = features_ref[...]
-        hot = one_hot(frames, index_ref[0:1, :])
-        picked = matmul(features, hot)
-        picked_squares = jnp.sum(picked * picked, axis=0, keepdims=True)
-        first_ref[0:width, :] = picked.astype(bf16)
-        rest = jnp.zeros((tail - 18, picks), bf16)
-        first_ref[width:depth, :] = jnp.concatenate([norm_rows(picked_squares, (2, 0, 1)), rest], 0)
-
-        hot = one_hot(frames, index_ref[1:2, :])
-        picked = matmul(features, hot)
-        picked_squares = jnp.sum(picked * picked, axis=0, keepdims=True)
-        second_ref[0:width, :] = picked.astype(bf16)
-        places = lax.broadcasted_iota(jnp.int32, (picks, picks), 0) + 1
-        meet = jnp.where(turn(index_ref[0:1, :]) == index_ref[1:2, :], places, 0)
-        place = jnp.max(meet, axis=0, keepdims=True)
-        place = jnp.where(owners_ref[0] == owners_ref[1], place, 0)
-        place = jnp.concatenate([place // LANES, place % LANES], 0).astype(f32).astype(bf16)
-        rest = jnp.zeros((tail - 20, picks), bf16)
-        second_ref[width:depth, :] = jnp.concatenate([norm_rows(picked_squares, (0, 2, 2)), place, rest], 0)
-        high, low = split(padded(residual_ref[...], rows), 2)
-        second_ref[depth:, :] = matmul(jnp.concatenate([high, low], 0), hot).astype(bf16)
-
+        rest = jnp.zeros((depth - width - 18, picks), bf16)
+        for step in range(steps):
+            picked = matmul(features, one_hot(frames, index_ref[step : step + 1, :]))
+            squares = jnp.sum(picked * picked, axis=0, keepdims=True)
+            out_ref[step][0:width, :] = picked.astype(bf16)
+            out_ref[step][width:depth, :] = jnp.concatenate([norm_rows(squares, kinds[step]), rest], 0)
+        row = lax.axis_index("rows")
+        for (step, rule), take_ref in zip(rules, out_ref[steps:]):
+            take = jnp.where(rule(row, owners_ref[step]), 1.0, 0.0)
+            take_ref[...] = jnp.full(take_ref.shape, take, f32)
+
+    return pl.pallas_call(
+        body,
+        in_specs=[smem, vmem, vmem],
+        out_specs=(vmem,) * (steps + len(rules)),
+        out_shape=(jax.ShapeDtypeStruct((depth, picks), bf16),) * steps
+        + (jax.ShapeDtypeStruct((1, picks), f32),) * len(rules),
+        compiler_params=params(),
+        name="pick_features",
+    )(owners, index, features_t)
+
+
+def lane_start(value, unit):
+    return pl.ds(pl.multiple_of(value * unit, unit), unit)
+
+
+def piece_col(piece):
+    mine = lax.axis_index("cols")
+    return ((mine // 2) ^ (piece // 2)) * 2 + ((mine % 2) ^ (piece % 2))
+
+
+def fold(update):
+    half = update.shape[0] // 2
+    return jnp.concatenate([update[:half], update[half:]], 1).astype(bf16)
+
+
+def prepare(features_t, inverse, picks):
+    width, frames = features_t.shape
+    depth = up(width + 18, 16)
+    steps, mine, block = inverse.shape
+
+    def body(features_ref, inverse_ref, local_ref, *stacked_ref):
+        features = features_ref[...]
         wide = features.astype(f32)
         squares = jnp.sum(wide * wide, axis=0, keepdims=True)
         local_ref[0:width, :] = features
-        rest = jnp.zeros((tail - 18, frames), bf16)
+        rest = jnp.zeros((depth - width - 18, frames), bf16)
         local_ref[width:depth, :] = jnp.concatenate([norm_rows(squares, (1, 1, 0)), rest], 0)
-
-    return pl.pallas_call(
-        body,
-        in_specs=[smem, vmem, vmem, vmem],
-        out_specs=(vmem, vmem, vmem),
-        out_shape=(
-            jax.ShapeDtypeStruct((depth, frames), bf16),
-            jax.ShapeDtypeStruct((depth, picks), bf16),
-            jax.ShapeDtypeStruct((depth + 2 * rows, picks), bf16),
-        ),
-        compiler_params=params(),
-        name="pick_features",
-    )(owners, index, features_t, residual_t)
-
-
-def lane_start(value, unit):
-    return pl.ds(pl.multiple_of(value * unit, unit), unit)
-
-
-def piece_col(piece):
-    mine = lax.axis_index("cols")
-    return ((mine // 2) ^ (piece // 2)) * 2 + ((mine % 2) ^ (piece % 2))
-
-
-def fold(update):
-    half = update.shape[0] // 2
-    return jnp.concatenate([update[:half], update[half:]], 1).astype(bf16)
-
-
-def stack_inverse(inverse_ref, picks, stacked):
-    for k in range(stacked.shape[1] // picks):
-        high, low = split(inverse_ref[0, :, lane_start(piece_col(k), picks)], 2)
-        stacked[:, k * picks : (k + 1) * picks] = jnp.concatenate([high, low], 0)
-
-
-def first_update(picked, inverse, step, picks):
-    rows, block = picked.shape
-    mine = inverse.shape[1]
-
-    def body(inverse_ref, picked_ref, out_ref, stacked):
-        stack_inverse(inverse_ref, picks, stacked)
-        product = matmul_nt(jnp.concatenate(split(picked_ref[...], 2), 0), stacked[...])
+        for step in range(steps):
+            for k in range(block // picks):
+                high, low = split(inverse_ref[step, :, lane_start(piece_col(k), picks)], 2)
+                stacked_ref[step][:, k * picks : (k + 1) * picks] = jnp.concatenate([high, low], 0)
+
+    return pl.pallas_call(
+        body,
+        in_specs=[vmem, vmem],
+        out_specs=(vmem,) * (1 + steps),
+        out_shape=(jax.ShapeDtypeStruct((depth, frames), bf16),)
+        + (jax.ShapeDtypeStruct((2 * mine, block), bf16),) * steps,
+        compiler_params=params(),
+        name="prepare",
+    )(features_t, inverse)
+
+
+def block_update(picked, stacked, scaled):
+    rows, _ = picked.shape
+    mine = stacked.shape[0] // 2
+
+    def body(stacked_ref, picked_ref, out_ref):
+        product = matmul_nt(jnp.concatenate(split(picked_ref[...], 2), 0), stacked_ref[...])
         product = product[:rows] + product[rows:]
-        out_ref[...] = fold(product[:, :mine] + product[:, mine:])
-
-    return pl.pallas_call(
-        body,
-        grid=(1,),
-        in_specs=[pl.BlockSpec((1, mine, block), lambda i: (step, 0, 0)), vmem],
+        out_ref[...] = fold((product[:, :mine] + product[:, mine:]) * scaled)
+
+    return pl.pallas_call(
+        body,
+        in_specs=[vmem, vmem],
         out_specs=vmem,
         out_shape=jax.ShapeDtypeStruct((rows // 2, 2 * mine), bf16),
-        scratch_shapes=[pltpu.VMEM((2 * mine, block), bf16)],
-        compiler_params=params(),
-        name="first_update",
-    )(inverse, picked)
-
-
-def second_operator(first, second, inverse, step, width, scale):
-    depth, picks = first[0].shape
-    count = len(first)
-    block = picks * count
-    mine = inverse.shape[1]
-    rows = (second[0].shape[0] - depth) // 2
-    wide = 2 * picks
-
-    def body(inverse_ref, *refs):
-        first_ref, second_ref = refs[:count], refs[count : 2 * count]
-        operator_ref, base_ref, turned, stacked, kernel, meet = refs[2 * count :]
-        stack_inverse(inverse_ref, picks, stacked)
+        compiler_params=params(),
+    )(stacked, picked)
+
+
+def meeting_kernel(owners, index, pieces, second, scale):
+    depth, picks = second.shape
+    count = len(pieces)
+
+    def body(owners_ref, index_ref, second_ref, *refs):
+        pieces_ref, out_ref = refs[:count], refs[-1]
         for k in range(count):
-            turned[k * picks : (k + 1) * picks, :] = jnp.transpose(second_ref[k][0:depth, :])
-        base = jnp.zeros((2 * rows, 2 * mine), f32)
-        lanes = lax.broadcasted_iota(jnp.int32, (picks, picks), 1) + 1
-        for k in range(count):
-            base = base + matmul_nt(second_ref[k][depth:, :], stacked[:, k * picks : (k + 1) * picks])
-            place = turned[k * picks : (k + 1) * picks, width + 18 : width + 20].astype(f32)
-            place = (place[:, 0:1] * LANES + place[:, 1:2]).astype(jnp.int32)
-            meet[k * picks : (k + 1) * picks, :] = jnp.where(place == lanes, penalty, 0.0).astype(bf16)
-        for n in range(0, count, 2):
-            columns = jnp.concatenate([first_ref[n][...], first_ref[n + 1][...]], 1)
-            for k in range(count):
-                here = slice(k * picks, (k + 1) * picks)
-                inner = matmul(turned[here, :], columns)
-                kernel[here, :] = jnp.exp2(inner * scale).astype(bf16)
-            for k in (n, n + 1):
-                here = slice(k * picks, (k + 1) * picks)
-                there = slice((k - n) * picks, (k - n + 1) * picks)
-                kernel[here, there] = kernel[here, there] + meet[here, :]
-            product = matmul(stacked[...], kernel[...])
-            high, low = split(product[0:mine, :] + product[mine:, :], 2)
-            operator_ref[0:mine, n * picks : n * picks + wide] = high
-            operator_ref[mine:, n * picks : n * picks + wide] = low
-        base = base[:rows] + base[rows:]
-        base_ref[...] = base[:, :mine] + base[:, mine:]
-
-    flops = 2 * block * block * (depth + 2 * mine)
-    return pl.pallas_call(
-        body,
-        grid=(1,),
-        in_specs=[pl.BlockSpec((1, mine, block), lambda i: (step, 0, 0))] + [vmem] * (2 * count),
-        out_specs=(vmem, vmem),
-        out_shape=(
-            jax.ShapeDtypeStruct((2 * mine, block), bf16),
-            jax.ShapeDtypeStruct((rows, mine), f32),
+            inner = matmul(jnp.transpose(pieces_ref[k][...]), second_ref[...])
+            kernel = jnp.exp2(inner * scale).astype(bf16)
+            if k == 0:
+                same = turn(index_ref[0:1, :]) == index_ref[1:2, :]
+                bonus = jnp.where(owners_ref[0] == owners_ref[1], penalty, 0.0)
+                kernel = kernel + jnp.where(same, bonus, 0.0).astype(bf16)
+            out_ref[k * picks : (k + 1) * picks, :] = kernel
+
+    return pl.pallas_call(
+        body,
+        in_specs=[smem, vmem, vmem] + [vmem] * count,
+        out_specs=vmem,
+        out_shape=jax.ShapeDtypeStruct((count * picks, picks), bf16),
+        cost_estimate=pl.CostEstimate(
+            flops=2 * count * picks * picks * depth, transcendentals=count * picks * picks, bytes_accessed=10**6
         ),
-        scratch_shapes=[
-            pltpu.VMEM((block, depth), bf16),
-            pltpu.VMEM((2 * mine, block), bf16),
-            pltpu.VMEM((block, wide), bf16),
-            pltpu.VMEM((block, picks), bf16),
-        ],
-        cost_estimate=pl.CostEstimate(flops=flops, transcendentals=block * block, bytes_accessed=10**7),
-        compiler_params=params(),
-        name="second_operator",
-    )(inverse, *first, *second)
+        compiler_params=params(),
+        name="meeting_kernel",
+    )(owners, index, second, *pieces)
+
+
+def advance(kernel, before, pieces, scaled):
+    rows, picks = before.shape
+    block = kernel.shape[0]
+    count = len(pieces)
+
+    def body(kernel_ref, before_ref, *refs):
+        pieces_ref, out_ref, canon = refs[:count], refs[-2], refs[-1]
+        unfold(pieces_ref, pieces[0].shape[0] * 2 // rows, picks, canon)
+        out_ref[...] = (before_ref[...] - matmul(canon[...], kernel_ref[...])) * scaled
+
+    return pl.pallas_call(
+        body,
+        in_specs=[vmem] * (2 + count),
+        out_specs=vmem,
+        out_shape=jax.ShapeDtypeStruct((rows, picks), f32),
+        scratch_shapes=[pltpu.VMEM((rows, block), bf16)],
+        compiler_params=params(),
+        name="advance",
+    )(kernel, before, *pieces)
 
 
 def block_kernel(pieces, local, scale):
@@ -308,28 +295,6 @@
             canon[half:, place] = lower.astype(bf16)
 
 
-def second_update(pieces, operator, base, picks):
-    rows, mine = base.shape
-    block = operator.shape[1]
-    count = len(pieces)
-
-    def body(operator_ref, base_ref, *refs):
-        pieces_ref, out_ref, canon = refs[:count], refs[-2], refs[-1]
-        unfold(pieces_ref, pieces[0].shape[0] * 2 // rows, picks, canon)
-        product = matmul_nt(canon[...], operator_ref[...])
-        out_ref[...] = fold(base_ref[...] - (product[:, :mine] + product[:, mine:]))
-
-    return pl.pallas_call(
-        body,
-        in_specs=[vmem] * (2 + count),
-        out_specs=vmem,
-        out_shape=jax.ShapeDtypeStruct((rows // 2, 2 * mine), bf16),
-        scratch_shapes=[pltpu.VMEM((rows, block), bf16)],
-        compiler_params=params(),
-        name="second_update",
-    )(operator, base, *pieces)
-
-
 def apply_update(owners, pieces, kernel, index, step, residual_t, coeffs_t):
     outputs, frames = residual_t.shape
     block = kernel.shape[0]
@@ -377,7 +342,6 @@
 class Sender:
     def __init__(self, rows, cols):
         self.rows, self.cols, self.chips = rows, cols, cols // 2
-        self.row = lax.axis_index("rows")
 
     def send(self, value, row=None, chip_step=0, core_step=0):
         pairs = []
@@ -390,34 +354,10 @@
             pairs.append((i, to * self.cols + col))
         return lax.ppermute(value, ("rows", "cols"), pairs)
 
-    def doubling(self, value, owner):
-        step = 1
-        while step < self.rows:
-            other = self.send(value, row=lambda at, step=step: at ^ step)
-            value = jnp.where(((owner ^ self.row) & step) != 0, other, value)
-            step *= 2
-        return value
-
-    def along(self, value, owner):
-        count, row = self.rows, self.row
-        half = count // 2
-        lower = row < half
-        moves = []
-        for s in range(half - 1):
-            moves.append((s, {s: s + 1, count - 1 - s: count - 2 - s}))
-        moves.append((None, {half - 1: half, half: half - 1}))
-        for s in reversed(range(half - 1)):
-            moves.append((~s, {s + 1: s, count - 2 - s: count - 1 - s}))
-        for s, move in moves:
-            other = self.send(value, row=move.get)
-            if s is None:
-                take = ((row == half - 1) & (owner >= half)) | ((row == half) & (owner < half))
-            elif s >= 0:
-                take = ((row == s + 1) & (owner <= s)) | ((row == count - 2 - s) & (owner >= count - 1 - s))
-            else:
-                s = ~s
-                take = ((row == s) & (owner > s)) | ((row == count - 1 - s) & (owner < count - 1 - s))
-            value = jnp.where(take, other, value)
+    def spread(self, value, moves, takes):
+        for move, take in zip(moves, takes):
+            other = self.send(value, row=move)
+            value = jnp.where(take > 0.5, other, value)
         return value
 
     def over_rows(self, value):
@@ -425,30 +365,45 @@
         got = {k: self.send(value, row=lambda at, k=k: at ^ k) for k in steps}
         return [value] + [got[k] for k in range(1, self.rows)]
 
+    def over_cores(self, values):
+        return [side for v in values for side in (v, self.send(v, core_step=1))]
+
     def over_cols(self, value):
-        found = []
-        for k in range(self.chips):
-            mine = value if k == 0 else self.send(value, chip_step=k)
-            found += [mine, self.send(mine, core_step=1)]
-        return found
+        values = [value] + [self.send(value, chip_step=k) for k in range(1, self.chips)]
+        return self.over_cores(values)
+
+
+def doubling(rows):
+    steps = [1 << k for k in range(rows.bit_length() - 1)]
+    moves = [lambda at, step=step: at ^ step for step in steps]
+    rules = [lambda row, owner, step=step: ((row ^ owner) & step) != 0 for step in steps]
+    return moves, rules
 
 
 def per_device_pieces(rows, cols, features, residual, coeffs, block_inverse, block_index, owners):
     scale = 2.0 / features.shape[1] * 1.4426950408889634
     sender = Sender(rows, cols)
-    width, picks = features.shape[1], block_index.shape[1]
+    picks = block_index.shape[1]
+    moves, rules = doubling(rows)
+    scaled = 2.0**-4 * (2048 / block_inverse.shape[2]) ** 2
     features_t, residual_t, coeffs_t = features.T, residual.T, coeffs.T
-    first = pick_residual(block_index, residual_t)
-    first = sender.over_cols(sender.doubling(first.astype(f16), owners[0]))
-    local, first_block, second_block = pick_features(owners, block_index, features_t, residual_t)
-    first_block = sender.over_cols(sender.along(first_block, owners[0]))
-    second_block = sender.over_cols(sender.along(second_block, owners[1]))
-    update = first_update(jnp.concatenate(first, 1).astype(f32), block_inverse, 0, picks)
+    first, second = pick_residual(block_index, residual_t)
+    first_block, second_block, *takes = pick_features(
+        owners, block_index, features_t, [(step, rule) for step in range(2) for rule in rules]
+    )
+    local, *stacked = prepare(features_t, block_inverse, picks)
+    first = sender.over_cols(sender.spread(first.astype(f16), moves, takes))
+    first_block = sender.over_cols(sender.spread(first_block, moves, takes))
+    second = sender.spread(second.astype(f16), moves, takes[len(rules) :]).astype(f32)
+    second_block = sender.spread(second_block, moves, takes[len(rules) :])
+    update = block_update(jnp.concatenate(first, 1).astype(f32), stacked[0], 1.0)
     update = sender.over_cols(jnp.concatenate(sender.over_rows(update), 0))
+    meeting = meeting_kernel(owners, block_index, first_block, second_block, scale)
+    second = sender.over_cols(advance(meeting, second, update, scaled).astype(f16))
     first_kernel = block_kernel(first_block, local, scale)
-    operator, base = second_operator(first_block, second_block, block_inverse, 1, width, scale)
-    later = second_update(update, operator, base, picks)
+    later = block_update(jnp.concatenate(second, 1).astype(f32), stacked[1], 1.0 / scaled)
     later = sender.over_cols(jnp.concatenate(sender.over_rows(later), 0))
+    second_block = sender.over_cols(second_block)
     second_kernel = block_kernel(second_block, local, scale)
     residual_t, coeffs_t = apply_update(
         owners, update, first_kernel, block_index, 0, residual_t, coeffs_t

time: 137 us -> 126 us (0.920)
  between operations: 9.58 us -> 1.08 us
  waiting for transfers between devices: 32.8 us -> 38.2 us
  Pallas kernels: 32.8 us -> 28.3 us
    ppermute x49 -> x56, waiting for transfers between devices: 32.8 us -> 38.2 us  [send(): return lax.ppermute(value, ('rows', 'cols'), pairs)]
    pallas_call x5 -> x7, Pallas kernels: 10.8 us -> 6.29 us  [the longest x1 1.69 us: pick_features(): pl.pallas_call(body, in_specs=[smem, vmem, vmem], out_specs=(vmem,) * (st...]
    ppermute x49 -> x56, starting transfers between devices: 54.5 us -> 53.7 us  [send(): return lax.ppermute(value, ('rows', 'cols'), pairs)]
    unnamed x26 -> x30, local copies, waits for them, and re-layouts: 4.86 us -> 4.28 us
  transfers between devices with their start and end apart: 49 -> 56, of which waited for: 12 -> 17; matrix products, arithmetic and copies ran while one was open for 1% -> 1% of each run, Pallas kernels for 19% -> 17%
where the time goes in v1:
time: 126 us
  starting transfers between devices  53.7 us (43%)
  waiting for transfers between devices  38.2 us (30%)
  Pallas kernels  28.3 us (22%)
  local copies, waits for them, and re-layouts  4.31 us (3%)
    ppermute x56, starting transfers between devices, send(): return lax.ppermute(value, ('rows', 'cols'), pairs)  53.7 us
    ppermute x56, waiting for transfers between devices, send(): return lax.ppermute(value, ('rows', 'cols'), pairs)  38.2 us
    pallas_call x2, Pallas kernels, block_kernel(): pl.pallas_call(body, grid=(frames // tile,), in_specs=[pl.BlockSpec((dept...  13 us
    pallas_call x2, Pallas kernels, apply_update(): pl.pallas_call(body, grid=(frames // tile,), in_specs=[smem, vmem, pl.Blo...  9.07 us
    unnamed x30, local copies, waits for them, and re-layouts  4.28 us
  transfers between devices with their start and end apart: 56, of which 17 were waited for; matrix products, arithmetic and copies ran while one was open for 1% of the time, Pallas kernels for 17%

profile of v1, /device:TPU:0, one launch (start us, length us, event | category | flops | bytes accessed | tf_op | source)
XLA Modules:
  0.0 126.2 jit_solution(10614791943144209398)
XLA Ops:
  0.6 1.5 %copy-done = bf16[2048,440]{0,1:T(8,128)(2,1)S(1)} copy-done((bf16[2048,440]{0,1:T(8,128)(2,1)S(1)}, bf16[2048,440]{0,1:T(8,128)(2,1)}, u32[]{:S(2)}) %copy-start) | copy-done | bytes 1802264
  2.1 0.7 copy-done.5
  2.8 0.7 copy-done.7
  3.5 1.7 %pick_features.1 = (bf16[464,256]{1,0:T(8,128)(2,1)S(1)}, bf16[464,256]{1,0:T(8,128)(2,1)S(1)}, f32[1,256]{1,0:T(1,128)S(1)}, f32[1,256]{1,0:T(1,128)S(1)}, f32[1,256]{1,0:T(1,128)S(1)}, /*index=5*/f32[1,256]{1,0:T(1,128)S(1)}) custom-call(s32[2]{0:T(128)S(1)} %copy-done.7, s32[2,256]{1,0:T(2,128)S(1)} %copy-done.5, bf16[440,2048]{1,0:T(8,128)(2,1)S(1)} %bitcast.5), custom_call_target="tpu_custom_call" | custom-call | tf_op jit(solution)/shard_map/pick_features/pallas_call | solution.py:120
  5.2 3.1 %collective-permute-start.9 = (bf16[464,256]{1,0:T(8,128)(2,1)S(1)}, bf16[464,256]{1,0:T(8,128)(2,1)S(1)}, u32[]{:S(2)}, u32[]{:S(2)}) collective-permute-start(bf16[464,256]{1,0:T(8,128)(2,1)S(1)} %get-tuple-element.23), channel_id=1, source_target_pairs={{0,8},{1,9},{2,10},{3,11},{4,12},{5,13},{6,14},{7,15},{8,0},{9,1},... | collective-permute-start | bytes 712712 | tf_op jit(solution)/shard_map/ppermute | solution.py:355
  8.4 0.9 pick_residual.1
  9.3 2.0 %collective-permute-start.18 = (f16[160,256]{1,0:T(8,128)(2,1)S(1)}, f16[160,256]{1,0:T(8,128)(2,1)S(1)}, u32[]{:S(2)}, u32[]{:S(2)}) collective-permute-start(f16[160,256]{1,0:T(8,128)(2,1)S(1)} %convert_element_type.18), channel_id=1, source_target_pairs={{0,8},{1,9},{2,10},{3,11},{4,12},{5,13},{6,14},{7,15},{8,0},{9,1},... | collective-permute-start | bytes 245768 | tf_op jit(solution)/shard_map/ppermute | solution.py:355
  11.5 10.3 %collective-permute-done.18 = f16[160,256]{1,0:T(8,128)(2,1)S(1)} collective-permute-done((f16[160,256]{1,0:T(8,128)(2,1)S(1)}, f16[160,256]{1,0:T(8,128)(2,1)S(1)}, u32[]{:S(2)}, u32[]{:S(2)}) %collective-permute-start.18) | collective-permute-done | bytes 81952 | tf_op jit(solution)/shard_map/ppermute | solution.py:355
  21.8 2.8 %collective-permute-start.19 = (f16[160,256]{1,0:T(8,128)(2,1)S(1)}, f16[160,256]{1,0:T(8,128)(2,1)S(1)}, u32[]{:S(2)}, u32[]{:S(2)}) collective-permute-start(f16[160,256]{1,0:T(8,128)(2,1)S(1)} %broadcast_select_fusion.5), channel_id=1, source_target_pairs={{0,16},{1,17},{2,18},{3,19},{4,20},{5,21},{6,22},{7,23},{8,24},{9,... | collective-permute-start | bytes 245768 | tf_op jit(solution)/shard_map/ppermute | solution.py:355
  24.7 1.2 copy-done.4
  26.3 0.9 collective-permute-done.19
  27.3 1.7 %collective-permute-start.21 = (f16[160,256]{1,0:T(8,128)(2,1)S(1)}, f16[160,256]{1,0:T(8,128)(2,1)S(1)}, u32[]{:S(2)}, u32[]{:S(2)}) collective-permute-start(f16[160,256]{1,0:T(8,128)(2,1)S(1)} %get-tuple-element.35), channel_id=1, source_target_pairs={{0,2},{1,3},{2,0},{3,1},{4,6},{5,7},{6,4},{7,5},{8,10},{9,11},{10,... | collective-permute-start | bytes 245768 | tf_op jit(solution)/shard_map/ppermute | solution.py:355
  29.1 1.5 %collective-permute-start.23 = (f16[160,256]{1,0:T(8,128)(2,1)S(1)}, f16[160,256]{1,0:T(8,128)(2,1)S(1)}, u32[]{:S(2)}, u32[]{:S(2)}) collective-permute-start(f16[160,256]{1,0:T(8,128)(2,1)S(1)} %get-tuple-element.35), channel_id=1, source_target_pairs={{0,4},{1,5},{2,6},{3,7},{4,0},{5,1},{6,2},{7,3},{8,12},{9,13},{10,... | collective-permute-start | bytes 245768 | tf_op jit(solution)/shard_map/ppermute | solution.py:355
  30.6 0.6 collective-permute-start.25
  31.2 0.9 collective-permute-done.21
  32.2 2.2 %collective-permute-done.23 = f16[160,256]{1,0:T(8,128)(2,1)S(1)} collective-permute-done((f16[160,256]{1,0:T(8,128)(2,1)S(1)}, f16[160,256]{1,0:T(8,128)(2,1)S(1)}, u32[]{:S(2)}, u32[]{:S(2)}) %collective-permute-start.23) | collective-permute-done | bytes 81952 | tf_op jit(solution)/shard_map/ppermute | solution.py:355
  34.4 2.7 %collective-permute-start.10 = (bf16[464,256]{1,0:T(8,128)(2,1)S(1)}, bf16[464,256]{1,0:T(8,128)(2,1)S(1)}, u32[]{:S(2)}, u32[]{:S(2)}) collective-permute-start(bf16[464,256]{1,0:T(8,128)(2,1)S(1)} %broadcast_select_fusion), channel_id=1, source_target_pairs={{0,16},{1,17},{2,18},{3,19},{4,20},{5,21},{6,22},{7,23},{8,24},{9,... | collective-permute-start | bytes 712712 | tf_op jit(solution)/shard_map/ppermute | solution.py:355
  37.1 0.5 collective-permute-start.26
  37.6 0.7 collective-permute-done.24
  38.6 0.7 shard_map.79
  39.3 2.3 %collective-permute-start.27 = (bf16[80,128]{1,0:T(8,128)(2,1)S(1)}, bf16[80,128]{1,0:T(8,128)(2,1)S(1)}, u32[]{:S(2)}, u32[]{:S(2)}) collective-permute-start(bf16[80,128]{1,0:T(8,128)(2,1)S(1)} %shard_map.79), channel_id=1, source_target_pairs={{0,8},{1,9},{2,10},{3,11},{4,12},{5,13},{6,14},{7,15},{8,0},{9,1},... | collective-permute-start | bytes 61448 | tf_op jit(solution)/shard_map/ppermute | solution.py:355
  41.6 1.6 %collective-permute-start.28 = (bf16[80,128]{1,0:T(8,128)(2,1)S(1)}, bf16[80,128]{1,0:T(8,128)(2,1)S(1)}, u32[]{:S(2)}, u32[]{:S(2)}) collective-permute-start(bf16[80,128]{1,0:T(8,128)(2,1)S(1)} %shard_map.79), channel_id=1, source_target_pairs={{0,16},{1,17},{2,18},{3,19},{4,20},{5,21},{6,22},{7,23},{8,24},{9,... | collective-permute-start | bytes 61448 | tf_op jit(solution)/shard_map/ppermute | solution.py:355
  43.3 0.8 collective-permute-start.29
  44.1 2.2 %collective-permute-start.38 = (f16[160,256]{1,0:T(8,128)(2,1)S(1)}, f16[160,256]{1,0:T(8,128)(2,1)S(1)}, u32[]{:S(2)}, u32[]{:S(2)}) collective-permute-start(f16[160,256]{1,0:T(8,128)(2,1)S(1)} %broadcast_select_fusion.4), channel_id=1, source_target_pairs={{0,16},{1,17},{2,18},{3,19},{4,20},{5,21},{6,22},{7,23},{8,24},{9,... | collective-permute-start | bytes 245768 | tf_op jit(solution)/shard_map/ppermute | solution.py:355
  46.3 2.0 %collective-permute-done.28 = bf16[80,128]{1,0:T(8,128)(2,1)S(1)} collective-permute-done((bf16[80,128]{1,0:T(8,128)(2,1)S(1)}, bf16[80,128]{1,0:T(8,128)(2,1)S(1)}, u32[]{:S(2)}, u32[]{:S(2)}) %collective-permute-start.28) | collective-permute-done | bytes 20512 | tf_op jit(solution)/shard_map/ppermute | solution.py:355
  48.3 0.6 collective-permute-done.29
  48.9 2.8 %collective-permute-start.31 = (bf16[320,128]{1,0:T(8,128)(2,1)S(1)}, bf16[320,128]{1,0:T(8,128)(2,1)S(1)}, u32[]{:S(2)}, u32[]{:S(2)}) collective-permute-start(bf16[320,128]{1,0:T(8,128)(2,1)S(1)} %pad_maximum_fusion.refs_0_), channel_id=1, source_target_pairs={{0,2},{1,3},{2,0},{3,1},{4,6},{5,7},{6,4},{7,5},{8,10},{9,11},{10,... | collective-permute-start | bytes 245768 | tf_op jit(solution)/shard_map/ppermute | solution.py:355
  51.8 2.4 %collective-permute-start.33 = (bf16[320,128]{1,0:T(8,128)(2,1)S(1)}, bf16[320,128]{1,0:T(8,128)(2,1)S(1)}, u32[]{:S(2)}, u32[]{:S(2)}) collective-permute-start(bf16[320,128]{1,0:T(8,128)(2,1)S(1)} %pad_maximum_fusion.refs_0_), channel_id=1, source_target_pairs={{0,4},{1,5},{2,6},{3,7},{4,0},{5,1},{6,2},{7,3},{8,12},{9,13},{10,... | collective-permute-start | bytes 245768 | tf_op jit(solution)/shard_map/ppermute | solution.py:355
  54.2 1.5 %collective-permute-start.12 = (bf16[464,256]{1,0:T(8,128)(2,1)S(1)}, bf16[464,256]{1,0:T(8,128)(2,1)S(1)}, u32[]{:S(2)}, u32[]{:S(2)}) collective-permute-start(bf16[464,256]{1,0:T(8,128)(2,1)S(1)} %broadcast_select_fusion.1.refs_0_), channel_id=1, source_target_pairs={{0,2},{1,3},{2,0},{3,1},{4,6},{5,7},{6,4},{7,5},{8,10},{9,11},{10,... | collective-permute-start | bytes 712712 | tf_op jit(solution)/shard_map/ppermute | solution.py:355
  55.7 2.0 %collective-permute-start.14 = (bf16[464,256]{1,0:T(8,128)(2,1)S(1)}, bf16[464,256]{1,0:T(8,128)(2,1)S(1)}, u32[]{:S(2)}, u32[]{:S(2)}) collective-permute-start(bf16[464,256]{1,0:T(8,128)(2,1)S(1)} %broadcast_select_fusion.1.refs_0_), channel_id=1, source_target_pairs={{0,4},{1,5},{2,6},{3,7},{4,0},{5,1},{6,2},{7,3},{8,12},{9,13},{10,... | collective-permute-start | bytes 712712 | tf_op jit(solution)/shard_map/ppermute | solution.py:355
  57.8 2.1 %collective-permute-start.1 = (bf16[464,256]{1,0:T(8,128)(2,1)S(1)}, bf16[464,256]{1,0:T(8,128)(2,1)S(1)}, u32[]{:S(2)}, u32[]{:S(2)}) collective-permute-start(bf16[464,256]{1,0:T(8,128)(2,1)S(1)} %broadcast_select_fusion.2), channel_id=1, source_target_pairs={{0,16},{1,17},{2,18},{3,19},{4,20},{5,21},{6,22},{7,23},{8,24},{9,... | collective-permute-start | bytes 712712 | tf_op jit(solution)/shard_map/ppermute | solution.py:355
  59.9 0.8 collective-permute-start.16
  60.7 0.8 collective-permute-done.12.refs_2_
  61.5 5.9 %collective-permute-done.14.refs_4_ = bf16[464,256]{1,0:T(8,128)(2,1)S(1)} collective-permute-done((bf16[464,256]{1,0:T(8,128)(2,1)S(1)}, bf16[464,256]{1,0:T(8,128)(2,1)S(1)}, u32[]{:S(2)}, u32[]{:S(2)}) %collective-permute-start.14) | collective-permute-done | bytes 237600 | tf_op jit(solution)/shard_map/ppermute | solution.py:355
  67.4 2.0 %collective-permute-done.1 = bf16[464,256]{1,0:T(8,128)(2,1)S(1)} collective-permute-done((bf16[464,256]{1,0:T(8,128)(2,1)S(1)}, bf16[464,256]{1,0:T(8,128)(2,1)S(1)}, u32[]{:S(2)}, u32[]{:S(2)}) %collective-permute-start.1) | collective-permute-done | bytes 237600 | tf_op jit(solution)/shard_map/ppermute | solution.py:355
  69.4 0.5 collective-permute-start.32
  70.0 0.4 collective-permute-start.36
  70.6 1.4 %collective-permute-done.17.refs_7_ = bf16[464,256]{1,0:T(8,128)(2,1)S(1)} collective-permute-done((bf16[464,256]{1,0:T(8,128)(2,1)S(1)}, bf16[464,256]{1,0:T(8,128)(2,1)S(1)}, u32[]{:S(2)}, u32[]{:S(2)}) %collective-permute-start.17) | collective-permute-done | bytes 237600 | tf_op jit(solution)/shard_map/ppermute | solution.py:355
  72.0 1.4 %meeting_kernel.1.kernel_ref = bf16[2048,256]{1,0:T(8,128)(2,1)S(1)} custom-call(s32[2]{0:T(128)S(1)} %copy-done.8, s32[2,256]{1,0:T(2,128)S(1)} %copy-done.6, bf16[464,256]{1,0:T(8,128)(2,1)S(1)} %broadcast_select_fusion.3.refs_0_.second_ref, bf16[464,256]{1,0:T(8,128)(2,1)S(1)} %broadcast_select_fusion.1.refs_0_, ...), custom_call_target="tpu_custom_call" | custom-call | flops 486539264 | bytes 1000000 | tf_op jit(solution)/shard_map/meeting_kernel/pallas_call | solution.py:206
  73.4 0.7 advance.1
  74.7 1.7 %collective-permute-start.3 = (bf16[464,256]{1,0:T(8,128)(2,1)S(1)}, bf16[464,256]{1,0:T(8,128)(2,1)S(1)}, u32[]{:S(2)}, u32[]{:S(2)}) collective-permute-start(bf16[464,256]{1,0:T(8,128)(2,1)S(1)} %broadcast_select_fusion.3.refs_0_.second_ref), channel_id=1, source_target_pairs={{0,2},{1,3},{2,0},{3,1},{4,6},{5,7},{6,4},{7,5},{8,10},{9,11},{10,... | collective-permute-start | bytes 712712 | tf_op jit(solution)/shard_map/ppermute | solution.py:355
  76.7 1.6 %collective-permute-start.42 = (f16[160,256]{1,0:T(8,128)(2,1)S(1)}, f16[160,256]{1,0:T(8,128)(2,1)S(1)}, u32[]{:S(2)}, u32[]{:S(2)}) collective-permute-start(f16[160,256]{1,0:T(8,128)(2,1)S(1)} %get-tuple-element.33), channel_id=1, source_target_pairs={{0,4},{1,5},{2,6},{3,7},{4,0},{5,1},{6,2},{7,3},{8,12},{9,13},{10,... | collective-permute-start | bytes 245768 | tf_op jit(solution)/shard_map/ppermute | solution.py:355
  78.4 0.4 collective-permute-start.44
  78.8 0.9 collective-permute-done.40
  79.7 7.7 %collective-permute-done.42 = f16[160,256]{1,0:T(8,128)(2,1)S(1)} collective-permute-done((f16[160,256]{1,0:T(8,128)(2,1)S(1)}, f16[160,256]{1,0:T(8,128)(2,1)S(1)}, u32[]{:S(2)}, u32[]{:S(2)}) %collective-permute-start.42) | collective-permute-done | bytes 81952 | tf_op jit(solution)/shard_map/ppermute | solution.py:355
  87.4 0.4 collective-permute-start.7
  87.8 0.5 collective-permute-start.45
  88.3 0.7 collective-permute-done.43
  89.3 0.6 shard_map.81
  90.0 1.4 %collective-permute-start.46 = (bf16[80,128]{1,0:T(8,128)(2,1)S(1)}, bf16[80,128]{1,0:T(8,128)(2,1)S(1)}, u32[]{:S(2)}, u32[]{:S(2)}) collective-permute-start(bf16[80,128]{1,0:T(8,128)(2,1)S(1)} %shard_map.81), channel_id=1, source_target_pairs={{0,8},{1,9},{2,10},{3,11},{4,12},{5,13},{6,14},{7,15},{8,0},{9,1},... | collective-permute-start | bytes 61448 | tf_op jit(solution)/shard_map/ppermute | solution.py:355
  91.4 3.0 %collective-permute-start.47 = (bf16[80,128]{1,0:T(8,128)(2,1)S(1)}, bf16[80,128]{1,0:T(8,128)(2,1)S(1)}, u32[]{:S(2)}, u32[]{:S(2)}) collective-permute-start(bf16[80,128]{1,0:T(8,128)(2,1)S(1)} %shard_map.81), channel_id=1, source_target_pairs={{0,16},{1,17},{2,18},{3,19},{4,20},{5,21},{6,22},{7,23},{8,24},{9,... | collective-permute-start | bytes 61448 | tf_op jit(solution)/shard_map/ppermute | solution.py:355
  94.4 0.5 collective-permute-start.4
  95.0 0.5 collective-permute-start.8
  95.4 0.9 collective-permute-done.47
  96.3 3.1 %collective-permute-start.48 = (bf16[80,128]{1,0:T(8,128)(2,1)S(1)}, bf16[80,128]{1,0:T(8,128)(2,1)S(1)}, u32[]{:S(2)}, u32[]{:S(2)}) collective-permute-start(bf16[80,128]{1,0:T(8,128)(2,1)S(1)} %shard_map.81), channel_id=1, source_target_pairs={{0,24},{1,25},{2,26},{3,27},{4,28},{5,29},{6,30},{7,31},{8,16},{9,... | collective-permute-start | bytes 61448 | tf_op jit(solution)/shard_map/ppermute | solution.py:355
  99.4 6.5 %shard_map.78.kernel_ref = bf16[2048,2048]{1,0:T(8,128)(2,1)S(1)} custom-call(bf16[464,2048]{1,0:T(8,128)(2,1)S(1)} %get-tuple-element.17.local_ref, bf16[464,256]{1,0:T(8,128)(2,1)S(1)} %broadcast_select_fusion.1.refs_0_, bf16[464,256]{1,0:T(8,128)(2,1)S(1)} %collective-permute-done.11.refs_1_, bf16[464,256]{1,0:T(8,128)(2,1)S(1)} %collective-permute-done.12.refs_2_, ...), custom_call_target="tpu_custom_call" | custom-call | flops 3892314112 | bytes 10000000 | tf_op jit(solution)/shard_map/pallas_call | solution.py:260
  105.9 1.2 collective-permute-start.50
  107.1 0.6 collective-permute-start.52
  107.7 1.8 %collective-permute-start.54 = (bf16[320,128]{1,0:T(8,128)(2,1)S(1)}, bf16[320,128]{1,0:T(8,128)(2,1)S(1)}, u32[]{:S(2)}, u32[]{:S(2)}) collective-permute-start(bf16[320,128]{1,0:T(8,128)(2,1)S(1)} %pad_maximum_fusion.1.refs_0_), channel_id=1, source_target_pairs={{0,6},{1,7},{2,4},{3,5},{4,2},{5,3},{6,0},{7,1},{8,14},{9,15},{10,... | collective-permute-start | bytes 245768 | tf_op jit(solution)/shard_map/ppermute | solution.py:355
  109.5 6.5 %shard_map.77.kernel_ref = bf16[2048,2048]{1,0:T(8,128)(2,1)S(1)} custom-call(bf16[464,2048]{1,0:T(8,128)(2,1)S(1)} %get-tuple-element.17.local_ref, bf16[464,256]{1,0:T(8,128)(2,1)S(1)} %broadcast_select_fusion.3.refs_0_.second_ref, bf16[464,256]{1,0:T(8,128)(2,1)S(1)} %collective-permute-done.2.refs_1_, ...), custom_call_target="tpu_custom_call" | custom-call | flops 3892314112 | bytes 10000000 | tf_op jit(solution)/shard_map/pallas_call | solution.py:260
  116.1 0.5 collective-permute-start.51
  116.7 0.4 collective-permute-start.55
  117.1 4.2 %shard_map.80 = (f32[147,2048]{1,0:T(8,128)S(1)}, f32[147,2048]{1,0:T(8,128)S(1)}) custom-call(s32[2]{0:T(128)S(1)} %copy-done.8, s32[2,256]{1,0:T(2,128)S(1)} %copy-done.6, bf16[2048,2048]{1,0:T(8,128)(2,1)S(1)} %shard_map.78.kernel_ref, f32[147,2048]{1,0:T(8,128)S(1)} %bitcast.8, f32[147,2048]{1,0:T(8,128)S(1)} %bitcast.9, ...), custom_call_target="tpu_custom_call" | custom-call | flops 1342177280 | bytes 8388608 | tf_op jit(solution)/shard_map/pallas_call | solution.py:325
  121.4 4.8 %shard_map.82 = (f32[147,2048]{1,0:T(8,128)}, f32[147,2048]{1,0:T(8,128)}) custom-call(s32[2]{0:T(128)S(1)} %copy-done.8, s32[2,256]{1,0:T(2,128)S(1)} %copy-done.6, bf16[2048,2048]{1,0:T(8,128)(2,1)S(1)} %shard_map.77.kernel_ref, f32[147,2048]{1,0:T(8,128)S(1)} %get-tuple-element.26.residual_ref, f32[147,2048]{1,0:T(8,128)S(1)} %get-tuple-element.27.coeffs_ref, ...), custom_call_target="tpu_custom_call" | custom-call | flops 1342177280 | bytes 8388608 | tf_op jit(solution)/shard_map/pallas_call | solution.py:325
  (110 shorter events, 3.2 us)
Async XLA Ops:
  0.6 1.5 %copy-start = (bf16[2048,440]{0,1:T(8,128)(2,1)S(1)}, bf16[2048,440]{0,1:T(8,128)(2,1)}, u32[]{:S(2)}) copy-start(bf16[2048,440]{0,1:T(8,128)(2,1)} %param.6) | copy-start | bytes 5406724
  2.1 0.7 copy-start.5
  3.5 4.9 %copy-start.2 = (f32[2048,147]{0,1:T(8,128)S(1)}, f32[2048,147]{0,1:T(8,128)}, u32[]{:S(2)}) copy-start(f32[2048,147]{0,1:T(8,128)} %param.7) | copy-start | bytes 3612676
  5.2 19.5 %copy-start.1 = (bf16[2048,440]{0,1:T(8,128)(2,1)S(1)}, bf16[2048,440]{0,1:T(8,128)(2,1)}, u32[]{:S(2)}) copy-start(bf16[2048,440]{0,1:T(8,128)(2,1)} %param.6) | copy-start | bytes 5406724
  5.2 23.9 %collective-permute-start.9 = (bf16[464,256]{1,0:T(8,128)(2,1)S(1)}, bf16[464,256]{1,0:T(8,128)(2,1)S(1)}, u32[]{:S(2)}, u32[]{:S(2)}) collective-permute-start(bf16[464,256]{1,0:T(8,128)(2,1)S(1)} %get-tuple-element.23), channel_id=1, source_target_pairs={{0,8},{1,9},{2,10},{3,11},{4,12},{5,13},{6,14},{7,15},{8,0},{9,1},... | collective-permute-start | bytes 712712 | tf_op jit(solution)/shard_map/ppermute | solution.py:355
  8.3 47.5 %collective-permute-start = (bf16[464,256]{1,0:T(8,128)(2,1)S(1)}, bf16[464,256]{1,0:T(8,128)(2,1)S(1)}, u32[]{:S(2)}, u32[]{:S(2)}) collective-permute-start(bf16[464,256]{1,0:T(8,128)(2,1)S(1)} %get-tuple-element.20), channel_id=1, source_target_pairs={{0,8},{1,9},{2,10},{3,11},{4,12},{5,13},{6,14},{7,15},{8,0},{9,1},... | collective-permute-start | bytes 712712 | tf_op jit(solution)/shard_map/ppermute | solution.py:355
  9.3 12.5 %collective-permute-start.18 = (f16[160,256]{1,0:T(8,128)(2,1)S(1)}, f16[160,256]{1,0:T(8,128)(2,1)S(1)}, u32[]{:S(2)}, u32[]{:S(2)}) collective-permute-start(f16[160,256]{1,0:T(8,128)(2,1)S(1)} %convert_element_type.18), channel_id=1, source_target_pairs={{0,8},{1,9},{2,10},{3,11},{4,12},{5,13},{6,14},{7,15},{8,0},{9,1},... | collective-permute-start | bytes 245768 | tf_op jit(solution)/shard_map/ppermute | solution.py:355
  11.3 32.0 %collective-permute-start.37 = (f16[160,256]{1,0:T(8,128)(2,1)S(1)}, f16[160,256]{1,0:T(8,128)(2,1)S(1)}, u32[]{:S(2)}, u32[]{:S(2)}) collective-permute-start(f16[160,256]{1,0:T(8,128)(2,1)S(1)} %convert_element_type.20), channel_id=1, source_target_pairs={{0,8},{1,9},{2,10},{3,11},{4,12},{5,13},{6,14},{7,15},{8,0},{9,1},... | collective-permute-start | bytes 245768 | tf_op jit(solution)/shard_map/ppermute | solution.py:355
  21.8 5.4 %collective-permute-start.19 = (f16[160,256]{1,0:T(8,128)(2,1)S(1)}, f16[160,256]{1,0:T(8,128)(2,1)S(1)}, u32[]{:S(2)}, u32[]{:S(2)}) collective-permute-start(f16[160,256]{1,0:T(8,128)(2,1)S(1)} %broadcast_select_fusion.5), channel_id=1, source_target_pairs={{0,16},{1,17},{2,18},{3,19},{4,20},{5,21},{6,22},{7,23},{8,24},{9,... | collective-permute-start | bytes 245768 | tf_op jit(solution)/shard_map/ppermute | solution.py:355
  24.7 1.2 copy-start.4
  27.2 3.4 %collective-permute-start.20 = (f16[160,256]{1,0:T(8,128)(2,1)S(1)}, f16[160,256]{1,0:T(8,128)(2,1)S(1)}, u32[]{:S(2)}, u32[]{:S(2)}) collective-permute-start(f16[160,256]{1,0:T(8,128)(2,1)S(1)} %get-tuple-element.35), channel_id=1, source_target_pairs={{0,1},{1,0},{2,3},{3,2},{4,5},{5,4},{6,7},{7,6},{8,9},{9,8},{10,11... | collective-permute-start | bytes 245768 | tf_op jit(solution)/shard_map/ppermute | solution.py:355
  27.3 4.8 %collective-permute-start.21 = (f16[160,256]{1,0:T(8,128)(2,1)S(1)}, f16[160,256]{1,0:T(8,128)(2,1)S(1)}, u32[]{:S(2)}, u32[]{:S(2)}) collective-permute-start(f16[160,256]{1,0:T(8,128)(2,1)S(1)} %get-tuple-element.35), channel_id=1, source_target_pairs={{0,2},{1,3},{2,0},{3,1},{4,6},{5,7},{6,4},{7,5},{8,10},{9,11},{10,... | collective-permute-start | bytes 245768 | tf_op jit(solution)/shard_map/ppermute | solution.py:355
  29.1 5.3 %collective-permute-start.23 = (f16[160,256]{1,0:T(8,128)(2,1)S(1)}, f16[160,256]{1,0:T(8,128)(2,1)S(1)}, u32[]{:S(2)}, u32[]{:S(2)}) collective-permute-start(f16[160,256]{1,0:T(8,128)(2,1)S(1)} %get-tuple-element.35), channel_id=1, source_target_pairs={{0,4},{1,5},{2,6},{3,7},{4,0},{5,1},{6,2},{7,3},{8,12},{9,13},{10,... | collective-permute-start | bytes 245768 | tf_op jit(solution)/shard_map/ppermute | solution.py:355
  30.6 6.4 %collective-permute-start.25 = (f16[160,256]{1,0:T(8,128)(2,1)S(1)}, f16[160,256]{1,0:T(8,128)(2,1)S(1)}, u32[]{:S(2)}, u32[]{:S(2)}) collective-permute-start(f16[160,256]{1,0:T(8,128)(2,1)S(1)} %get-tuple-element.35), channel_id=1, source_target_pairs={{0,6},{1,7},{2,4},{3,5},{4,2},{5,3},{6,0},{7,1},{8,14},{9,15},{10,... | collective-permute-start | bytes 245768 | tf_op jit(solution)/shard_map/ppermute | solution.py:355
  32.2 4.9 %collective-permute-start.22 = (f16[160,256]{1,0:T(8,128)(2,1)S(1)}, f16[160,256]{1,0:T(8,128)(2,1)S(1)}, u32[]{:S(2)}, u32[]{:S(2)}) collective-permute-start(f16[160,256]{1,0:T(8,128)(2,1)S(1)} %collective-permute-done.21), channel_id=1, source_target_pairs={{0,1},{1,0},{2,3},{3,2},{4,5},{5,4},{6,7},{7,6},{8,9},{9,8},{10,11... | collective-permute-start | bytes 245768 | tf_op jit(solution)/shard_map/ppermute | solution.py:355
  34.4 19.8 %collective-permute-start.10 = (bf16[464,256]{1,0:T(8,128)(2,1)S(1)}, bf16[464,256]{1,0:T(8,128)(2,1)S(1)}, u32[]{:S(2)}, u32[]{:S(2)}) collective-permute-start(bf16[464,256]{1,0:T(8,128)(2,1)S(1)} %broadcast_select_fusion), channel_id=1, source_target_pairs={{0,16},{1,17},{2,18},{3,19},{4,20},{5,21},{6,22},{7,23},{8,24},{9,... | collective-permute-start | bytes 712712 | tf_op jit(solution)/shard_map/ppermute | solution.py:355
  37.1 1.3 %collective-permute-start.24 = (f16[160,256]{1,0:T(8,128)(2,1)S(1)}, f16[160,256]{1,0:T(8,128)(2,1)S(1)}, u32[]{:S(2)}, u32[]{:S(2)}) collective-permute-start(f16[160,256]{1,0:T(8,128)(2,1)S(1)} %collective-permute-done.23), channel_id=1, source_target_pairs={{0,1},{1,0},{2,3},{3,2},{4,5},{5,4},{6,7},{7,6},{8,9},{9,8},{10,11... | collective-permute-start | bytes 245768 | tf_op jit(solution)/shard_map/ppermute | solution.py:355
  37.1 1.4 %collective-permute-start.26 = (f16[160,256]{1,0:T(8,128)(2,1)S(1)}, f16[160,256]{1,0:T(8,128)(2,1)S(1)}, u32[]{:S(2)}, u32[]{:S(2)}) collective-permute-start(f16[160,256]{1,0:T(8,128)(2,1)S(1)} %collective-permute-done.25), channel_id=1, source_target_pairs={{0,1},{1,0},{2,3},{3,2},{4,5},{5,4},{6,7},{7,6},{8,9},{9,8},{10,11... | collective-permute-start | bytes 245768 | tf_op jit(solution)/shard_map/ppermute | solution.py:355
  39.3 4.8 %collective-permute-start.27 = (bf16[80,128]{1,0:T(8,128)(2,1)S(1)}, bf16[80,128]{1,0:T(8,128)(2,1)S(1)}, u32[]{:S(2)}, u32[]{:S(2)}) collective-permute-start(bf16[80,128]{1,0:T(8,128)(2,1)S(1)} %shard_map.79), channel_id=1, source_target_pairs={{0,8},{1,9},{2,10},{3,11},{4,12},{5,13},{6,14},{7,15},{8,0},{9,1},... | collective-permute-start | bytes 61448 | tf_op jit(solution)/shard_map/ppermute | solution.py:355
  41.6 6.7 %collective-permute-start.28 = (bf16[80,128]{1,0:T(8,128)(2,1)S(1)}, bf16[80,128]{1,0:T(8,128)(2,1)S(1)}, u32[]{:S(2)}, u32[]{:S(2)}) collective-permute-start(bf16[80,128]{1,0:T(8,128)(2,1)S(1)} %shard_map.79), channel_id=1, source_target_pairs={{0,16},{1,17},{2,18},{3,19},{4,20},{5,21},{6,22},{7,23},{8,24},{9,... | collective-permute-start | bytes 61448 | tf_op jit(solution)/shard_map/ppermute | solution.py:355
  43.3 5.7 %collective-permute-start.29 = (bf16[80,128]{1,0:T(8,128)(2,1)S(1)}, bf16[80,128]{1,0:T(8,128)(2,1)S(1)}, u32[]{:S(2)}, u32[]{:S(2)}) collective-permute-start(bf16[80,128]{1,0:T(8,128)(2,1)S(1)} %shard_map.79), channel_id=1, source_target_pairs={{0,24},{1,25},{2,26},{3,27},{4,28},{5,29},{6,30},{7,31},{8,16},{9,... | collective-permute-start | bytes 61448 | tf_op jit(solution)/shard_map/ppermute | solution.py:355
  44.1 27.9 %copy-start.6 = (s32[2,256]{1,0:T(2,128)S(1)}, s32[2,256]{1,0:T(2,128)}, u32[]{:S(2)}) copy-start(s32[2,256]{1,0:T(2,128)} %index_ref.9) | copy-start | bytes 6148
  44.1 27.9 %copy-start.8 = (s32[2]{0:T(128)S(1)}, s32[2]{0:T(128)}, u32[]{:S(2)}) copy-start(s32[2]{0:T(128)} %owners_ref.7) | copy-start | bytes 28
  44.1 10.1 %collective-permute-start.38 = (f16[160,256]{1,0:T(8,128)(2,1)S(1)}, f16[160,256]{1,0:T(8,128)(2,1)S(1)}, u32[]{:S(2)}, u32[]{:S(2)}) collective-permute-start(f16[160,256]{1,0:T(8,128)(2,1)S(1)} %broadcast_select_fusion.4), channel_id=1, source_target_pairs={{0,16},{1,17},{2,18},{3,19},{4,20},{5,21},{6,22},{7,23},{8,24},{9,... | collective-permute-start | bytes 245768 | tf_op jit(solution)/shard_map/ppermute | solution.py:355
  48.9 8.9 %collective-permute-start.31 = (bf16[320,128]{1,0:T(8,128)(2,1)S(1)}, bf16[320,128]{1,0:T(8,128)(2,1)S(1)}, u32[]{:S(2)}, u32[]{:S(2)}) collective-permute-start(bf16[320,128]{1,0:T(8,128)(2,1)S(1)} %pad_maximum_fusion.refs_0_), channel_id=1, source_target_pairs={{0,2},{1,3},{2,0},{3,1},{4,6},{5,7},{6,4},{7,5},{8,10},{9,11},{10,... | collective-permute-start | bytes 245768 | tf_op jit(solution)/shard_map/ppermute | solution.py:355
  51.8 8.1 %collective-permute-start.33 = (bf16[320,128]{1,0:T(8,128)(2,1)S(1)}, bf16[320,128]{1,0:T(8,128)(2,1)S(1)}, u32[]{:S(2)}, u32[]{:S(2)}) collective-permute-start(bf16[320,128]{1,0:T(8,128)(2,1)S(1)} %pad_maximum_fusion.refs_0_), channel_id=1, source_target_pairs={{0,4},{1,5},{2,6},{3,7},{4,0},{5,1},{6,2},{7,3},{8,12},{9,13},{10,... | collective-permute-start | bytes 245768 | tf_op jit(solution)/shard_map/ppermute | solution.py:355
  54.2 6.5 %collective-permute-start.35 = (bf16[320,128]{1,0:T(8,128)(2,1)S(1)}, bf16[320,128]{1,0:T(8,128)(2,1)S(1)}, u32[]{:S(2)}, u32[]{:S(2)}) collective-permute-start(bf16[320,128]{1,0:T(8,128)(2,1)S(1)} %pad_maximum_fusion.refs_0_), channel_id=1, source_target_pairs={{0,6},{1,7},{2,4},{3,5},{4,2},{5,3},{6,0},{7,1},{8,14},{9,15},{10,... | collective-permute-start | bytes 245768 | tf_op jit(solution)/shard_map/ppermute | solution.py:355
  54.2 7.3 %collective-permute-start.12 = (bf16[464,256]{1,0:T(8,128)(2,1)S(1)}, bf16[464,256]{1,0:T(8,128)(2,1)S(1)}, u32[]{:S(2)}, u32[]{:S(2)}) collective-permute-start(bf16[464,256]{1,0:T(8,128)(2,1)S(1)} %broadcast_select_fusion.1.refs_0_), channel_id=1, source_target_pairs={{0,2},{1,3},{2,0},{3,1},{4,6},{5,7},{6,4},{7,5},{8,10},{9,11},{10,... | collective-permute-start | bytes 712712 | tf_op jit(solution)/shard_map/ppermute | solution.py:355
  55.7 11.6 %collective-permute-start.14 = (bf16[464,256]{1,0:T(8,128)(2,1)S(1)}, bf16[464,256]{1,0:T(8,128)(2,1)S(1)}, u32[]{:S(2)}, u32[]{:S(2)}) collective-permute-start(bf16[464,256]{1,0:T(8,128)(2,1)S(1)} %broadcast_select_fusion.1.refs_0_), channel_id=1, source_target_pairs={{0,4},{1,5},{2,6},{3,7},{4,0},{5,1},{6,2},{7,3},{8,12},{9,13},{10,... | collective-permute-start | bytes 712712 | tf_op jit(solution)/shard_map/ppermute | solution.py:355
  57.8 11.6 %collective-permute-start.1 = (bf16[464,256]{1,0:T(8,128)(2,1)S(1)}, bf16[464,256]{1,0:T(8,128)(2,1)S(1)}, u32[]{:S(2)}, u32[]{:S(2)}) collective-permute-start(bf16[464,256]{1,0:T(8,128)(2,1)S(1)} %broadcast_select_fusion.2), channel_id=1, source_target_pairs={{0,16},{1,17},{2,18},{3,19},{4,20},{5,21},{6,22},{7,23},{8,24},{9,... | collective-permute-start | bytes 712712 | tf_op jit(solution)/shard_map/ppermute | solution.py:355
  59.9 9.6 %collective-permute-start.16 = (bf16[464,256]{1,0:T(8,128)(2,1)S(1)}, bf16[464,256]{1,0:T(8,128)(2,1)S(1)}, u32[]{:S(2)}, u32[]{:S(2)}) collective-permute-start(bf16[464,256]{1,0:T(8,128)(2,1)S(1)} %broadcast_select_fusion.1.refs_0_), channel_id=1, source_target_pairs={{0,6},{1,7},{2,4},{3,5},{4,2},{5,3},{6,0},{7,1},{8,14},{9,15},{10,... | collective-permute-start | bytes 712712 | tf_op jit(solution)/shard_map/ppermute | solution.py:355
  60.7 9.3 %collective-permute-start.11 = (bf16[464,256]{1,0:T(8,128)(2,1)S(1)}, bf16[464,256]{1,0:T(8,128)(2,1)S(1)}, u32[]{:S(2)}, u32[]{:S(2)}) collective-permute-start(bf16[464,256]{1,0:T(8,128)(2,1)S(1)} %broadcast_select_fusion.1.refs_0_), channel_id=1, source_target_pairs={{0,1},{1,0},{2,3},{3,2},{4,5},{5,4},{6,7},{7,6},{8,9},{9,8},{10,11... | collective-permute-start | bytes 712712 | tf_op jit(solution)/shard_map/ppermute | solution.py:355
  61.5 8.5 %collective-permute-start.13 = (bf16[464,256]{1,0:T(8,128)(2,1)S(1)}, bf16[464,256]{1,0:T(8,128)(2,1)S(1)}, u32[]{:S(2)}, u32[]{:S(2)}) collective-permute-start(bf16[464,256]{1,0:T(8,128)(2,1)S(1)} %collective-permute-done.12.refs_2_), channel_id=1, source_target_pairs={{0,1},{1,0},{2,3},{3,2},{4,5},{5,4},{6,7},{7,6},{8,9},{9,8},{10,11... | collective-permute-start | bytes 712712 | tf_op jit(solution)/shard_map/ppermute | solution.py:355
  67.4 3.1 %collective-permute-start.15 = (bf16[464,256]{1,0:T(8,128)(2,1)S(1)}, bf16[464,256]{1,0:T(8,128)(2,1)S(1)}, u32[]{:S(2)}, u32[]{:S(2)}) collective-permute-start(bf16[464,256]{1,0:T(8,128)(2,1)S(1)} %collective-permute-done.14.refs_4_), channel_id=1, source_target_pairs={{0,1},{1,0},{2,3},{3,2},{4,5},{5,4},{6,7},{7,6},{8,9},{9,8},{10,11... | collective-permute-start | bytes 712712 | tf_op jit(solution)/shard_map/ppermute | solution.py:355
  69.4 3.9 %collective-permute-start.30 = (bf16[320,128]{1,0:T(8,128)(2,1)S(1)}, bf16[320,128]{1,0:T(8,128)(2,1)S(1)}, u32[]{:S(2)}, u32[]{:S(2)}) collective-permute-start(bf16[320,128]{1,0:T(8,128)(2,1)S(1)} %pad_maximum_fusion.refs_0_), channel_id=1, source_target_pairs={{0,1},{1,0},{2,3},{3,2},{4,5},{5,4},{6,7},{7,6},{8,9},{9,8},{10,11... | collective-permute-start | bytes 245768 | tf_op jit(solution)/shard_map/ppermute | solution.py:355
  69.4 3.9 %collective-permute-start.32 = (bf16[320,128]{1,0:T(8,128)(2,1)S(1)}, bf16[320,128]{1,0:T(8,128)(2,1)S(1)}, u32[]{:S(2)}, u32[]{:S(2)}) collective-permute-start(bf16[320,128]{1,0:T(8,128)(2,1)S(1)} %collective-permute-done.31.refs_2_), channel_id=1, source_target_pairs={{0,1},{1,0},{2,3},{3,2},{4,5},{5,4},{6,7},{7,6},{8,9},{9,8},{10,11... | collective-permute-start | bytes 245768 | tf_op jit(solution)/shard_map/ppermute | solution.py:355
  70.0 3.4 %collective-permute-start.34 = (bf16[320,128]{1,0:T(8,128)(2,1)S(1)}, bf16[320,128]{1,0:T(8,128)(2,1)S(1)}, u32[]{:S(2)}, u32[]{:S(2)}) collective-permute-start(bf16[320,128]{1,0:T(8,128)(2,1)S(1)} %collective-permute-done.33.refs_4_), channel_id=1, source_target_pairs={{0,1},{1,0},{2,3},{3,2},{4,5},{5,4},{6,7},{7,6},{8,9},{9,8},{10,11... | collective-permute-start | bytes 245768 | tf_op jit(solution)/shard_map/ppermute | solution.py:355
  70.0 3.4 %collective-permute-start.36 = (bf16[320,128]{1,0:T(8,128)(2,1)S(1)}, bf16[320,128]{1,0:T(8,128)(2,1)S(1)}, u32[]{:S(2)}, u32[]{:S(2)}) collective-permute-start(bf16[320,128]{1,0:T(8,128)(2,1)S(1)} %collective-permute-done.35.refs_6_), channel_id=1, source_target_pairs={{0,1},{1,0},{2,3},{3,2},{4,5},{5,4},{6,7},{7,6},{8,9},{9,8},{10,11... | collective-permute-start | bytes 245768 | tf_op jit(solution)/shard_map/ppermute | solution.py:355
  70.5 1.5 %collective-permute-start.17 = (bf16[464,256]{1,0:T(8,128)(2,1)S(1)}, bf16[464,256]{1,0:T(8,128)(2,1)S(1)}, u32[]{:S(2)}, u32[]{:S(2)}) collective-permute-start(bf16[464,256]{1,0:T(8,128)(2,1)S(1)} %collective-permute-done.16.refs_6_), channel_id=1, source_target_pairs={{0,1},{1,0},{2,3},{3,2},{4,5},{5,4},{6,7},{7,6},{8,9},{9,8},{10,11... | collective-permute-start | bytes 712712 | tf_op jit(solution)/shard_map/ppermute | solution.py:355
  74.1 4.3 %collective-permute-start.39 = (f16[160,256]{1,0:T(8,128)(2,1)S(1)}, f16[160,256]{1,0:T(8,128)(2,1)S(1)}, u32[]{:S(2)}, u32[]{:S(2)}) collective-permute-start(f16[160,256]{1,0:T(8,128)(2,1)S(1)} %get-tuple-element.33), channel_id=1, source_target_pairs={{0,1},{1,0},{2,3},{3,2},{4,5},{5,4},{6,7},{7,6},{8,9},{9,8},{10,11... | collective-permute-start | bytes 245768 | tf_op jit(solution)/shard_map/ppermute | solution.py:355
  74.3 5.3 %collective-permute-start.40 = (f16[160,256]{1,0:T(8,128)(2,1)S(1)}, f16[160,256]{1,0:T(8,128)(2,1)S(1)}, u32[]{:S(2)}, u32[]{:S(2)}) collective-permute-start(f16[160,256]{1,0:T(8,128)(2,1)S(1)} %get-tuple-element.33), channel_id=1, source_target_pairs={{0,2},{1,3},{2,0},{3,1},{4,6},{5,7},{6,4},{7,5},{8,10},{9,11},{10,... | collective-permute-start | bytes 245768 | tf_op jit(solution)/shard_map/ppermute | solution.py:355
  74.7 19.7 %collective-permute-start.3 = (bf16[464,256]{1,0:T(8,128)(2,1)S(1)}, bf16[464,256]{1,0:T(8,128)(2,1)S(1)}, u32[]{:S(2)}, u32[]{:S(2)}) collective-permute-start(bf16[464,256]{1,0:T(8,128)(2,1)S(1)} %broadcast_select_fusion.3.refs_0_.second_ref), channel_id=1, source_target_pairs={{0,2},{1,3},{2,0},{3,1},{4,6},{5,7},{6,4},{7,5},{8,10},{9,11},{10,... | collective-permute-start | bytes 712712 | tf_op jit(solution)/shard_map/ppermute | solution.py:355
  76.4 18.0 %collective-permute-start.5 = (bf16[464,256]{1,0:T(8,128)(2,1)S(1)}, bf16[464,256]{1,0:T(8,128)(2,1)S(1)}, u32[]{:S(2)}, u32[]{:S(2)}) collective-permute-start(bf16[464,256]{1,0:T(8,128)(2,1)S(1)} %broadcast_select_fusion.3.refs_0_.second_ref), channel_id=1, source_target_pairs={{0,4},{1,5},{2,6},{3,7},{4,0},{5,1},{6,2},{7,3},{8,12},{9,13},{10,... | collective-permute-start | bytes 712712 | tf_op jit(solution)/shard_map/ppermute | solution.py:355
  76.7 10.6 %collective-permute-start.42 = (f16[160,256]{1,0:T(8,128)(2,1)S(1)}, f16[160,256]{1,0:T(8,128)(2,1)S(1)}, u32[]{:S(2)}, u32[]{:S(2)}) collective-permute-start(f16[160,256]{1,0:T(8,128)(2,1)S(1)} %get-tuple-element.33), channel_id=1, source_target_pairs={{0,4},{1,5},{2,6},{3,7},{4,0},{5,1},{6,2},{7,3},{8,12},{9,13},{10,... | collective-permute-start | bytes 245768 | tf_op jit(solution)/shard_map/ppermute | solution.py:355
  78.4 9.4 %collective-permute-start.44 = (f16[160,256]{1,0:T(8,128)(2,1)S(1)}, f16[160,256]{1,0:T(8,128)(2,1)S(1)}, u32[]{:S(2)}, u32[]{:S(2)}) collective-permute-start(f16[160,256]{1,0:T(8,128)(2,1)S(1)} %get-tuple-element.33), channel_id=1, source_target_pairs={{0,6},{1,7},{2,4},{3,5},{4,2},{5,3},{6,0},{7,1},{8,14},{9,15},{10,... | collective-permute-start | bytes 245768 | tf_op jit(solution)/shard_map/ppermute | solution.py:355
  79.6 8.1 %collective-permute-start.41 = (f16[160,256]{1,0:T(8,128)(2,1)S(1)}, f16[160,256]{1,0:T(8,128)(2,1)S(1)}, u32[]{:S(2)}, u32[]{:S(2)}) collective-permute-start(f16[160,256]{1,0:T(8,128)(2,1)S(1)} %collective-permute-done.40), channel_id=1, source_target_pairs={{0,1},{1,0},{2,3},{3,2},{4,5},{5,4},{6,7},{7,6},{8,9},{9,8},{10,11... | collective-permute-start | bytes 245768 | tf_op jit(solution)/shard_map/ppermute | solution.py:355
  87.4 7.5 %collective-permute-start.7 = (bf16[464,256]{1,0:T(8,128)(2,1)S(1)}, bf16[464,256]{1,0:T(8,128)(2,1)S(1)}, u32[]{:S(2)}, u32[]{:S(2)}) collective-permute-start(bf16[464,256]{1,0:T(8,128)(2,1)S(1)} %broadcast_select_fusion.3.refs_0_.second_ref), channel_id=1, source_target_pairs={{0,6},{1,7},{2,4},{3,5},{4,2},{5,3},{6,0},{7,1},{8,14},{9,15},{10,... | collective-permute-start | bytes 712712 | tf_op jit(solution)/shard_map/ppermute | solution.py:355
  87.8 1.3 %collective-permute-start.43 = (f16[160,256]{1,0:T(8,128)(2,1)S(1)}, f16[160,256]{1,0:T(8,128)(2,1)S(1)}, u32[]{:S(2)}, u32[]{:S(2)}) collective-permute-start(f16[160,256]{1,0:T(8,128)(2,1)S(1)} %collective-permute-done.42), channel_id=1, source_target_pairs={{0,1},{1,0},{2,3},{3,2},{4,5},{5,4},{6,7},{7,6},{8,9},{9,8},{10,11... | collective-permute-start | bytes 245768 | tf_op jit(solution)/shard_map/ppermute | solution.py:355
  87.8 1.4 %collective-permute-start.45 = (f16[160,256]{1,0:T(8,128)(2,1)S(1)}, f16[160,256]{1,0:T(8,128)(2,1)S(1)}, u32[]{:S(2)}, u32[]{:S(2)}) collective-permute-start(f16[160,256]{1,0:T(8,128)(2,1)S(1)} %collective-permute-done.44), channel_id=1, source_target_pairs={{0,1},{1,0},{2,3},{3,2},{4,5},{5,4},{6,7},{7,6},{8,9},{9,8},{10,11... | collective-permute-start | bytes 245768 | tf_op jit(solution)/shard_map/ppermute | solution.py:355
  90.0 5.0 %collective-permute-start.46 = (bf16[80,128]{1,0:T(8,128)(2,1)S(1)}, bf16[80,128]{1,0:T(8,128)(2,1)S(1)}, u32[]{:S(2)}, u32[]{:S(2)}) collective-permute-start(bf16[80,128]{1,0:T(8,128)(2,1)S(1)} %shard_map.81), channel_id=1, source_target_pairs={{0,8},{1,9},{2,10},{3,11},{4,12},{5,13},{6,14},{7,15},{8,0},{9,1},... | collective-permute-start | bytes 61448 | tf_op jit(solution)/shard_map/ppermute | solution.py:355
  91.4 4.9 %collective-permute-start.47 = (bf16[80,128]{1,0:T(8,128)(2,1)S(1)}, bf16[80,128]{1,0:T(8,128)(2,1)S(1)}, u32[]{:S(2)}, u32[]{:S(2)}) collective-permute-start(bf16[80,128]{1,0:T(8,128)(2,1)S(1)} %shard_map.81), channel_id=1, source_target_pairs={{0,16},{1,17},{2,18},{3,19},{4,20},{5,21},{6,22},{7,23},{8,24},{9,... | collective-permute-start | bytes 61448 | tf_op jit(solution)/shard_map/ppermute | solution.py:355
  94.4 12.7 %collective-permute-start.2 = (bf16[464,256]{1,0:T(8,128)(2,1)S(1)}, bf16[464,256]{1,0:T(8,128)(2,1)S(1)}, u32[]{:S(2)}, u32[]{:S(2)}) collective-permute-start(bf16[464,256]{1,0:T(8,128)(2,1)S(1)} %broadcast_select_fusion.3.refs_0_.second_ref), channel_id=1, source_target_pairs={{0,1},{1,0},{2,3},{3,2},{4,5},{5,4},{6,7},{7,6},{8,9},{9,8},{10,11... | collective-permute-start | bytes 712712 | tf_op jit(solution)/shard_map/ppermute | solution.py:355
  94.4 13.3 %collective-permute-start.4 = (bf16[464,256]{1,0:T(8,128)(2,1)S(1)}, bf16[464,256]{1,0:T(8,128)(2,1)S(1)}, u32[]{:S(2)}, u32[]{:S(2)}) collective-permute-start(bf16[464,256]{1,0:T(8,128)(2,1)S(1)} %collective-permute-done.3.refs_2_), channel_id=1, source_target_pairs={{0,1},{1,0},{2,3},{3,2},{4,5},{5,4},{6,7},{7,6},{8,9},{9,8},{10,11... | collective-permute-start | bytes 712712 | tf_op jit(solution)/shard_map/ppermute | solution.py:355
  94.9 14.6 %collective-permute-start.6 = (bf16[464,256]{1,0:T(8,128)(2,1)S(1)}, bf16[464,256]{1,0:T(8,128)(2,1)S(1)}, u32[]{:S(2)}, u32[]{:S(2)}) collective-permute-start(bf16[464,256]{1,0:T(8,128)(2,1)S(1)} %collective-permute-done.5.refs_4_), channel_id=1, source_target_pairs={{0,1},{1,0},{2,3},{3,2},{4,5},{5,4},{6,7},{7,6},{8,9},{9,8},{10,11... | collective-permute-start | bytes 712712 | tf_op jit(solution)/shard_map/ppermute | solution.py:355
  95.0 14.6 %collective-permute-start.8 = (bf16[464,256]{1,0:T(8,128)(2,1)S(1)}, bf16[464,256]{1,0:T(8,128)(2,1)S(1)}, u32[]{:S(2)}, u32[]{:S(2)}) collective-permute-start(bf16[464,256]{1,0:T(8,128)(2,1)S(1)} %collective-permute-done.7.refs_6_), channel_id=1, source_target_pairs={{0,1},{1,0},{2,3},{3,2},{4,5},{5,4},{6,7},{7,6},{8,9},{9,8},{10,11... | collective-permute-start | bytes 712712 | tf_op jit(solution)/shard_map/ppermute | solution.py:355
  96.3 9.6 %collective-permute-start.48 = (bf16[80,128]{1,0:T(8,128)(2,1)S(1)}, bf16[80,128]{1,0:T(8,128)(2,1)S(1)}, u32[]{:S(2)}, u32[]{:S(2)}) collective-permute-start(bf16[80,128]{1,0:T(8,128)(2,1)S(1)} %shard_map.81), channel_id=1, source_target_pairs={{0,24},{1,25},{2,26},{3,27},{4,28},{5,29},{6,30},{7,31},{8,16},{9,... | collective-permute-start | bytes 61448 | tf_op jit(solution)/shard_map/ppermute | solution.py:355
  105.9 11.2 %copy-start.3 = (f32[2048,147]{0,1:T(8,128)S(1)}, f32[2048,147]{0,1:T(8,128)}, u32[]{:S(2)}) copy-start(f32[2048,147]{0,1:T(8,128)} %param.8) | copy-start | bytes 3612676
  105.9 10.1 %collective-permute-start.50 = (bf16[320,128]{1,0:T(8,128)(2,1)S(1)}, bf16[320,128]{1,0:T(8,128)(2,1)S(1)}, u32[]{:S(2)}, u32[]{:S(2)}) collective-permute-start(bf16[320,128]{1,0:T(8,128)(2,1)S(1)} %pad_maximum_fusion.1.refs_0_), channel_id=1, source_target_pairs={{0,2},{1,3},{2,0},{3,1},{4,6},{5,7},{6,4},{7,5},{8,10},{9,11},{10,... | collective-permute-start | bytes 245768 | tf_op jit(solution)/shard_map/ppermute | solution.py:355
  107.1 9.5 %collective-permute-start.52 = (bf16[320,128]{1,0:T(8,128)(2,1)S(1)}, bf16[320,128]{1,0:T(8,128)(2,1)S(1)}, u32[]{:S(2)}, u32[]{:S(2)}) collective-permute-start(bf16[320,128]{1,0:T(8,128)(2,1)S(1)} %pad_maximum_fusion.1.refs_0_), channel_id=1, source_target_pairs={{0,4},{1,5},{2,6},{3,7},{4,0},{5,1},{6,2},{7,3},{8,12},{9,13},{10,... | collective-permute-start | bytes 245768 | tf_op jit(solution)/shard_map/ppermute | solution.py:355
  107.7 9.0 %collective-permute-start.54 = (bf16[320,128]{1,0:T(8,128)(2,1)S(1)}, bf16[320,128]{1,0:T(8,128)(2,1)S(1)}, u32[]{:S(2)}, u32[]{:S(2)}) collective-permute-start(bf16[320,128]{1,0:T(8,128)(2,1)S(1)} %pad_maximum_fusion.1.refs_0_), channel_id=1, source_target_pairs={{0,6},{1,7},{2,4},{3,5},{4,2},{5,3},{6,0},{7,1},{8,14},{9,15},{10,... | collective-permute-start | bytes 245768 | tf_op jit(solution)/shard_map/ppermute | solution.py:355
  116.0 5.4 %collective-permute-start.49 = (bf16[320,128]{1,0:T(8,128)(2,1)S(1)}, bf16[320,128]{1,0:T(8,128)(2,1)S(1)}, u32[]{:S(2)}, u32[]{:S(2)}) collective-permute-start(bf16[320,128]{1,0:T(8,128)(2,1)S(1)} %pad_maximum_fusion.1.refs_0_), channel_id=1, source_target_pairs={{0,1},{1,0},{2,3},{3,2},{4,5},{5,4},{6,7},{7,6},{8,9},{9,8},{10,11... | collective-permute-start | bytes 245768 | tf_op jit(solution)/shard_map/ppermute | solution.py:355
  116.1 5.3 %collective-permute-start.51 = (bf16[320,128]{1,0:T(8,128)(2,1)S(1)}, bf16[320,128]{1,0:T(8,128)(2,1)S(1)}, u32[]{:S(2)}, u32[]{:S(2)}) collective-permute-start(bf16[320,128]{1,0:T(8,128)(2,1)S(1)} %collective-permute-done.50.refs_2_), channel_id=1, source_target_pairs={{0,1},{1,0},{2,3},{3,2},{4,5},{5,4},{6,7},{7,6},{8,9},{9,8},{10,11... | collective-permute-start | bytes 245768 | tf_op jit(solution)/shard_map/ppermute | solution.py:355
  116.6 4.8 %collective-permute-start.53 = (bf16[320,128]{1,0:T(8,128)(2,1)S(1)}, bf16[320,128]{1,0:T(8,128)(2,1)S(1)}, u32[]{:S(2)}, u32[]{:S(2)}) collective-permute-start(bf16[320,128]{1,0:T(8,128)(2,1)S(1)} %collective-permute-done.52.refs_4_), channel_id=1, source_target_pairs={{0,1},{1,0},{2,3},{3,2},{4,5},{5,4},{6,7},{7,6},{8,9},{9,8},{10,11... | collective-permute-start | bytes 245768 | tf_op jit(solution)/shard_map/ppermute | solution.py:355
  116.7 4.7 %collective-permute-start.55 = (bf16[320,128]{1,0:T(8,128)(2,1)S(1)}, bf16[320,128]{1,0:T(8,128)(2,1)S(1)}, u32[]{:S(2)}, u32[]{:S(2)}) collective-permute-start(bf16[320,128]{1,0:T(8,128)(2,1)S(1)} %collective-permute-done.54.refs_6_), channel_id=1, source_target_pairs={{0,1},{1,0},{2,3},{3,2},{4,5},{5,4},{6,7},{7,6},{8,9},{9,8},{10,11... | collective-permute-start | bytes 245768 | tf_op jit(solution)/shard_map/ppermute | solution.py:355
  (1 other events, 0.7 us)

commit v2 on v1

--- a/solution.py
+++ b/solution.py
@@ -1,3 +1,5 @@
+import math
+
 import jax
 import jax.numpy as jnp
 from jax import lax
@@ -245,25 +247,18 @@
     tile = min(512, frames)
 
     def body(local_ref, *refs):
-        pieces_ref, out_ref, turned = refs[:count], refs[-2], refs[-1]
-
-        @pl.when(pl.program_id(0) == 0)
-        def _():
-            for k in range(count):
-                turned[k * picks : (k + 1) * picks, :] = jnp.transpose(pieces_ref[k][0:depth, :])
-
+        pieces_ref, out_ref = refs[:count], refs[-1]
         for k in range(count):
-            here = slice(k * picks, (k + 1) * picks)
-            inner = matmul(turned[here, :], local_ref[...])
-            out_ref[here, :] = jnp.exp2(inner * scale).astype(bf16)
-
-    return pl.pallas_call(
-        body,
-        grid=(frames // tile,),
-        in_specs=[pl.BlockSpec((depth, tile), lambda i: (0, i))] + [vmem] * count,
-        out_specs=pl.BlockSpec((block, tile), lambda i: (0, i)),
+            turned = jnp.transpose(pieces_ref[k][...])
+            for start in range(0, frames, tile):
+                inner = matmul(turned, local_ref[:, start : start + tile])
+                out_ref[k * picks : (k + 1) * picks, start : start + tile] = jnp.exp2(inner * scale).astype(bf16)
+
+    return pl.pallas_call(
+        body,
+        in_specs=[vmem] * (1 + count),
+        out_specs=vmem,
         out_shape=jax.ShapeDtypeStruct((block, frames), bf16),
-        scratch_shapes=[pltpu.VMEM((block, depth), bf16)],
         cost_estimate=pl.CostEstimate(
             flops=2 * block * frames * depth, transcendentals=block * frames, bytes_accessed=10**7
         ),
@@ -301,11 +296,11 @@
     picks = index.shape[1]
     count = len(pieces)
     rows = up(outputs, 16)
-    tile = min(512, frames)
+    tile = min(1024, frames)
 
     def body(owners_ref, index_ref, kernel_ref, residual_ref, coeffs_ref, *refs):
         pieces_ref = refs[:count]
-        new_residual_ref, new_coeffs_ref, canon, own = refs[count:]
+        new_residual_ref, new_coeffs_ref, canon, own, places = refs[count:]
         here = pl.program_id(0)
 
         @pl.when(here == 0)
@@ -313,11 +308,12 @@
             unfold(pieces_ref, pieces[0].shape[0] * 2 // rows, picks, canon)
             mine = canon[:, 0:picks]
             own[...] = jnp.where(lax.axis_index("rows") == owners_ref[step], mine, jnp.zeros_like(mine))
-
-        change = matmul(canon[...], kernel_ref[...])
-        frame = lax.broadcasted_iota(jnp.int32, (tile, picks), 0) + here * tile
-        hot = jnp.where(frame == index_ref[step : step + 1, :], 1.0, 0.0).astype(bf16)
-        put = matmul_nt(own[...], hot)
+            places[...] = turn(index_ref[step : step + 1, :])
+
+        change = matmul(canon[...], kernel_ref[:, lane_start(here, tile)])
+        frame = lax.broadcasted_iota(jnp.int32, (picks, tile), 1) + here * tile
+        hot = jnp.where(frame == places[...], 1.0, 0.0).astype(bf16)
+        put = matmul(own[...], hot)
         new_residual_ref[...] = residual_ref[...] - (change + penalty * put)[:outputs]
         new_coeffs_ref[...] = coeffs_ref[...] + put[:outputs]
 
@@ -325,13 +321,17 @@
     return pl.pallas_call(
         body,
         grid=(frames // tile,),
-        in_specs=[smem, vmem, pl.BlockSpec((block, tile), lambda i: (0, i)), strip, strip] + [vmem] * count,
+        in_specs=[smem, vmem, vmem, strip, strip] + [vmem] * count,
         out_specs=(strip, strip),
         out_shape=(
             jax.ShapeDtypeStruct((outputs, frames), f32),
             jax.ShapeDtypeStruct((outputs, frames), f32),
         ),
-        scratch_shapes=[pltpu.VMEM((rows, block), bf16), pltpu.VMEM((rows, picks), bf16)],
+        scratch_shapes=[
+            pltpu.VMEM((rows, block), bf16),
+            pltpu.VMEM((rows, picks), bf16),
+            pltpu.VMEM((picks, 1), jnp.int32),
+        ],
         cost_estimate=pl.CostEstimate(
             flops=2 * rows * block * frames, transcendentals=0, bytes_accessed=2 * block * frames
         ),
@@ -361,7 +361,7 @@
         return value
 
     def over_rows(self, value):
-        steps = sorted(range(1, self.rows), key=lambda k: -k)
+        steps = range(1, self.rows)
         got = {k: self.send(value, row=lambda at, k=k: at ^ k) for k in steps}
         return [value] + [got[k] for k in range(1, self.rows)]
 
@@ -385,7 +385,9 @@
     sender = Sender(rows, cols)
     picks = block_index.shape[1]
     moves, rules = doubling(rows)
-    scaled = 2.0**-4 * (2048 / block_inverse.shape[2]) ** 2
+    block = block_inverse.shape[2]
+    bound = 6.0 + (block + penalty) * block * 6.0 * 0.0234375
+    scaled = 2.0 ** -max(0, math.ceil(math.log2(bound / 60000.0)))
     features_t, residual_t, coeffs_t = features.T, residual.T, coeffs.T
     first, second = pick_residual(block_index, residual_t)
     first_block, second_block, *takes = pick_features(
@@ -495,7 +497,7 @@
             and block_index.shape[0] == 2
             and block_index.shape[1] % LANES == 0
             and 2 * block_inverse.shape[1] == LANES
-            and features.shape[0] % 512 == 0
+            and features.shape[0] % 1024 == 0
         )
 
     small = power_of_two(rows) and power_of_two(cols) and 2 <= rows <= 8 and 4 <= cols <= 16

time: 126 us -> 121 us (0.960)
  Pallas kernels: 28.3 us -> 23.3 us
    pallas_call x4, Pallas kernels: 22 us -> 17 us  [the longest x2 9.49 us: block_kernel(): pl.pallas_call(body, in_specs=[vmem] * (1 + count), out_specs=vmem, out_s...]
  transfers between devices with their start and end apart: 56 -> 56, of which waited for: 17 -> 17; matrix products, arithmetic and copies ran while one was open for 1% -> 1% of each run, Pallas kernels for 17% -> 14%
where the time goes in v2:
time: 121 us
  starting transfers between devices  53.7 us (44%)
  waiting for transfers between devices  38.2 us (32%)
  Pallas kernels  23.3 us (19%)
  local copies, waits for them, and re-layouts  4.31 us (4%)
    ppermute x56, starting transfers between devices, send(): return lax.ppermute(value, ('rows', 'cols'), pairs)  53.7 us
    ppermute x56, waiting for transfers between devices, send(): return lax.ppermute(value, ('rows', 'cols'), pairs)  38.2 us
    pallas_call x2, Pallas kernels, block_kernel(): pl.pallas_call(body, in_specs=[vmem] * (1 + count), out_specs=vmem, out_s...  9.49 us
    pallas_call x2, Pallas kernels, apply_update(): pl.pallas_call(body, grid=(frames // tile,), in_specs=[smem, vmem, vmem,...  7.5 us
    unnamed x30, local copies, waits for them, and re-layouts  4.28 us
  transfers between devices with their start and end apart: 56, of which 17 were waited for; matrix products, arithmetic and copies ran while one was open for 1% of the time, Pallas kernels for 14%

profile of v2, /device:TPU:0, one launch (start us, length us, event | category | flops | bytes accessed | tf_op | source)
XLA Modules:
  0.0 121.2 jit_solution(1266370823370636375)
XLA Ops:
  0.6 1.5 %copy-done = bf16[2048,440]{0,1:T(8,128)(2,1)S(1)} copy-done((bf16[2048,440]{0,1:T(8,128)(2,1)S(1)}, bf16[2048,440]{0,1:T(8,128)(2,1)}, u32[]{:S(2)}) %copy-start) | copy-done | bytes 1802264
  2.1 0.7 copy-done.5
  2.8 0.7 copy-done.7
  3.5 1.7 %pick_features.1 = (bf16[464,256]{1,0:T(8,128)(2,1)S(1)}, bf16[464,256]{1,0:T(8,128)(2,1)S(1)}, f32[1,256]{1,0:T(1,128)S(1)}, f32[1,256]{1,0:T(1,128)S(1)}, f32[1,256]{1,0:T(1,128)S(1)}, /*index=5*/f32[1,256]{1,0:T(1,128)S(1)}) custom-call(s32[2]{0:T(128)S(1)} %copy-done.7, s32[2,256]{1,0:T(2,128)S(1)} %copy-done.5, bf16[440,2048]{1,0:T(8,128)(2,1)S(1)} %bitcast.5), custom_call_target="tpu_custom_call" | custom-call | tf_op jit(solution)/shard_map/pick_features/pallas_call | solution.py:122
  5.2 3.1 %collective-permute-start.9 = (bf16[464,256]{1,0:T(8,128)(2,1)S(1)}, bf16[464,256]{1,0:T(8,128)(2,1)S(1)}, u32[]{:S(2)}, u32[]{:S(2)}) collective-permute-start(bf16[464,256]{1,0:T(8,128)(2,1)S(1)} %get-tuple-element.23), channel_id=1, source_target_pairs={{0,8},{1,9},{2,10},{3,11},{4,12},{5,13},{6,14},{7,15},{8,0},{9,1},... | collective-permute-start | bytes 712712 | tf_op jit(solution)/shard_map/ppermute | solution.py:355
  8.4 0.9 pick_residual.1
  9.3 2.0 %collective-permute-start.18 = (f16[160,256]{1,0:T(8,128)(2,1)S(1)}, f16[160,256]{1,0:T(8,128)(2,1)S(1)}, u32[]{:S(2)}, u32[]{:S(2)}) collective-permute-start(f16[160,256]{1,0:T(8,128)(2,1)S(1)} %convert_element_type.18), channel_id=1, source_target_pairs={{0,8},{1,9},{2,10},{3,11},{4,12},{5,13},{6,14},{7,15},{8,0},{9,1},... | collective-permute-start | bytes 245768 | tf_op jit(solution)/shard_map/ppermute | solution.py:355
  11.5 10.3 %collective-permute-done.18 = f16[160,256]{1,0:T(8,128)(2,1)S(1)} collective-permute-done((f16[160,256]{1,0:T(8,128)(2,1)S(1)}, f16[160,256]{1,0:T(8,128)(2,1)S(1)}, u32[]{:S(2)}, u32[]{:S(2)}) %collective-permute-start.18) | collective-permute-done | bytes 81952 | tf_op jit(solution)/shard_map/ppermute | solution.py:355
  21.8 2.8 %collective-permute-start.19 = (f16[160,256]{1,0:T(8,128)(2,1)S(1)}, f16[160,256]{1,0:T(8,128)(2,1)S(1)}, u32[]{:S(2)}, u32[]{:S(2)}) collective-permute-start(f16[160,256]{1,0:T(8,128)(2,1)S(1)} %broadcast_select_fusion.5), channel_id=1, source_target_pairs={{0,16},{1,17},{2,18},{3,19},{4,20},{5,21},{6,22},{7,23},{8,24},{9,... | collective-permute-start | bytes 245768 | tf_op jit(solution)/shard_map/ppermute | solution.py:355
  24.7 1.2 %copy-done.4 = f32[2,64,2048]{2,1,0:T(8,128)S(1)} copy-done((f32[2,64,2048]{2,1,0:T(8,128)S(1)}, f32[2,64,2048]{2,1,0:T(8,128)}, u32[]{:S(2)}) %copy-start.4) | copy-done | bytes 1048600
  26.3 0.9 collective-permute-done.19
  27.3 1.7 %collective-permute-start.21 = (f16[160,256]{1,0:T(8,128)(2,1)S(1)}, f16[160,256]{1,0:T(8,128)(2,1)S(1)}, u32[]{:S(2)}, u32[]{:S(2)}) collective-permute-start(f16[160,256]{1,0:T(8,128)(2,1)S(1)} %get-tuple-element.35), channel_id=1, source_target_pairs={{0,2},{1,3},{2,0},{3,1},{4,6},{5,7},{6,4},{7,5},{8,10},{9,11},{10,... | collective-permute-start | bytes 245768 | tf_op jit(solution)/shard_map/ppermute | solution.py:355
  29.1 1.5 %collective-permute-start.23 = (f16[160,256]{1,0:T(8,128)(2,1)S(1)}, f16[160,256]{1,0:T(8,128)(2,1)S(1)}, u32[]{:S(2)}, u32[]{:S(2)}) collective-permute-start(f16[160,256]{1,0:T(8,128)(2,1)S(1)} %get-tuple-element.35), channel_id=1, source_target_pairs={{0,4},{1,5},{2,6},{3,7},{4,0},{5,1},{6,2},{7,3},{8,12},{9,13},{10,... | collective-permute-start | bytes 245768 | tf_op jit(solution)/shard_map/ppermute | solution.py:355
  30.6 0.6 collective-permute-start.25
  31.2 0.9 collective-permute-done.21
  32.2 2.2 %collective-permute-done.23 = f16[160,256]{1,0:T(8,128)(2,1)S(1)} collective-permute-done((f16[160,256]{1,0:T(8,128)(2,1)S(1)}, f16[160,256]{1,0:T(8,128)(2,1)S(1)}, u32[]{:S(2)}, u32[]{:S(2)}) %collective-permute-start.23) | collective-permute-done | bytes 81952 | tf_op jit(solution)/shard_map/ppermute | solution.py:355
  34.4 2.7 %collective-permute-start.10 = (bf16[464,256]{1,0:T(8,128)(2,1)S(1)}, bf16[464,256]{1,0:T(8,128)(2,1)S(1)}, u32[]{:S(2)}, u32[]{:S(2)}) collective-permute-start(bf16[464,256]{1,0:T(8,128)(2,1)S(1)} %broadcast_select_fusion), channel_id=1, source_target_pairs={{0,16},{1,17},{2,18},{3,19},{4,20},{5,21},{6,22},{7,23},{8,24},{9,... | collective-permute-start | bytes 712712 | tf_op jit(solution)/shard_map/ppermute | solution.py:355
  37.1 0.5 collective-permute-start.26
  37.6 0.7 collective-permute-done.24
  38.6 0.7 shard_map.79
  39.3 2.3 %collective-permute-start.27 = (bf16[80,128]{1,0:T(8,128)(2,1)S(1)}, bf16[80,128]{1,0:T(8,128)(2,1)S(1)}, u32[]{:S(2)}, u32[]{:S(2)}) collective-permute-start(bf16[80,128]{1,0:T(8,128)(2,1)S(1)} %shard_map.79), channel_id=1, source_target_pairs={{0,8},{1,9},{2,10},{3,11},{4,12},{5,13},{6,14},{7,15},{8,0},{9,1},... | collective-permute-start | bytes 61448 | tf_op jit(solution)/shard_map/ppermute | solution.py:355
  41.6 1.6 %collective-permute-start.28 = (bf16[80,128]{1,0:T(8,128)(2,1)S(1)}, bf16[80,128]{1,0:T(8,128)(2,1)S(1)}, u32[]{:S(2)}, u32[]{:S(2)}) collective-permute-start(bf16[80,128]{1,0:T(8,128)(2,1)S(1)} %shard_map.79), channel_id=1, source_target_pairs={{0,16},{1,17},{2,18},{3,19},{4,20},{5,21},{6,22},{7,23},{8,24},{9,... | collective-permute-start | bytes 61448 | tf_op jit(solution)/shard_map/ppermute | solution.py:355
  43.3 0.8 collective-permute-start.29
  44.1 2.2 %collective-permute-start.38 = (f16[160,256]{1,0:T(8,128)(2,1)S(1)}, f16[160,256]{1,0:T(8,128)(2,1)S(1)}, u32[]{:S(2)}, u32[]{:S(2)}) collective-permute-start(f16[160,256]{1,0:T(8,128)(2,1)S(1)} %broadcast_select_fusion.4), channel_id=1, source_target_pairs={{0,16},{1,17},{2,18},{3,19},{4,20},{5,21},{6,22},{7,23},{8,24},{9,... | collective-permute-start | bytes 245768 | tf_op jit(solution)/shard_map/ppermute | solution.py:355
  46.3 2.0 %collective-permute-done.28 = bf16[80,128]{1,0:T(8,128)(2,1)S(1)} collective-permute-done((bf16[80,128]{1,0:T(8,128)(2,1)S(1)}, bf16[80,128]{1,0:T(8,128)(2,1)S(1)}, u32[]{:S(2)}, u32[]{:S(2)}) %collective-permute-start.28) | collective-permute-done | bytes 20512 | tf_op jit(solution)/shard_map/ppermute | solution.py:355
  48.3 0.6 collective-permute-done.29
  48.9 2.8 %collective-permute-start.31 = (bf16[320,128]{1,0:T(8,128)(2,1)S(1)}, bf16[320,128]{1,0:T(8,128)(2,1)S(1)}, u32[]{:S(2)}, u32[]{:S(2)}) collective-permute-start(bf16[320,128]{1,0:T(8,128)(2,1)S(1)} %pad_maximum_fusion.refs_0_), channel_id=1, source_target_pairs={{0,2},{1,3},{2,0},{3,1},{4,6},{5,7},{6,4},{7,5},{8,10},{9,11},{10,... | collective-permute-start | bytes 245768 | tf_op jit(solution)/shard_map/ppermute | solution.py:355
  51.8 2.4 %collective-permute-start.33 = (bf16[320,128]{1,0:T(8,128)(2,1)S(1)}, bf16[320,128]{1,0:T(8,128)(2,1)S(1)}, u32[]{:S(2)}, u32[]{:S(2)}) collective-permute-start(bf16[320,128]{1,0:T(8,128)(2,1)S(1)} %pad_maximum_fusion.refs_0_), channel_id=1, source_target_pairs={{0,4},{1,5},{2,6},{3,7},{4,0},{5,1},{6,2},{7,3},{8,12},{9,13},{10,... | collective-permute-start | bytes 245768 | tf_op jit(solution)/shard_map/ppermute | solution.py:355
  54.2 1.5 %collective-permute-start.12 = (bf16[464,256]{1,0:T(8,128)(2,1)S(1)}, bf16[464,256]{1,0:T(8,128)(2,1)S(1)}, u32[]{:S(2)}, u32[]{:S(2)}) collective-permute-start(bf16[464,256]{1,0:T(8,128)(2,1)S(1)} %broadcast_select_fusion.1.refs_0_), channel_id=1, source_target_pairs={{0,2},{1,3},{2,0},{3,1},{4,6},{5,7},{6,4},{7,5},{8,10},{9,11},{10,... | collective-permute-start | bytes 712712 | tf_op jit(solution)/shard_map/ppermute | solution.py:355
  55.7 2.0 %collective-permute-start.14 = (bf16[464,256]{1,0:T(8,128)(2,1)S(1)}, bf16[464,256]{1,0:T(8,128)(2,1)S(1)}, u32[]{:S(2)}, u32[]{:S(2)}) collective-permute-start(bf16[464,256]{1,0:T(8,128)(2,1)S(1)} %broadcast_select_fusion.1.refs_0_), channel_id=1, source_target_pairs={{0,4},{1,5},{2,6},{3,7},{4,0},{5,1},{6,2},{7,3},{8,12},{9,13},{10,... | collective-permute-start | bytes 712712 | tf_op jit(solution)/shard_map/ppermute | solution.py:355
  57.8 2.1 %collective-permute-start.1 = (bf16[464,256]{1,0:T(8,128)(2,1)S(1)}, bf16[464,256]{1,0:T(8,128)(2,1)S(1)}, u32[]{:S(2)}, u32[]{:S(2)}) collective-permute-start(bf16[464,256]{1,0:T(8,128)(2,1)S(1)} %broadcast_select_fusion.2), channel_id=1, source_target_pairs={{0,16},{1,17},{2,18},{3,19},{4,20},{5,21},{6,22},{7,23},{8,24},{9,... | collective-permute-start | bytes 712712 | tf_op jit(solution)/shard_map/ppermute | solution.py:355
  59.9 0.8 collective-permute-start.16
  60.7 0.8 collective-permute-done.12.refs_2_
  61.5 5.9 %collective-permute-done.14.refs_4_ = bf16[464,256]{1,0:T(8,128)(2,1)S(1)} collective-permute-done((bf16[464,256]{1,0:T(8,128)(2,1)S(1)}, bf16[464,256]{1,0:T(8,128)(2,1)S(1)}, u32[]{:S(2)}, u32[]{:S(2)}) %collective-permute-start.14) | collective-permute-done | bytes 237600 | tf_op jit(solution)/shard_map/ppermute | solution.py:355
  67.4 2.0 %collective-permute-done.1 = bf16[464,256]{1,0:T(8,128)(2,1)S(1)} collective-permute-done((bf16[464,256]{1,0:T(8,128)(2,1)S(1)}, bf16[464,256]{1,0:T(8,128)(2,1)S(1)}, u32[]{:S(2)}, u32[]{:S(2)}) %collective-permute-start.1) | collective-permute-done | bytes 237600 | tf_op jit(solution)/shard_map/ppermute | solution.py:355
  69.4 0.5 collective-permute-start.32
  70.0 0.4 collective-permute-start.36
  70.6 1.4 %collective-permute-done.17.refs_7_ = bf16[464,256]{1,0:T(8,128)(2,1)S(1)} collective-permute-done((bf16[464,256]{1,0:T(8,128)(2,1)S(1)}, bf16[464,256]{1,0:T(8,128)(2,1)S(1)}, u32[]{:S(2)}, u32[]{:S(2)}) %collective-permute-start.17) | collective-permute-done | bytes 237600 | tf_op jit(solution)/shard_map/ppermute | solution.py:355
  72.0 1.4 %meeting_kernel.1.kernel_ref = bf16[2048,256]{1,0:T(8,128)(2,1)S(1)} custom-call(s32[2]{0:T(128)S(1)} %copy-done.8, s32[2,256]{1,0:T(2,128)S(1)} %copy-done.6, bf16[464,256]{1,0:T(8,128)(2,1)S(1)} %broadcast_select_fusion.3.refs_0_.second_ref, bf16[464,256]{1,0:T(8,128)(2,1)S(1)} %broadcast_select_fusion.1.refs_0_, ...), custom_call_target="tpu_custom_call" | custom-call | flops 486539264 | bytes 1000000 | tf_op jit(solution)/shard_map/meeting_kernel/pallas_call | solution.py:208
  73.4 0.7 advance.1
  74.7 1.7 %collective-permute-start.3 = (bf16[464,256]{1,0:T(8,128)(2,1)S(1)}, bf16[464,256]{1,0:T(8,128)(2,1)S(1)}, u32[]{:S(2)}, u32[]{:S(2)}) collective-permute-start(bf16[464,256]{1,0:T(8,128)(2,1)S(1)} %broadcast_select_fusion.3.refs_0_.second_ref), channel_id=1, source_target_pairs={{0,2},{1,3},{2,0},{3,1},{4,6},{5,7},{6,4},{7,5},{8,10},{9,11},{10,... | collective-permute-start | bytes 712712 | tf_op jit(solution)/shard_map/ppermute | solution.py:355
  76.7 1.6 %collective-permute-start.42 = (f16[160,256]{1,0:T(8,128)(2,1)S(1)}, f16[160,256]{1,0:T(8,128)(2,1)S(1)}, u32[]{:S(2)}, u32[]{:S(2)}) collective-permute-start(f16[160,256]{1,0:T(8,128)(2,1)S(1)} %get-tuple-element.33), channel_id=1, source_target_pairs={{0,4},{1,5},{2,6},{3,7},{4,0},{5,1},{6,2},{7,3},{8,12},{9,13},{10,... | collective-permute-start | bytes 245768 | tf_op jit(solution)/shard_map/ppermute | solution.py:355
  78.4 0.4 collective-permute-start.44
  78.8 0.9 collective-permute-done.40
  79.7 7.7 %collective-permute-done.42 = f16[160,256]{1,0:T(8,128)(2,1)S(1)} collective-permute-done((f16[160,256]{1,0:T(8,128)(2,1)S(1)}, f16[160,256]{1,0:T(8,128)(2,1)S(1)}, u32[]{:S(2)}, u32[]{:S(2)}) %collective-permute-start.42) | collective-permute-done | bytes 81952 | tf_op jit(solution)/shard_map/ppermute | solution.py:355
  87.4 0.4 collective-permute-start.7
  87.8 0.5 collective-permute-start.45
  88.3 0.7 collective-permute-done.43
  89.3 0.6 shard_map.81
  90.0 1.4 %collective-permute-start.46 = (bf16[80,128]{1,0:T(8,128)(2,1)S(1)}, bf16[80,128]{1,0:T(8,128)(2,1)S(1)}, u32[]{:S(2)}, u32[]{:S(2)}) collective-permute-start(bf16[80,128]{1,0:T(8,128)(2,1)S(1)} %shard_map.81), channel_id=1, source_target_pairs={{0,8},{1,9},{2,10},{3,11},{4,12},{5,13},{6,14},{7,15},{8,0},{9,1},... | collective-permute-start | bytes 61448 | tf_op jit(solution)/shard_map/ppermute | solution.py:355
  91.4 3.0 %collective-permute-start.47 = (bf16[80,128]{1,0:T(8,128)(2,1)S(1)}, bf16[80,128]{1,0:T(8,128)(2,1)S(1)}, u32[]{:S(2)}, u32[]{:S(2)}) collective-permute-start(bf16[80,128]{1,0:T(8,128)(2,1)S(1)} %shard_map.81), channel_id=1, source_target_pairs={{0,16},{1,17},{2,18},{3,19},{4,20},{5,21},{6,22},{7,23},{8,24},{9,... | collective-permute-start | bytes 61448 | tf_op jit(solution)/shard_map/ppermute | solution.py:355
  94.4 0.5 collective-permute-start.4
  95.0 0.5 collective-permute-start.8
  95.4 0.9 collective-permute-done.47
  96.3 3.1 %collective-permute-start.48 = (bf16[80,128]{1,0:T(8,128)(2,1)S(1)}, bf16[80,128]{1,0:T(8,128)(2,1)S(1)}, u32[]{:S(2)}, u32[]{:S(2)}) collective-permute-start(bf16[80,128]{1,0:T(8,128)(2,1)S(1)} %shard_map.81), channel_id=1, source_target_pairs={{0,24},{1,25},{2,26},{3,27},{4,28},{5,29},{6,30},{7,31},{8,16},{9,... | collective-permute-start | bytes 61448 | tf_op jit(solution)/shard_map/ppermute | solution.py:355
  99.4 4.8 %shard_map.78.kernel_ref = bf16[2048,2048]{1,0:T(8,128)(2,1)S(1)} custom-call(bf16[464,2048]{1,0:T(8,128)(2,1)S(1)} %get-tuple-element.17.local_ref, bf16[464,256]{1,0:T(8,128)(2,1)S(1)} %broadcast_select_fusion.1.refs_0_, bf16[464,256]{1,0:T(8,128)(2,1)S(1)} %collective-permute-done.11.refs_1_, bf16[464,256]{1,0:T(8,128)(2,1)S(1)} %collective-permute-done.12.refs_2_, ...), custom_call_target="tpu_custom_call" | custom-call | flops 3892314112 | bytes 10000000 | tf_op jit(solution)/shard_map/pallas_call | solution.py:257
  104.3 1.2 collective-permute-start.50
  105.5 0.6 collective-permute-start.52
  106.0 1.8 %collective-permute-start.54 = (bf16[320,128]{1,0:T(8,128)(2,1)S(1)}, bf16[320,128]{1,0:T(8,128)(2,1)S(1)}, u32[]{:S(2)}, u32[]{:S(2)}) collective-permute-start(bf16[320,128]{1,0:T(8,128)(2,1)S(1)} %pad_maximum_fusion.1.refs_0_), channel_id=1, source_target_pairs={{0,6},{1,7},{2,4},{3,5},{4,2},{5,3},{6,0},{7,1},{8,14},{9,15},{10,... | collective-permute-start | bytes 245768 | tf_op jit(solution)/shard_map/ppermute | solution.py:355
  107.9 4.7 %shard_map.77.kernel_ref = bf16[2048,2048]{1,0:T(8,128)(2,1)S(1)} custom-call(bf16[464,2048]{1,0:T(8,128)(2,1)S(1)} %get-tuple-element.17.local_ref, bf16[464,256]{1,0:T(8,128)(2,1)S(1)} %broadcast_select_fusion.3.refs_0_.second_ref, bf16[464,256]{1,0:T(8,128)(2,1)S(1)} %collective-permute-done.2.refs_1_, ...), custom_call_target="tpu_custom_call" | custom-call | flops 3892314112 | bytes 10000000 | tf_op jit(solution)/shard_map/pallas_call | solution.py:257
  112.6 0.5 collective-permute-start.51
  113.2 0.4 collective-permute-start.55
  113.6 3.4 %shard_map.80 = (f32[147,2048]{1,0:T(8,128)S(1)}, f32[147,2048]{1,0:T(8,128)S(1)}) custom-call(s32[2]{0:T(128)S(1)} %copy-done.8, s32[2,256]{1,0:T(2,128)S(1)} %copy-done.6, bf16[2048,2048]{1,0:T(8,128)(2,1)S(1)} %shard_map.78.kernel_ref, f32[147,2048]{1,0:T(8,128)S(1)} %bitcast.8, f32[147,2048]{1,0:T(8,128)S(1)} %bitcast.9, ...), custom_call_target="tpu_custom_call" | custom-call | flops 1342177280 | bytes 8388608 | tf_op jit(solution)/shard_map/pallas_call | solution.py:321
  117.1 4.1 %shard_map.82 = (f32[147,2048]{1,0:T(8,128)}, f32[147,2048]{1,0:T(8,128)}) custom-call(s32[2]{0:T(128)S(1)} %copy-done.8, s32[2,256]{1,0:T(2,128)S(1)} %copy-done.6, bf16[2048,2048]{1,0:T(8,128)(2,1)S(1)} %shard_map.77.kernel_ref, f32[147,2048]{1,0:T(8,128)S(1)} %get-tuple-element.26.residual_ref, f32[147,2048]{1,0:T(8,128)S(1)} %get-tuple-element.27.coeffs_ref, ...), custom_call_target="tpu_custom_call" | custom-call | flops 1342177280 | bytes 8388608 | tf_op jit(solution)/shard_map/pallas_call | solution.py:321
  (110 shorter events, 3.2 us)
Async XLA Ops:
  0.6 1.5 %copy-start = (bf16[2048,440]{0,1:T(8,128)(2,1)S(1)}, bf16[2048,440]{0,1:T(8,128)(2,1)}, u32[]{:S(2)}) copy-start(bf16[2048,440]{0,1:T(8,128)(2,1)} %param.6) | copy-start | bytes 5406724
  2.1 0.7 copy-start.5
  3.5 4.9 %copy-start.2 = (f32[2048,147]{0,1:T(8,128)S(1)}, f32[2048,147]{0,1:T(8,128)}, u32[]{:S(2)}) copy-start(f32[2048,147]{0,1:T(8,128)} %param.7) | copy-start | bytes 3612676
  5.2 19.5 %copy-start.1 = (bf16[2048,440]{0,1:T(8,128)(2,1)S(1)}, bf16[2048,440]{0,1:T(8,128)(2,1)}, u32[]{:S(2)}) copy-start(bf16[2048,440]{0,1:T(8,128)(2,1)} %param.6) | copy-start | bytes 5406724
  5.2 23.9 %collective-permute-start.9 = (bf16[464,256]{1,0:T(8,128)(2,1)S(1)}, bf16[464,256]{1,0:T(8,128)(2,1)S(1)}, u32[]{:S(2)}, u32[]{:S(2)}) collective-permute-start(bf16[464,256]{1,0:T(8,128)(2,1)S(1)} %get-tuple-element.23), channel_id=1, source_target_pairs={{0,8},{1,9},{2,10},{3,11},{4,12},{5,13},{6,14},{7,15},{8,0},{9,1},... | collective-permute-start | bytes 712712 | tf_op jit(solution)/shard_map/ppermute | solution.py:355
  8.3 47.5 %collective-permute-start = (bf16[464,256]{1,0:T(8,128)(2,1)S(1)}, bf16[464,256]{1,0:T(8,128)(2,1)S(1)}, u32[]{:S(2)}, u32[]{:S(2)}) collective-permute-start(bf16[464,256]{1,0:T(8,128)(2,1)S(1)} %get-tuple-element.20), channel_id=1, source_target_pairs={{0,8},{1,9},{2,10},{3,11},{4,12},{5,13},{6,14},{7,15},{8,0},{9,1},... | collective-permute-start | bytes 712712 | tf_op jit(solution)/shard_map/ppermute | solution.py:355
  9.3 12.5 %collective-permute-start.18 = (f16[160,256]{1,0:T(8,128)(2,1)S(1)}, f16[160,256]{1,0:T(8,128)(2,1)S(1)}, u32[]{:S(2)}, u32[]{:S(2)}) collective-permute-start(f16[160,256]{1,0:T(8,128)(2,1)S(1)} %convert_element_type.18), channel_id=1, source_target_pairs={{0,8},{1,9},{2,10},{3,11},{4,12},{5,13},{6,14},{7,15},{8,0},{9,1},... | collective-permute-start | bytes 245768 | tf_op jit(solution)/shard_map/ppermute | solution.py:355
  11.3 32.0 %collective-permute-start.37 = (f16[160,256]{1,0:T(8,128)(2,1)S(1)}, f16[160,256]{1,0:T(8,128)(2,1)S(1)}, u32[]{:S(2)}, u32[]{:S(2)}) collective-permute-start(f16[160,256]{1,0:T(8,128)(2,1)S(1)} %convert_element_type.20), channel_id=1, source_target_pairs={{0,8},{1,9},{2,10},{3,11},{4,12},{5,13},{6,14},{7,15},{8,0},{9,1},... | collective-permute-start | bytes 245768 | tf_op jit(solution)/shard_map/ppermute | solution.py:355
  21.8 5.4 %collective-permute-start.19 = (f16[160,256]{1,0:T(8,128)(2,1)S(1)}, f16[160,256]{1,0:T(8,128)(2,1)S(1)}, u32[]{:S(2)}, u32[]{:S(2)}) collective-permute-start(f16[160,256]{1,0:T(8,128)(2,1)S(1)} %broadcast_select_fusion.5), channel_id=1, source_target_pairs={{0,16},{1,17},{2,18},{3,19},{4,20},{5,21},{6,22},{7,23},{8,24},{9,... | collective-permute-start | bytes 245768 | tf_op jit(solution)/shard_map/ppermute | solution.py:355
  24.7 1.2 %copy-start.4 = (f32[2,64,2048]{2,1,0:T(8,128)S(1)}, f32[2,64,2048]{2,1,0:T(8,128)}, u32[]{:S(2)}) copy-start(f32[2,64,2048]{2,1,0:T(8,128)} %inverse_ref.1) | copy-start | bytes 3145732
  27.2 3.4 %collective-permute-start.20 = (f16[160,256]{1,0:T(8,128)(2,1)S(1)}, f16[160,256]{1,0:T(8,128)(2,1)S(1)}, u32[]{:S(2)}, u32[]{:S(2)}) collective-permute-start(f16[160,256]{1,0:T(8,128)(2,1)S(1)} %get-tuple-element.35), channel_id=1, source_target_pairs={{0,1},{1,0},{2,3},{3,2},{4,5},{5,4},{6,7},{7,6},{8,9},{9,8},{10,11... | collective-permute-start | bytes 245768 | tf_op jit(solution)/shard_map/ppermute | solution.py:355
  27.3 4.8 %collective-permute-start.21 = (f16[160,256]{1,0:T(8,128)(2,1)S(1)}, f16[160,256]{1,0:T(8,128)(2,1)S(1)}, u32[]{:S(2)}, u32[]{:S(2)}) collective-permute-start(f16[160,256]{1,0:T(8,128)(2,1)S(1)} %get-tuple-element.35), channel_id=1, source_target_pairs={{0,2},{1,3},{2,0},{3,1},{4,6},{5,7},{6,4},{7,5},{8,10},{9,11},{10,... | collective-permute-start | bytes 245768 | tf_op jit(solution)/shard_map/ppermute | solution.py:355
  29.1 5.3 %collective-permute-start.23 = (f16[160,256]{1,0:T(8,128)(2,1)S(1)}, f16[160,256]{1,0:T(8,128)(2,1)S(1)}, u32[]{:S(2)}, u32[]{:S(2)}) collective-permute-start(f16[160,256]{1,0:T(8,128)(2,1)S(1)} %get-tuple-element.35), channel_id=1, source_target_pairs={{0,4},{1,5},{2,6},{3,7},{4,0},{5,1},{6,2},{7,3},{8,12},{9,13},{10,... | collective-permute-start | bytes 245768 | tf_op jit(solution)/shard_map/ppermute | solution.py:355
  30.6 6.4 %collective-permute-start.25 = (f16[160,256]{1,0:T(8,128)(2,1)S(1)}, f16[160,256]{1,0:T(8,128)(2,1)S(1)}, u32[]{:S(2)}, u32[]{:S(2)}) collective-permute-start(f16[160,256]{1,0:T(8,128)(2,1)S(1)} %get-tuple-element.35), channel_id=1, source_target_pairs={{0,6},{1,7},{2,4},{3,5},{4,2},{5,3},{6,0},{7,1},{8,14},{9,15},{10,... | collective-permute-start | bytes 245768 | tf_op jit(solution)/shard_map/ppermute | solution.py:355
  32.2 4.9 %collective-permute-start.22 = (f16[160,256]{1,0:T(8,128)(2,1)S(1)}, f16[160,256]{1,0:T(8,128)(2,1)S(1)}, u32[]{:S(2)}, u32[]{:S(2)}) collective-permute-start(f16[160,256]{1,0:T(8,128)(2,1)S(1)} %collective-permute-done.21), channel_id=1, source_target_pairs={{0,1},{1,0},{2,3},{3,2},{4,5},{5,4},{6,7},{7,6},{8,9},{9,8},{10,11... | collective-permute-start | bytes 245768 | tf_op jit(solution)/shard_map/ppermute | solution.py:355
  34.4 19.8 %collective-permute-start.10 = (bf16[464,256]{1,0:T(8,128)(2,1)S(1)}, bf16[464,256]{1,0:T(8,128)(2,1)S(1)}, u32[]{:S(2)}, u32[]{:S(2)}) collective-permute-start(bf16[464,256]{1,0:T(8,128)(2,1)S(1)} %broadcast_select_fusion), channel_id=1, source_target_pairs={{0,16},{1,17},{2,18},{3,19},{4,20},{5,21},{6,22},{7,23},{8,24},{9,... | collective-permute-start | bytes 712712 | tf_op jit(solution)/shard_map/ppermute | solution.py:355
  37.1 1.3 %collective-permute-start.24 = (f16[160,256]{1,0:T(8,128)(2,1)S(1)}, f16[160,256]{1,0:T(8,128)(2,1)S(1)}, u32[]{:S(2)}, u32[]{:S(2)}) collective-permute-start(f16[160,256]{1,0:T(8,128)(2,1)S(1)} %collective-permute-done.23), channel_id=1, source_target_pairs={{0,1},{1,0},{2,3},{3,2},{4,5},{5,4},{6,7},{7,6},{8,9},{9,8},{10,11... | collective-permute-start | bytes 245768 | tf_op jit(solution)/shard_map/ppermute | solution.py:355
  37.1 1.4 %collective-permute-start.26 = (f16[160,256]{1,0:T(8,128)(2,1)S(1)}, f16[160,256]{1,0:T(8,128)(2,1)S(1)}, u32[]{:S(2)}, u32[]{:S(2)}) collective-permute-start(f16[160,256]{1,0:T(8,128)(2,1)S(1)} %collective-permute-done.25), channel_id=1, source_target_pairs={{0,1},{1,0},{2,3},{3,2},{4,5},{5,4},{6,7},{7,6},{8,9},{9,8},{10,11... | collective-permute-start | bytes 245768 | tf_op jit(solution)/shard_map/ppermute | solution.py:355
  39.3 4.8 %collective-permute-start.27 = (bf16[80,128]{1,0:T(8,128)(2,1)S(1)}, bf16[80,128]{1,0:T(8,128)(2,1)S(1)}, u32[]{:S(2)}, u32[]{:S(2)}) collective-permute-start(bf16[80,128]{1,0:T(8,128)(2,1)S(1)} %shard_map.79), channel_id=1, source_target_pairs={{0,8},{1,9},{2,10},{3,11},{4,12},{5,13},{6,14},{7,15},{8,0},{9,1},... | collective-permute-start | bytes 61448 | tf_op jit(solution)/shard_map/ppermute | solution.py:355
  41.6 6.7 %collective-permute-start.28 = (bf16[80,128]{1,0:T(8,128)(2,1)S(1)}, bf16[80,128]{1,0:T(8,128)(2,1)S(1)}, u32[]{:S(2)}, u32[]{:S(2)}) collective-permute-start(bf16[80,128]{1,0:T(8,128)(2,1)S(1)} %shard_map.79), channel_id=1, source_target_pairs={{0,16},{1,17},{2,18},{3,19},{4,20},{5,21},{6,22},{7,23},{8,24},{9,... | collective-permute-start | bytes 61448 | tf_op jit(solution)/shard_map/ppermute | solution.py:355
  43.3 5.7 %collective-permute-start.29 = (bf16[80,128]{1,0:T(8,128)(2,1)S(1)}, bf16[80,128]{1,0:T(8,128)(2,1)S(1)}, u32[]{:S(2)}, u32[]{:S(2)}) collective-permute-start(bf16[80,128]{1,0:T(8,128)(2,1)S(1)} %shard_map.79), channel_id=1, source_target_pairs={{0,24},{1,25},{2,26},{3,27},{4,28},{5,29},{6,30},{7,31},{8,16},{9,... | collective-permute-start | bytes 61448 | tf_op jit(solution)/shard_map/ppermute | solution.py:355
  44.1 27.9 %copy-start.6 = (s32[2,256]{1,0:T(2,128)S(1)}, s32[2,256]{1,0:T(2,128)}, u32[]{:S(2)}) copy-start(s32[2,256]{1,0:T(2,128)} %index_ref.9) | copy-start | bytes 6148
  44.1 27.9 %copy-start.8 = (s32[2]{0:T(128)S(1)}, s32[2]{0:T(128)}, u32[]{:S(2)}) copy-start(s32[2]{0:T(128)} %owners_ref.7) | copy-start | bytes 28
  44.1 10.1 %collective-permute-start.38 = (f16[160,256]{1,0:T(8,128)(2,1)S(1)}, f16[160,256]{1,0:T(8,128)(2,1)S(1)}, u32[]{:S(2)}, u32[]{:S(2)}) collective-permute-start(f16[160,256]{1,0:T(8,128)(2,1)S(1)} %broadcast_select_fusion.4), channel_id=1, source_target_pairs={{0,16},{1,17},{2,18},{3,19},{4,20},{5,21},{6,22},{7,23},{8,24},{9,... | collective-permute-start | bytes 245768 | tf_op jit(solution)/shard_map/ppermute | solution.py:355
  48.9 8.9 %collective-permute-start.31 = (bf16[320,128]{1,0:T(8,128)(2,1)S(1)}, bf16[320,128]{1,0:T(8,128)(2,1)S(1)}, u32[]{:S(2)}, u32[]{:S(2)}) collective-permute-start(bf16[320,128]{1,0:T(8,128)(2,1)S(1)} %pad_maximum_fusion.refs_0_), channel_id=1, source_target_pairs={{0,2},{1,3},{2,0},{3,1},{4,6},{5,7},{6,4},{7,5},{8,10},{9,11},{10,... | collective-permute-start | bytes 245768 | tf_op jit(solution)/shard_map/ppermute | solution.py:355
  51.8 8.1 %collective-permute-start.33 = (bf16[320,128]{1,0:T(8,128)(2,1)S(1)}, bf16[320,128]{1,0:T(8,128)(2,1)S(1)}, u32[]{:S(2)}, u32[]{:S(2)}) collective-permute-start(bf16[320,128]{1,0:T(8,128)(2,1)S(1)} %pad_maximum_fusion.refs_0_), channel_id=1, source_target_pairs={{0,4},{1,5},{2,6},{3,7},{4,0},{5,1},{6,2},{7,3},{8,12},{9,13},{10,... | collective-permute-start | bytes 245768 | tf_op jit(solution)/shard_map/ppermute | solution.py:355
  54.2 6.5 %collective-permute-start.35 = (bf16[320,128]{1,0:T(8,128)(2,1)S(1)}, bf16[320,128]{1,0:T(8,128)(2,1)S(1)}, u32[]{:S(2)}, u32[]{:S(2)}) collective-permute-start(bf16[320,128]{1,0:T(8,128)(2,1)S(1)} %pad_maximum_fusion.refs_0_), channel_id=1, source_target_pairs={{0,6},{1,7},{2,4},{3,5},{4,2},{5,3},{6,0},{7,1},{8,14},{9,15},{10,... | collective-permute-start | bytes 245768 | tf_op jit(solution)/shard_map/ppermute | solution.py:355
  54.2 7.3 %collective-permute-start.12 = (bf16[464,256]{1,0:T(8,128)(2,1)S(1)}, bf16[464,256]{1,0:T(8,128)(2,1)S(1)}, u32[]{:S(2)}, u32[]{:S(2)}) collective-permute-start(bf16[464,256]{1,0:T(8,128)(2,1)S(1)} %broadcast_select_fusion.1.refs_0_), channel_id=1, source_target_pairs={{0,2},{1,3},{2,0},{3,1},{4,6},{5,7},{6,4},{7,5},{8,10},{9,11},{10,... | collective-permute-start | bytes 712712 | tf_op jit(solution)/shard_map/ppermute | solution.py:355
  55.7 11.6 %collective-permute-start.14 = (bf16[464,256]{1,0:T(8,128)(2,1)S(1)}, bf16[464,256]{1,0:T(8,128)(2,1)S(1)}, u32[]{:S(2)}, u32[]{:S(2)}) collective-permute-start(bf16[464,256]{1,0:T(8,128)(2,1)S(1)} %broadcast_select_fusion.1.refs_0_), channel_id=1, source_target_pairs={{0,4},{1,5},{2,6},{3,7},{4,0},{5,1},{6,2},{7,3},{8,12},{9,13},{10,... | collective-permute-start | bytes 712712 | tf_op jit(solution)/shard_map/ppermute | solution.py:355
  57.8 11.6 %collective-permute-start.1 = (bf16[464,256]{1,0:T(8,128)(2,1)S(1)}, bf16[464,256]{1,0:T(8,128)(2,1)S(1)}, u32[]{:S(2)}, u32[]{:S(2)}) collective-permute-start(bf16[464,256]{1,0:T(8,128)(2,1)S(1)} %broadcast_select_fusion.2), channel_id=1, source_target_pairs={{0,16},{1,17},{2,18},{3,19},{4,20},{5,21},{6,22},{7,23},{8,24},{9,... | collective-permute-start | bytes 712712 | tf_op jit(solution)/shard_map/ppermute | solution.py:355
  59.9 9.6 %collective-permute-start.16 = (bf16[464,256]{1,0:T(8,128)(2,1)S(1)}, bf16[464,256]{1,0:T(8,128)(2,1)S(1)}, u32[]{:S(2)}, u32[]{:S(2)}) collective-permute-start(bf16[464,256]{1,0:T(8,128)(2,1)S(1)} %broadcast_select_fusion.1.refs_0_), channel_id=1, source_target_pairs={{0,6},{1,7},{2,4},{3,5},{4,2},{5,3},{6,0},{7,1},{8,14},{9,15},{10,... | collective-permute-start | bytes 712712 | tf_op jit(solution)/shard_map/ppermute | solution.py:355
  60.7 9.3 %collective-permute-start.11 = (bf16[464,256]{1,0:T(8,128)(2,1)S(1)}, bf16[464,256]{1,0:T(8,128)(2,1)S(1)}, u32[]{:S(2)}, u32[]{:S(2)}) collective-permute-start(bf16[464,256]{1,0:T(8,128)(2,1)S(1)} %broadcast_select_fusion.1.refs_0_), channel_id=1, source_target_pairs={{0,1},{1,0},{2,3},{3,2},{4,5},{5,4},{6,7},{7,6},{8,9},{9,8},{10,11... | collective-permute-start | bytes 712712 | tf_op jit(solution)/shard_map/ppermute | solution.py:355
  61.5 8.5 %collective-permute-start.13 = (bf16[464,256]{1,0:T(8,128)(2,1)S(1)}, bf16[464,256]{1,0:T(8,128)(2,1)S(1)}, u32[]{:S(2)}, u32[]{:S(2)}) collective-permute-start(bf16[464,256]{1,0:T(8,128)(2,1)S(1)} %collective-permute-done.12.refs_2_), channel_id=1, source_target_pairs={{0,1},{1,0},{2,3},{3,2},{4,5},{5,4},{6,7},{7,6},{8,9},{9,8},{10,11... | collective-permute-start | bytes 712712 | tf_op jit(solution)/shard_map/ppermute | solution.py:355
  67.4 3.1 %collective-permute-start.15 = (bf16[464,256]{1,0:T(8,128)(2,1)S(1)}, bf16[464,256]{1,0:T(8,128)(2,1)S(1)}, u32[]{:S(2)}, u32[]{:S(2)}) collective-permute-start(bf16[464,256]{1,0:T(8,128)(2,1)S(1)} %collective-permute-done.14.refs_4_), channel_id=1, source_target_pairs={{0,1},{1,0},{2,3},{3,2},{4,5},{5,4},{6,7},{7,6},{8,9},{9,8},{10,11... | collective-permute-start | bytes 712712 | tf_op jit(solution)/shard_map/ppermute | solution.py:355
  69.4 3.9 %collective-permute-start.30 = (bf16[320,128]{1,0:T(8,128)(2,1)S(1)}, bf16[320,128]{1,0:T(8,128)(2,1)S(1)}, u32[]{:S(2)}, u32[]{:S(2)}) collective-permute-start(bf16[320,128]{1,0:T(8,128)(2,1)S(1)} %pad_maximum_fusion.refs_0_), channel_id=1, source_target_pairs={{0,1},{1,0},{2,3},{3,2},{4,5},{5,4},{6,7},{7,6},{8,9},{9,8},{10,11... | collective-permute-start | bytes 245768 | tf_op jit(solution)/shard_map/ppermute | solution.py:355
  69.4 3.9 %collective-permute-start.32 = (bf16[320,128]{1,0:T(8,128)(2,1)S(1)}, bf16[320,128]{1,0:T(8,128)(2,1)S(1)}, u32[]{:S(2)}, u32[]{:S(2)}) collective-permute-start(bf16[320,128]{1,0:T(8,128)(2,1)S(1)} %collective-permute-done.31.refs_2_), channel_id=1, source_target_pairs={{0,1},{1,0},{2,3},{3,2},{4,5},{5,4},{6,7},{7,6},{8,9},{9,8},{10,11... | collective-permute-start | bytes 245768 | tf_op jit(solution)/shard_map/ppermute | solution.py:355
  70.0 3.4 %collective-permute-start.34 = (bf16[320,128]{1,0:T(8,128)(2,1)S(1)}, bf16[320,128]{1,0:T(8,128)(2,1)S(1)}, u32[]{:S(2)}, u32[]{:S(2)}) collective-permute-start(bf16[320,128]{1,0:T(8,128)(2,1)S(1)} %collective-permute-done.33.refs_4_), channel_id=1, source_target_pairs={{0,1},{1,0},{2,3},{3,2},{4,5},{5,4},{6,7},{7,6},{8,9},{9,8},{10,11... | collective-permute-start | bytes 245768 | tf_op jit(solution)/shard_map/ppermute | solution.py:355
  70.0 3.4 %collective-permute-start.36 = (bf16[320,128]{1,0:T(8,128)(2,1)S(1)}, bf16[320,128]{1,0:T(8,128)(2,1)S(1)}, u32[]{:S(2)}, u32[]{:S(2)}) collective-permute-start(bf16[320,128]{1,0:T(8,128)(2,1)S(1)} %collective-permute-done.35.refs_6_), channel_id=1, source_target_pairs={{0,1},{1,0},{2,3},{3,2},{4,5},{5,4},{6,7},{7,6},{8,9},{9,8},{10,11... | collective-permute-start | bytes 245768 | tf_op jit(solution)/shard_map/ppermute | solution.py:355
  70.5 1.5 %collective-permute-start.17 = (bf16[464,256]{1,0:T(8,128)(2,1)S(1)}, bf16[464,256]{1,0:T(8,128)(2,1)S(1)}, u32[]{:S(2)}, u32[]{:S(2)}) collective-permute-start(bf16[464,256]{1,0:T(8,128)(2,1)S(1)} %collective-permute-done.16.refs_6_), channel_id=1, source_target_pairs={{0,1},{1,0},{2,3},{3,2},{4,5},{5,4},{6,7},{7,6},{8,9},{9,8},{10,11... | collective-permute-start | bytes 712712 | tf_op jit(solution)/shard_map/ppermute | solution.py:355
  74.1 4.3 %collective-permute-start.39 = (f16[160,256]{1,0:T(8,128)(2,1)S(1)}, f16[160,256]{1,0:T(8,128)(2,1)S(1)}, u32[]{:S(2)}, u32[]{:S(2)}) collective-permute-start(f16[160,256]{1,0:T(8,128)(2,1)S(1)} %get-tuple-element.33), channel_id=1, source_target_pairs={{0,1},{1,0},{2,3},{3,2},{4,5},{5,4},{6,7},{7,6},{8,9},{9,8},{10,11... | collective-permute-start | bytes 245768 | tf_op jit(solution)/shard_map/ppermute | solution.py:355
  74.3 5.3 %collective-permute-start.40 = (f16[160,256]{1,0:T(8,128)(2,1)S(1)}, f16[160,256]{1,0:T(8,128)(2,1)S(1)}, u32[]{:S(2)}, u32[]{:S(2)}) collective-permute-start(f16[160,256]{1,0:T(8,128)(2,1)S(1)} %get-tuple-element.33), channel_id=1, source_target_pairs={{0,2},{1,3},{2,0},{3,1},{4,6},{5,7},{6,4},{7,5},{8,10},{9,11},{10,... | collective-permute-start | bytes 245768 | tf_op jit(solution)/shard_map/ppermute | solution.py:355
  74.7 19.7 %collective-permute-start.3 = (bf16[464,256]{1,0:T(8,128)(2,1)S(1)}, bf16[464,256]{1,0:T(8,128)(2,1)S(1)}, u32[]{:S(2)}, u32[]{:S(2)}) collective-permute-start(bf16[464,256]{1,0:T(8,128)(2,1)S(1)} %broadcast_select_fusion.3.refs_0_.second_ref), channel_id=1, source_target_pairs={{0,2},{1,3},{2,0},{3,1},{4,6},{5,7},{6,4},{7,5},{8,10},{9,11},{10,... | collective-permute-start | bytes 712712 | tf_op jit(solution)/shard_map/ppermute | solution.py:355
  76.4 18.0 %collective-permute-start.5 = (bf16[464,256]{1,0:T(8,128)(2,1)S(1)}, bf16[464,256]{1,0:T(8,128)(2,1)S(1)}, u32[]{:S(2)}, u32[]{:S(2)}) collective-permute-start(bf16[464,256]{1,0:T(8,128)(2,1)S(1)} %broadcast_select_fusion.3.refs_0_.second_ref), channel_id=1, source_target_pairs={{0,4},{1,5},{2,6},{3,7},{4,0},{5,1},{6,2},{7,3},{8,12},{9,13},{10,... | collective-permute-start | bytes 712712 | tf_op jit(solution)/shard_map/ppermute | solution.py:355
  76.7 10.6 %collective-permute-start.42 = (f16[160,256]{1,0:T(8,128)(2,1)S(1)}, f16[160,256]{1,0:T(8,128)(2,1)S(1)}, u32[]{:S(2)}, u32[]{:S(2)}) collective-permute-start(f16[160,256]{1,0:T(8,128)(2,1)S(1)} %get-tuple-element.33), channel_id=1, source_target_pairs={{0,4},{1,5},{2,6},{3,7},{4,0},{5,1},{6,2},{7,3},{8,12},{9,13},{10,... | collective-permute-start | bytes 245768 | tf_op jit(solution)/shard_map/ppermute | solution.py:355
  78.4 9.4 %collective-permute-start.44 = (f16[160,256]{1,0:T(8,128)(2,1)S(1)}, f16[160,256]{1,0:T(8,128)(2,1)S(1)}, u32[]{:S(2)}, u32[]{:S(2)}) collective-permute-start(f16[160,256]{1,0:T(8,128)(2,1)S(1)} %get-tuple-element.33), channel_id=1, source_target_pairs={{0,6},{1,7},{2,4},{3,5},{4,2},{5,3},{6,0},{7,1},{8,14},{9,15},{10,... | collective-permute-start | bytes 245768 | tf_op jit(solution)/shard_map/ppermute | solution.py:355
  79.6 8.1 %collective-permute-start.41 = (f16[160,256]{1,0:T(8,128)(2,1)S(1)}, f16[160,256]{1,0:T(8,128)(2,1)S(1)}, u32[]{:S(2)}, u32[]{:S(2)}) collective-permute-start(f16[160,256]{1,0:T(8,128)(2,1)S(1)} %collective-permute-done.40), channel_id=1, source_target_pairs={{0,1},{1,0},{2,3},{3,2},{4,5},{5,4},{6,7},{7,6},{8,9},{9,8},{10,11... | collective-permute-start | bytes 245768 | tf_op jit(solution)/shard_map/ppermute | solution.py:355
  87.4 7.5 %collective-permute-start.7 = (bf16[464,256]{1,0:T(8,128)(2,1)S(1)}, bf16[464,256]{1,0:T(8,128)(2,1)S(1)}, u32[]{:S(2)}, u32[]{:S(2)}) collective-permute-start(bf16[464,256]{1,0:T(8,128)(2,1)S(1)} %broadcast_select_fusion.3.refs_0_.second_ref), channel_id=1, source_target_pairs={{0,6},{1,7},{2,4},{3,5},{4,2},{5,3},{6,0},{7,1},{8,14},{9,15},{10,... | collective-permute-start | bytes 712712 | tf_op jit(solution)/shard_map/ppermute | solution.py:355
  87.8 1.3 %collective-permute-start.43 = (f16[160,256]{1,0:T(8,128)(2,1)S(1)}, f16[160,256]{1,0:T(8,128)(2,1)S(1)}, u32[]{:S(2)}, u32[]{:S(2)}) collective-permute-start(f16[160,256]{1,0:T(8,128)(2,1)S(1)} %collective-permute-done.42), channel_id=1, source_target_pairs={{0,1},{1,0},{2,3},{3,2},{4,5},{5,4},{6,7},{7,6},{8,9},{9,8},{10,11... | collective-permute-start | bytes 245768 | tf_op jit(solution)/shard_map/ppermute | solution.py:355
  87.8 1.4 %collective-permute-start.45 = (f16[160,256]{1,0:T(8,128)(2,1)S(1)}, f16[160,256]{1,0:T(8,128)(2,1)S(1)}, u32[]{:S(2)}, u32[]{:S(2)}) collective-permute-start(f16[160,256]{1,0:T(8,128)(2,1)S(1)} %collective-permute-done.44), channel_id=1, source_target_pairs={{0,1},{1,0},{2,3},{3,2},{4,5},{5,4},{6,7},{7,6},{8,9},{9,8},{10,11... | collective-permute-start | bytes 245768 | tf_op jit(solution)/shard_map/ppermute | solution.py:355
  90.0 5.0 %collective-permute-start.46 = (bf16[80,128]{1,0:T(8,128)(2,1)S(1)}, bf16[80,128]{1,0:T(8,128)(2,1)S(1)}, u32[]{:S(2)}, u32[]{:S(2)}) collective-permute-start(bf16[80,128]{1,0:T(8,128)(2,1)S(1)} %shard_map.81), channel_id=1, source_target_pairs={{0,8},{1,9},{2,10},{3,11},{4,12},{5,13},{6,14},{7,15},{8,0},{9,1},... | collective-permute-start | bytes 61448 | tf_op jit(solution)/shard_map/ppermute | solution.py:355
  91.4 4.9 %collective-permute-start.47 = (bf16[80,128]{1,0:T(8,128)(2,1)S(1)}, bf16[80,128]{1,0:T(8,128)(2,1)S(1)}, u32[]{:S(2)}, u32[]{:S(2)}) collective-permute-start(bf16[80,128]{1,0:T(8,128)(2,1)S(1)} %shard_map.81), channel_id=1, source_target_pairs={{0,16},{1,17},{2,18},{3,19},{4,20},{5,21},{6,22},{7,23},{8,24},{9,... | collective-permute-start | bytes 61448 | tf_op jit(solution)/shard_map/ppermute | solution.py:355
  94.4 11.1 %collective-permute-start.2 = (bf16[464,256]{1,0:T(8,128)(2,1)S(1)}, bf16[464,256]{1,0:T(8,128)(2,1)S(1)}, u32[]{:S(2)}, u32[]{:S(2)}) collective-permute-start(bf16[464,256]{1,0:T(8,128)(2,1)S(1)} %broadcast_select_fusion.3.refs_0_.second_ref), channel_id=1, source_target_pairs={{0,1},{1,0},{2,3},{3,2},{4,5},{5,4},{6,7},{7,6},{8,9},{9,8},{10,11... | collective-permute-start | bytes 712712 | tf_op jit(solution)/shard_map/ppermute | solution.py:355
  94.4 11.7 %collective-permute-start.4 = (bf16[464,256]{1,0:T(8,128)(2,1)S(1)}, bf16[464,256]{1,0:T(8,128)(2,1)S(1)}, u32[]{:S(2)}, u32[]{:S(2)}) collective-permute-start(bf16[464,256]{1,0:T(8,128)(2,1)S(1)} %collective-permute-done.3.refs_2_), channel_id=1, source_target_pairs={{0,1},{1,0},{2,3},{3,2},{4,5},{5,4},{6,7},{7,6},{8,9},{9,8},{10,11... | collective-permute-start | bytes 712712 | tf_op jit(solution)/shard_map/ppermute | solution.py:355
  94.9 13.0 %collective-permute-start.6 = (bf16[464,256]{1,0:T(8,128)(2,1)S(1)}, bf16[464,256]{1,0:T(8,128)(2,1)S(1)}, u32[]{:S(2)}, u32[]{:S(2)}) collective-permute-start(bf16[464,256]{1,0:T(8,128)(2,1)S(1)} %collective-permute-done.5.refs_4_), channel_id=1, source_target_pairs={{0,1},{1,0},{2,3},{3,2},{4,5},{5,4},{6,7},{7,6},{8,9},{9,8},{10,11... | collective-permute-start | bytes 712712 | tf_op jit(solution)/shard_map/ppermute | solution.py:355
  95.0 12.9 %collective-permute-start.8 = (bf16[464,256]{1,0:T(8,128)(2,1)S(1)}, bf16[464,256]{1,0:T(8,128)(2,1)S(1)}, u32[]{:S(2)}, u32[]{:S(2)}) collective-permute-start(bf16[464,256]{1,0:T(8,128)(2,1)S(1)} %collective-permute-done.7.refs_6_), channel_id=1, source_target_pairs={{0,1},{1,0},{2,3},{3,2},{4,5},{5,4},{6,7},{7,6},{8,9},{9,8},{10,11... | collective-permute-start | bytes 712712 | tf_op jit(solution)/shard_map/ppermute | solution.py:355
  96.3 7.9 %collective-permute-start.48 = (bf16[80,128]{1,0:T(8,128)(2,1)S(1)}, bf16[80,128]{1,0:T(8,128)(2,1)S(1)}, u32[]{:S(2)}, u32[]{:S(2)}) collective-permute-start(bf16[80,128]{1,0:T(8,128)(2,1)S(1)} %shard_map.81), channel_id=1, source_target_pairs={{0,24},{1,25},{2,26},{3,27},{4,28},{5,29},{6,30},{7,31},{8,16},{9,... | collective-permute-start | bytes 61448 | tf_op jit(solution)/shard_map/ppermute | solution.py:355
  104.3 9.3 %copy-start.3 = (f32[2048,147]{0,1:T(8,128)S(1)}, f32[2048,147]{0,1:T(8,128)}, u32[]{:S(2)}) copy-start(f32[2048,147]{0,1:T(8,128)} %param.8) | copy-start | bytes 3612676
  104.3 8.3 %collective-permute-start.50 = (bf16[320,128]{1,0:T(8,128)(2,1)S(1)}, bf16[320,128]{1,0:T(8,128)(2,1)S(1)}, u32[]{:S(2)}, u32[]{:S(2)}) collective-permute-start(bf16[320,128]{1,0:T(8,128)(2,1)S(1)} %pad_maximum_fusion.1.refs_0_), channel_id=1, source_target_pairs={{0,2},{1,3},{2,0},{3,1},{4,6},{5,7},{6,4},{7,5},{8,10},{9,11},{10,... | collective-permute-start | bytes 245768 | tf_op jit(solution)/shard_map/ppermute | solution.py:355
  105.5 7.6 %collective-permute-start.52 = (bf16[320,128]{1,0:T(8,128)(2,1)S(1)}, bf16[320,128]{1,0:T(8,128)(2,1)S(1)}, u32[]{:S(2)}, u32[]{:S(2)}) collective-permute-start(bf16[320,128]{1,0:T(8,128)(2,1)S(1)} %pad_maximum_fusion.1.refs_0_), channel_id=1, source_target_pairs={{0,4},{1,5},{2,6},{3,7},{4,0},{5,1},{6,2},{7,3},{8,12},{9,13},{10,... | collective-permute-start | bytes 245768 | tf_op jit(solution)/shard_map/ppermute | solution.py:355
  106.0 7.2 %collective-permute-start.54 = (bf16[320,128]{1,0:T(8,128)(2,1)S(1)}, bf16[320,128]{1,0:T(8,128)(2,1)S(1)}, u32[]{:S(2)}, u32[]{:S(2)}) collective-permute-start(bf16[320,128]{1,0:T(8,128)(2,1)S(1)} %pad_maximum_fusion.1.refs_0_), channel_id=1, source_target_pairs={{0,6},{1,7},{2,4},{3,5},{4,2},{5,3},{6,0},{7,1},{8,14},{9,15},{10,... | collective-permute-start | bytes 245768 | tf_op jit(solution)/shard_map/ppermute | solution.py:355
  112.5 4.5 %collective-permute-start.49 = (bf16[320,128]{1,0:T(8,128)(2,1)S(1)}, bf16[320,128]{1,0:T(8,128)(2,1)S(1)}, u32[]{:S(2)}, u32[]{:S(2)}) collective-permute-start(bf16[320,128]{1,0:T(8,128)(2,1)S(1)} %pad_maximum_fusion.1.refs_0_), channel_id=1, source_target_pairs={{0,1},{1,0},{2,3},{3,2},{4,5},{5,4},{6,7},{7,6},{8,9},{9,8},{10,11... | collective-permute-start | bytes 245768 | tf_op jit(solution)/shard_map/ppermute | solution.py:355
  112.6 4.4 %collective-permute-start.51 = (bf16[320,128]{1,0:T(8,128)(2,1)S(1)}, bf16[320,128]{1,0:T(8,128)(2,1)S(1)}, u32[]{:S(2)}, u32[]{:S(2)}) collective-permute-start(bf16[320,128]{1,0:T(8,128)(2,1)S(1)} %collective-permute-done.50.refs_2_), channel_id=1, source_target_pairs={{0,1},{1,0},{2,3},{3,2},{4,5},{5,4},{6,7},{7,6},{8,9},{9,8},{10,11... | collective-permute-start | bytes 245768 | tf_op jit(solution)/shard_map/ppermute | solution.py:355
  113.1 4.0 %collective-permute-start.53 = (bf16[320,128]{1,0:T(8,128)(2,1)S(1)}, bf16[320,128]{1,0:T(8,128)(2,1)S(1)}, u32[]{:S(2)}, u32[]{:S(2)}) collective-permute-start(bf16[320,128]{1,0:T(8,128)(2,1)S(1)} %collective-permute-done.52.refs_4_), channel_id=1, source_target_pairs={{0,1},{1,0},{2,3},{3,2},{4,5},{5,4},{6,7},{7,6},{8,9},{9,8},{10,11... | collective-permute-start | bytes 245768 | tf_op jit(solution)/shard_map/ppermute | solution.py:355
  113.2 3.9 %collective-permute-start.55 = (bf16[320,128]{1,0:T(8,128)(2,1)S(1)}, bf16[320,128]{1,0:T(8,128)(2,1)S(1)}, u32[]{:S(2)}, u32[]{:S(2)}) collective-permute-start(bf16[320,128]{1,0:T(8,128)(2,1)S(1)} %collective-permute-done.54.refs_6_), channel_id=1, source_target_pairs={{0,1},{1,0},{2,3},{3,2},{4,5},{5,4},{6,7},{7,6},{8,9},{9,8},{10,11... | collective-permute-start | bytes 245768 | tf_op jit(solution)/shard_map/ppermute | solution.py:355
  (1 other events, 0.7 us)

commit v3 on v2

--- a/solution.py
+++ b/solution.py
@@ -67,7 +67,14 @@
     rows = up(outputs, 16)
     steps, picks = index.shape
 
-    def body(index_ref, residual_ref, *out_ref):
+    def body(index_hbm, residual_hbm, *refs):
+        out_ref, (index_ref, residual_ref, index_sem, residual_sem) = refs[:steps], refs[steps:]
+        index_copy = pltpu.make_async_copy(index_hbm, index_ref, index_sem)
+        residual_copy = pltpu.make_async_copy(residual_hbm, residual_ref, residual_sem)
+        residual_copy.start()
+        index_copy.start()
+        index_copy.wait()
+        residual_copy.wait()
         both = jnp.concatenate(split(padded(residual_ref[...], rows), 2), 0)
         for step in range(steps):
             found = matmul(both, one_hot(frames, index_ref[step : step + 1, :]))
@@ -75,9 +82,15 @@
 
     return pl.pallas_call(
         body,
-        in_specs=[vmem, vmem],
+        in_specs=[pl.BlockSpec(memory_space=pl.ANY)] * 2,
         out_specs=(vmem,) * steps,
         out_shape=(jax.ShapeDtypeStruct((rows, picks), f32),) * steps,
+        scratch_shapes=[
+            pltpu.VMEM((steps, picks), jnp.int32),
+            pltpu.VMEM((outputs, frames), f32),
+            pltpu.SemaphoreType.DMA,
+            pltpu.SemaphoreType.DMA,
+        ],
         compiler_params=params(),
         name="pick_residual",
     )(index, residual_t)
@@ -144,18 +157,32 @@
     return jnp.concatenate([update[:half], update[half:]], 1).astype(bf16)
 
 
-def prepare(features_t, inverse, picks):
+def localize(features_t):
     width, frames = features_t.shape
     depth = up(width + 18, 16)
-    steps, mine, block = inverse.shape
-
-    def body(features_ref, inverse_ref, local_ref, *stacked_ref):
+
+    def body(features_ref, local_ref):
         features = features_ref[...]
         wide = features.astype(f32)
         squares = jnp.sum(wide * wide, axis=0, keepdims=True)
         local_ref[0:width, :] = features
         rest = jnp.zeros((depth - width - 18, frames), bf16)
         local_ref[width:depth, :] = jnp.concatenate([norm_rows(squares, (1, 1, 0)), rest], 0)
+
+    return pl.pallas_call(
+        body,
+        in_specs=[vmem],
+        out_specs=vmem,
+        out_shape=jax.ShapeDtypeStruct((depth, frames), bf16),
+        compiler_params=params(),
+        name="localize",
+    )(features_t)
+
+
+def prepare(inverse, picks):
+    steps, mine, block = inverse.shape
+
+    def body(inverse_ref, *stacked_ref):
         for step in range(steps):
             for k in range(block // picks):
                 high, low = split(inverse_ref[step, :, lane_start(piece_col(k), picks)], 2)
@@ -163,13 +190,12 @@
 
     return pl.pallas_call(
         body,
-        in_specs=[vmem, vmem],
-        out_specs=(vmem,) * (1 + steps),
-        out_shape=(jax.ShapeDtypeStruct((depth, frames), bf16),)
-        + (jax.ShapeDtypeStruct((2 * mine, block), bf16),) * steps,
+        in_specs=[vmem],
+        out_specs=(vmem,) * steps,
+        out_shape=(jax.ShapeDtypeStruct((2 * mine, block), bf16),) * steps,
         compiler_params=params(),
         name="prepare",
-    )(features_t, inverse)
+    )(inverse)
 
 
 def block_update(picked, stacked, scaled):
@@ -290,15 +316,16 @@
             canon[half:, place] = lower.astype(bf16)
 
 
-def apply_update(owners, pieces, kernel, index, step, residual_t, coeffs_t):
+def apply_update(owners, pieces, kernels, index, step, residual_t, coeffs_t):
     outputs, frames = residual_t.shape
-    block = kernel.shape[0]
+    block = sum(kernel.shape[0] for kernel in kernels)
     picks = index.shape[1]
     count = len(pieces)
     rows = up(outputs, 16)
     tile = min(1024, frames)
 
-    def body(owners_ref, index_ref, kernel_ref, residual_ref, coeffs_ref, *refs):
+    def body(owners_ref, index_ref, residual_ref, coeffs_ref, *refs):
+        kernels_ref, refs = refs[: len(kernels)], refs[len(kernels) :]
         pieces_ref = refs[:count]
         new_residual_ref, new_coeffs_ref, canon, own, places = refs[count:]
         here = pl.program_id(0)
@@ -310,18 +337,22 @@
             own[...] = jnp.where(lax.axis_index("rows") == owners_ref[step], mine, jnp.zeros_like(mine))
             places[...] = turn(index_ref[step : step + 1, :])
 
-        change = matmul(canon[...], kernel_ref[:, lane_start(here, tile)])
+        change, first = 0.0, 0
+        for kernel_ref in kernels_ref:
+            last = first + kernel_ref.shape[0]
+            change = change + matmul(canon[:, first:last], kernel_ref[:, lane_start(here, tile)])
+            first = last
         frame = lax.broadcasted_iota(jnp.int32, (picks, tile), 1) + here * tile
         hot = jnp.where(frame == places[...], 1.0, 0.0).astype(bf16)
         put = matmul(own[...], hot)
-        new_residual_ref[...] = residual_ref[...] - (change + penalty * put)[:outputs]
-        new_coeffs_ref[...] = coeffs_ref[...] + put[:outputs]
+        new_residual_ref[...] = residual_ref[:, lane_start(here, tile)] - (change + penalty * put)[:outputs]
+        new_coeffs_ref[...] = coeffs_ref[:, lane_start(here, tile)] + put[:outputs]
 
     strip = pl.BlockSpec((outputs, tile), lambda i: (0, i))
     return pl.pallas_call(
         body,
         grid=(frames // tile,),
-        in_specs=[smem, vmem, vmem, strip, strip] + [vmem] * count,
+        in_specs=[smem, vmem, vmem, vmem] + [vmem] * (len(kernels) + count),
         out_specs=(strip, strip),
         out_shape=(
             jax.ShapeDtypeStruct((outputs, frames), f32),
@@ -336,7 +367,7 @@
             flops=2 * rows * block * frames, transcendentals=0, bytes_accessed=2 * block * frames
         ),
         compiler_params=params(),
-    )(owners, index, kernel, residual_t, coeffs_t, *pieces)
+    )(owners, index, residual_t, coeffs_t, *kernels, *pieces)
 
 
 class Sender:
@@ -393,25 +424,30 @@
     first_block, second_block, *takes = pick_features(
         owners, block_index, features_t, [(step, rule) for step in range(2) for rule in rules]
     )
-    local, *stacked = prepare(features_t, block_inverse, picks)
+    stacked = prepare(block_inverse, picks)
+    local = localize(features_t)
     first = sender.over_cols(sender.spread(first.astype(f16), moves, takes))
     first_block = sender.over_cols(sender.spread(first_block, moves, takes))
-    second = sender.spread(second.astype(f16), moves, takes[len(rules) :]).astype(f32)
-    second_block = sender.spread(second_block, moves, takes[len(rules) :])
+    depth = second_block.shape[0]
+    both = jnp.concatenate([second_block.astype(f16), second.astype(f16)], 0)
+    both = sender.spread(both, moves, takes[len(rules) :])
+    second_block, second = both[:depth].astype(bf16), both[depth:].astype(f32)
     update = block_update(jnp.concatenate(first, 1).astype(f32), stacked[0], 1.0)
     update = sender.over_cols(jnp.concatenate(sender.over_rows(update), 0))
     meeting = meeting_kernel(owners, block_index, first_block, second_block, scale)
     second = sender.over_cols(advance(meeting, second, update, scaled).astype(f16))
-    first_kernel = block_kernel(first_block, local, scale)
+    near = len(first_block) // 2
+    near_kernel = block_kernel(first_block[:near], local, scale)
+    far_kernel = block_kernel(first_block[near:], local, scale)
     later = block_update(jnp.concatenate(second, 1).astype(f32), stacked[1], 1.0 / scaled)
     later = sender.over_cols(jnp.concatenate(sender.over_rows(later), 0))
     second_block = sender.over_cols(second_block)
     second_kernel = block_kernel(second_block, local, scale)
     residual_t, coeffs_t = apply_update(
-        owners, update, first_kernel, block_index, 0, residual_t, coeffs_t
+        owners, update, (near_kernel, far_kernel), block_index, 0, residual_t, coeffs_t
     )
     residual_t, coeffs_t = apply_update(
-        owners, later, second_kernel, block_index, 1, residual_t, coeffs_t
+        owners, later, (second_kernel,), block_index, 1, residual_t, coeffs_t
     )
     return (coeffs_t.T, residual_t.T)
 

time: 121 us -> 126 us (1.041)
  waiting for transfers between devices: 38.2 us -> 47.8 us
  starting transfers between devices: 53.7 us -> 49.3 us
    ppermute x56 -> x54, waiting for transfers between devices: 38.2 us -> 47.8 us  [send(): return lax.ppermute(value, ('rows', 'cols'), pairs)]
    ppermute x56 -> x54, starting transfers between devices: 53.7 us -> 49.3 us  [send(): return lax.ppermute(value, ('rows', 'cols'), pairs)]
    pallas_call x2 -> x3, Pallas kernels: 9.49 us -> 9.67 us  [block_kernel(): pl.pallas_call(body, in_specs=[vmem] * (1 + count), out_specs=vmem, out_s...]
  transfers between devices with their start and end apart: 56 -> 54, of which waited for: 17 -> 13; matrix products, arithmetic and copies ran while one was open for 1% -> 1% of each run, Pallas kernels for 14% -> 14%
where the time goes in v3:
time: 126 us
  starting transfers between devices  49.3 us (39%)
  waiting for transfers between devices  47.8 us (38%)
  Pallas kernels  23.4 us (19%)
  local copies, waits for them, and re-layouts  3.74 us (3%)
    ppermute x54, starting transfers between devices, send(): return lax.ppermute(value, ('rows', 'cols'), pairs)  49.3 us
    ppermute x54, waiting for transfers between devices, send(): return lax.ppermute(value, ('rows', 'cols'), pairs)  47.8 us
    pallas_call x3, Pallas kernels, block_kernel(): pl.pallas_call(body, in_specs=[vmem] * (1 + count), out_specs=vmem, out_s...  9.67 us
    pallas_call x2, Pallas kernels, apply_update(): pl.pallas_call(body, grid=(frames // tile,), in_specs=[smem, vmem, vmem,...  7.13 us
    unnamed x30, local copies, waits for them, and re-layouts  3.71 us
  transfers between devices with their start and end apart: 54, of which 13 were waited for; matrix products, arithmetic and copies ran while one was open for 1% of the time, Pallas kernels for 14%

profile of v3, /device:TPU:0, one launch (start us, length us, event | category | flops | bytes accessed | tf_op | source)
XLA Modules:
  0.0 126.2 jit_solution(4616135710165479198)
XLA Ops:
  0.7 1.3 %copy-done.2 = f32[2048,147]{0,1:T(8,128)S(1)} copy-done((f32[2048,147]{0,1:T(8,128)S(1)}, f32[2048,147]{0,1:T(8,128)}, u32[]{:S(2)}) %copy-start.2) | copy-done | bytes 1204248
  1.9 0.7 copy-done.6
  2.6 1.2 pick_residual.1
  3.9 3.1 %collective-permute-start.9 = (f16[160,256]{1,0:T(8,128)(2,1)S(1)}, f16[160,256]{1,0:T(8,128)(2,1)S(1)}, u32[]{:S(2)}, u32[]{:S(2)}) collective-permute-start(f16[160,256]{1,0:T(8,128)(2,1)S(1)} %convert_element_type.24), channel_id=1, source_target_pairs={{0,8},{1,9},{2,10},{3,11},{4,12},{5,13},{6,14},{7,15},{8,0},{9,1},... | collective-permute-start | bytes 245768 | tf_op jit(solution)/shard_map/ppermute | solution.py:386
  7.0 1.5 %copy-done = bf16[2048,440]{0,1:T(8,128)(2,1)S(1)} copy-done((bf16[2048,440]{0,1:T(8,128)(2,1)S(1)}, bf16[2048,440]{0,1:T(8,128)(2,1)}, u32[]{:S(2)}) %copy-start) | copy-done | bytes 1802264
  8.5 1.7 %pick_features.1 = (bf16[464,256]{1,0:T(8,128)(2,1)S(1)}, bf16[464,256]{1,0:T(8,128)(2,1)S(1)}, f32[1,256]{1,0:T(1,128)S(1)}, f32[1,256]{1,0:T(1,128)S(1)}, f32[1,256]{1,0:T(1,128)S(1)}, /*index=5*/f32[1,256]{1,0:T(1,128)S(1)}) custom-call(s32[2]{0:T(128)S(1)} %copy-done.8, s32[2,256]{1,0:T(2,128)S(1)} %copy-done.7, bf16[440,2048]{1,0:T(8,128)(2,1)S(1)} %bitcast.5), custom_call_target="tpu_custom_call" | custom-call | tf_op jit(solution)/shard_map/pick_features/pallas_call | solution.py:135
  10.4 2.1 %collective-permute-start.28 = (f16[624,256]{1,0:T(8,128)(2,1)S(1)}, f16[624,256]{1,0:T(8,128)(2,1)S(1)}, u32[]{:S(2)}, u32[]{:S(2)}) collective-permute-start(f16[624,256]{1,0:T(8,128)(2,1)S(1)} %pad_maximum_fusion), channel_id=1, source_target_pairs={{0,8},{1,9},{2,10},{3,11},{4,12},{5,13},{6,14},{7,15},{8,0},{9,1},... | collective-permute-start | bytes 958472 | tf_op jit(solution)/shard_map/ppermute | solution.py:386
  12.6 2.7 %collective-permute-start.10 = (f16[160,256]{1,0:T(8,128)(2,1)S(1)}, f16[160,256]{1,0:T(8,128)(2,1)S(1)}, u32[]{:S(2)}, u32[]{:S(2)}) collective-permute-start(f16[160,256]{1,0:T(8,128)(2,1)S(1)} %broadcast_select_fusion.4), channel_id=1, source_target_pairs={{0,16},{1,17},{2,18},{3,19},{4,20},{5,21},{6,22},{7,23},{8,24},{9,... | collective-permute-start | bytes 245768 | tf_op jit(solution)/shard_map/ppermute | solution.py:386
  15.4 8.5 %collective-permute-done.10 = f16[160,256]{1,0:T(8,128)(2,1)S(1)} collective-permute-done((f16[160,256]{1,0:T(8,128)(2,1)S(1)}, f16[160,256]{1,0:T(8,128)(2,1)S(1)}, u32[]{:S(2)}, u32[]{:S(2)}) %collective-permute-start.10) | collective-permute-done | bytes 81952 | tf_op jit(solution)/shard_map/ppermute | solution.py:386
  24.0 2.7 %collective-permute-start.16 = (f16[160,256]{1,0:T(8,128)(2,1)S(1)}, f16[160,256]{1,0:T(8,128)(2,1)S(1)}, u32[]{:S(2)}, u32[]{:S(2)}) collective-permute-start(f16[160,256]{1,0:T(8,128)(2,1)S(1)} %get-tuple-element.33), channel_id=1, source_target_pairs={{0,6},{1,7},{2,4},{3,5},{4,2},{5,3},{6,0},{7,1},{8,14},{9,15},{10,... | collective-permute-start | bytes 245768 | tf_op jit(solution)/shard_map/ppermute | solution.py:386
  26.6 0.5 collective-permute-start.14
  27.1 0.4 collective-permute-start.12
  27.6 2.4 %collective-permute-done.16 = f16[160,256]{1,0:T(8,128)(2,1)S(1)} collective-permute-done((f16[160,256]{1,0:T(8,128)(2,1)S(1)}, f16[160,256]{1,0:T(8,128)(2,1)S(1)}, u32[]{:S(2)}, u32[]{:S(2)}) %collective-permute-start.16) | collective-permute-done | bytes 81952 | tf_op jit(solution)/shard_map/ppermute | solution.py:386
  29.9 3.7 %collective-permute-start.1 = (bf16[464,256]{1,0:T(8,128)(2,1)S(1)}, bf16[464,256]{1,0:T(8,128)(2,1)S(1)}, u32[]{:S(2)}, u32[]{:S(2)}) collective-permute-start(bf16[464,256]{1,0:T(8,128)(2,1)S(1)} %broadcast_select_fusion.2), channel_id=1, source_target_pairs={{0,16},{1,17},{2,18},{3,19},{4,20},{5,21},{6,22},{7,23},{8,24},{9,... | collective-permute-start | bytes 712712 | tf_op jit(solution)/shard_map/ppermute | solution.py:386
  33.6 0.5 collective-permute-start.15
  34.4 1.3 %collective-permute-start.29 = (f16[624,256]{1,0:T(8,128)(2,1)S(1)}, f16[624,256]{1,0:T(8,128)(2,1)S(1)}, u32[]{:S(2)}, u32[]{:S(2)}) collective-permute-start(f16[624,256]{1,0:T(8,128)(2,1)S(1)} %broadcast_select_fusion), channel_id=1, source_target_pairs={{0,16},{1,17},{2,18},{3,19},{4,20},{5,21},{6,22},{7,23},{8,24},{9,... | collective-permute-start | bytes 958472 | tf_op jit(solution)/shard_map/ppermute | solution.py:386
  36.0 0.6 shard_map.79
  36.6 3.7 %collective-permute-start.20 = (bf16[80,128]{1,0:T(8,128)(2,1)S(1)}, bf16[80,128]{1,0:T(8,128)(2,1)S(1)}, u32[]{:S(2)}, u32[]{:S(2)}) collective-permute-start(bf16[80,128]{1,0:T(8,128)(2,1)S(1)} %shard_map.79), channel_id=1, source_target_pairs={{0,24},{1,25},{2,26},{3,27},{4,28},{5,29},{6,30},{7,31},{8,16},{9,... | collective-permute-start | bytes 61448 | tf_op jit(solution)/shard_map/ppermute | solution.py:386
  40.3 0.8 collective-permute-start.19
  41.1 11.1 %collective-permute-done.1 = bf16[464,256]{1,0:T(8,128)(2,1)S(1)} collective-permute-done((bf16[464,256]{1,0:T(8,128)(2,1)S(1)}, bf16[464,256]{1,0:T(8,128)(2,1)S(1)}, u32[]{:S(2)}, u32[]{:S(2)}) %collective-permute-start.1) | collective-permute-done | bytes 237600 | tf_op jit(solution)/shard_map/ppermute | solution.py:386
  52.3 2.3 %collective-permute-start.7 = (bf16[464,256]{1,0:T(8,128)(2,1)S(1)}, bf16[464,256]{1,0:T(8,128)(2,1)S(1)}, u32[]{:S(2)}, u32[]{:S(2)}) collective-permute-start(bf16[464,256]{1,0:T(8,128)(2,1)S(1)} %broadcast_select_fusion.3.refs_0_), channel_id=1, source_target_pairs={{0,6},{1,7},{2,4},{3,5},{4,2},{5,3},{6,0},{7,1},{8,14},{9,15},{10,... | collective-permute-start | bytes 712712 | tf_op jit(solution)/shard_map/ppermute | solution.py:386
  54.6 0.5 collective-permute-start.5
  55.1 0.2 localize.1.local_ref
  55.3 2.9 %collective-permute-done.19 = bf16[80,128]{1,0:T(8,128)(2,1)S(1)} collective-permute-done((bf16[80,128]{1,0:T(8,128)(2,1)S(1)}, bf16[80,128]{1,0:T(8,128)(2,1)S(1)}, u32[]{:S(2)}, u32[]{:S(2)}) %collective-permute-start.19) | collective-permute-done | bytes 20512 | tf_op jit(solution)/shard_map/ppermute | solution.py:386
  58.2 2.4 %collective-permute-start.26 = (bf16[320,128]{1,0:T(8,128)(2,1)S(1)}, bf16[320,128]{1,0:T(8,128)(2,1)S(1)}, u32[]{:S(2)}, u32[]{:S(2)}) collective-permute-start(bf16[320,128]{1,0:T(8,128)(2,1)S(1)} %pad_maximum_fusion.1.refs_2_.refs_0_), channel_id=1, source_target_pairs={{0,6},{1,7},{2,4},{3,5},{4,2},{5,3},{6,0},{7,1},{8,14},{9,15},{10,... | collective-permute-start | bytes 245768 | tf_op jit(solution)/shard_map/ppermute | solution.py:386
  60.7 0.6 collective-permute-start.24
  61.2 2.5 %collective-permute-done.26.refs_8_.refs_6_ = bf16[320,128]{1,0:T(8,128)(2,1)S(1)} collective-permute-done((bf16[320,128]{1,0:T(8,128)(2,1)S(1)}, bf16[320,128]{1,0:T(8,128)(2,1)S(1)}, u32[]{:S(2)}, u32[]{:S(2)}) %collective-permute-start.26) | collective-permute-done | bytes 81952 | tf_op jit(solution)/shard_map/ppermute | solution.py:386
  63.7 1.4 %collective-permute-start.3 = (bf16[464,256]{1,0:T(8,128)(2,1)S(1)}, bf16[464,256]{1,0:T(8,128)(2,1)S(1)}, u32[]{:S(2)}, u32[]{:S(2)}) collective-permute-start(bf16[464,256]{1,0:T(8,128)(2,1)S(1)} %broadcast_select_fusion.3.refs_0_), channel_id=1, source_target_pairs={{0,2},{1,3},{2,0},{3,1},{4,6},{5,7},{6,4},{7,5},{8,10},{9,11},{10,... | collective-permute-start | bytes 712712 | tf_op jit(solution)/shard_map/ppermute | solution.py:386
  65.2 0.5 collective-permute-start.8
  65.8 0.9 collective-permute-start.22
  66.7 4.0 %collective-permute-done.3.refs_2_ = bf16[464,256]{1,0:T(8,128)(2,1)S(1)} collective-permute-done((bf16[464,256]{1,0:T(8,128)(2,1)S(1)}, bf16[464,256]{1,0:T(8,128)(2,1)S(1)}, u32[]{:S(2)}, u32[]{:S(2)}) %collective-permute-start.3) | collective-permute-done | bytes 237600 | tf_op jit(solution)/shard_map/ppermute | solution.py:386
  70.8 0.8 collective-permute-done.22.refs_4_.refs_2_
  71.6 0.5 collective-permute-start.27
  72.2 0.4 collective-permute-start.23
  72.7 2.4 %collective-permute-start.35 = (bf16[464,256]{1,0:T(8,128)(2,1)S(1)}, bf16[464,256]{1,0:T(8,128)(2,1)S(1)}, u32[]{:S(2)}, u32[]{:S(2)}) collective-permute-start(bf16[464,256]{1,0:T(8,128)(2,1)S(1)} %slice_convert_fusion.refs_0_.second_ref), channel_id=1, source_target_pairs={{0,6},{1,7},{2,4},{3,5},{4,2},{5,3},{6,0},{7,1},{8,14},{9,15},{10,... | collective-permute-start | bytes 712712 | tf_op jit(solution)/shard_map/ppermute | solution.py:386
  75.1 1.4 %meeting_kernel.1.kernel_ref = bf16[2048,256]{1,0:T(8,128)(2,1)S(1)} custom-call(s32[2]{0:T(128)S(1)} %copy-done.8, s32[2,256]{1,0:T(2,128)S(1)} %copy-done.7, bf16[464,256]{1,0:T(8,128)(2,1)S(1)} %slice_convert_fusion.refs_0_.second_ref, bf16[464,256]{1,0:T(8,128)(2,1)S(1)} %broadcast_select_fusion.3.refs_0_, ...), custom_call_target="tpu_custom_call" | custom-call | flops 486539264 | bytes 1000000 | tf_op jit(solution)/shard_map/meeting_kernel/pallas_call | solution.py:234
  76.5 0.6 collective-permute-start.33
  77.1 0.6 collective-permute-start.31
  77.7 0.7 advance.1
  78.4 1.5 %collective-permute-start.38 = (f16[160,256]{1,0:T(8,128)(2,1)S(1)}, f16[160,256]{1,0:T(8,128)(2,1)S(1)}, u32[]{:S(2)}, u32[]{:S(2)}) collective-permute-start(f16[160,256]{1,0:T(8,128)(2,1)S(1)} %get-tuple-element.31), channel_id=1, source_target_pairs={{0,2},{1,3},{2,0},{3,1},{4,6},{5,7},{6,4},{7,5},{8,10},{9,11},{10,... | collective-permute-start | bytes 245768 | tf_op jit(solution)/shard_map/ppermute | solution.py:386
  79.9 2.4 %shard_map.78.refs_1_ = bf16[1024,2048]{1,0:T(8,128)(2,1)S(1)} custom-call(bf16[464,2048]{1,0:T(8,128)(2,1)S(1)} %localize.1.local_ref, bf16[464,256]{1,0:T(8,128)(2,1)S(1)} %collective-permute-done.5.refs_0_.refs_4_, bf16[464,256]{1,0:T(8,128)(2,1)S(1)} %collective-permute-done.6.refs_1_.refs_5_, ...), custom_call_target="tpu_custom_call" | custom-call | flops 1946157056 | bytes 10000000 | tf_op jit(solution)/shard_map/pallas_call | solution.py:283
  82.3 5.9 %collective-permute-done.38 = f16[160,256]{1,0:T(8,128)(2,1)S(1)} collective-permute-done((f16[160,256]{1,0:T(8,128)(2,1)S(1)}, f16[160,256]{1,0:T(8,128)(2,1)S(1)}, u32[]{:S(2)}, u32[]{:S(2)}) %collective-permute-start.38) | collective-permute-done | bytes 81952 | tf_op jit(solution)/shard_map/ppermute | solution.py:386
  88.2 0.6 collective-permute-start.40
  88.9 3.8 %collective-permute-done.40 = f16[160,256]{1,0:T(8,128)(2,1)S(1)} collective-permute-done((f16[160,256]{1,0:T(8,128)(2,1)S(1)}, f16[160,256]{1,0:T(8,128)(2,1)S(1)}, u32[]{:S(2)}, u32[]{:S(2)}) %collective-permute-start.40) | collective-permute-done | bytes 81952 | tf_op jit(solution)/shard_map/ppermute | solution.py:386
  92.7 1.4 %collective-permute-start.42 = (f16[160,256]{1,0:T(8,128)(2,1)S(1)}, f16[160,256]{1,0:T(8,128)(2,1)S(1)}, u32[]{:S(2)}, u32[]{:S(2)}) collective-permute-start(f16[160,256]{1,0:T(8,128)(2,1)S(1)} %get-tuple-element.31), channel_id=1, source_target_pairs={{0,6},{1,7},{2,4},{3,5},{4,2},{5,3},{6,0},{7,1},{8,14},{9,15},{10,... | collective-permute-start | bytes 245768 | tf_op jit(solution)/shard_map/ppermute | solution.py:386
  94.2 0.6 collective-permute-start.30
  94.8 3.3 %collective-permute-done.42 = f16[160,256]{1,0:T(8,128)(2,1)S(1)} collective-permute-done((f16[160,256]{1,0:T(8,128)(2,1)S(1)}, f16[160,256]{1,0:T(8,128)(2,1)S(1)}, u32[]{:S(2)}, u32[]{:S(2)}) %collective-permute-start.42) | collective-permute-done | bytes 81952 | tf_op jit(solution)/shard_map/ppermute | solution.py:386
  98.0 0.5 collective-permute-start.43
  98.6 1.1 collective-permute-done.43
  99.8 0.7 shard_map.82
  100.4 4.2 %collective-permute-start.46 = (bf16[80,128]{1,0:T(8,128)(2,1)S(1)}, bf16[80,128]{1,0:T(8,128)(2,1)S(1)}, u32[]{:S(2)}, u32[]{:S(2)}) collective-permute-start(bf16[80,128]{1,0:T(8,128)(2,1)S(1)} %shard_map.82), channel_id=1, source_target_pairs={{0,24},{1,25},{2,26},{3,27},{4,28},{5,29},{6,30},{7,31},{8,16},{9,... | collective-permute-start | bytes 61448 | tf_op jit(solution)/shard_map/ppermute | solution.py:386
  104.7 0.4 collective-permute-start.45
  105.1 0.5 collective-permute-start.44
  105.6 2.6 %shard_map.77.refs_0_ = bf16[1024,2048]{1,0:T(8,128)(2,1)S(1)} custom-call(bf16[464,2048]{1,0:T(8,128)(2,1)S(1)} %localize.1.local_ref, bf16[464,256]{1,0:T(8,128)(2,1)S(1)} %broadcast_select_fusion.3.refs_0_, bf16[464,256]{1,0:T(8,128)(2,1)S(1)} %collective-permute-done.2.refs_1_, bf16[464,256]{1,0:T(8,128)(2,1)S(1)} %collective-permute-done.3.refs_2_, ...), custom_call_target="tpu_custom_call" | custom-call | flops 1946157056 | bytes 10000000 | tf_op jit(solution)/shard_map/pallas_call | solution.py:283
  108.3 1.0 collective-permute-done.45
  109.4 1.5 %collective-permute-start.52 = (bf16[320,128]{1,0:T(8,128)(2,1)S(1)}, bf16[320,128]{1,0:T(8,128)(2,1)S(1)}, u32[]{:S(2)}, u32[]{:S(2)}) collective-permute-start(bf16[320,128]{1,0:T(8,128)(2,1)S(1)} %pad_maximum_fusion.2.refs_1_), channel_id=1, source_target_pairs={{0,6},{1,7},{2,4},{3,5},{4,2},{5,3},{6,0},{7,1},{8,14},{9,15},{10,... | collective-permute-start | bytes 245768 | tf_op jit(solution)/shard_map/ppermute | solution.py:386
  110.9 1.3 %collective-permute-start.50 = (bf16[320,128]{1,0:T(8,128)(2,1)S(1)}, bf16[320,128]{1,0:T(8,128)(2,1)S(1)}, u32[]{:S(2)}, u32[]{:S(2)}) collective-permute-start(bf16[320,128]{1,0:T(8,128)(2,1)S(1)} %pad_maximum_fusion.2.refs_1_), channel_id=1, source_target_pairs={{0,4},{1,5},{2,6},{3,7},{4,0},{5,1},{6,2},{7,3},{8,12},{9,13},{10,... | collective-permute-start | bytes 245768 | tf_op jit(solution)/shard_map/ppermute | solution.py:386
  112.2 0.7 collective-permute-start.48
  113.0 3.1 %shard_map.80 = (f32[147,2048]{1,0:T(8,128)S(1)}, f32[147,2048]{1,0:T(8,128)S(1)}) custom-call(s32[2]{0:T(128)S(1)} %copy-done.8, s32[2,256]{1,0:T(2,128)S(1)} %copy-done.7, f32[147,2048]{1,0:T(8,128)S(1)} %bitcast.8, f32[147,2048]{1,0:T(8,128)S(1)} %bitcast.9, bf16[1024,2048]{1,0:T(8,128)(2,1)S(1)} %shard_map.77.refs_0_, ...), custom_call_target="tpu_custom_call" | custom-call | flops 1342177280 | bytes 8388608 | tf_op jit(solution)/shard_map/pallas_call | solution.py:352
  116.2 0.5 collective-permute-start.53
  116.7 0.3 collective-permute-done.50.refs_5_
  117.0 0.5 collective-permute-start.49
  117.5 4.6 %shard_map.81.refs_0_ = bf16[2048,2048]{1,0:T(8,128)(2,1)S(1)} custom-call(bf16[464,2048]{1,0:T(8,128)(2,1)S(1)} %localize.1.local_ref, bf16[464,256]{1,0:T(8,128)(2,1)S(1)} %slice_convert_fusion.refs_0_.second_ref, bf16[464,256]{1,0:T(8,128)(2,1)S(1)} %collective-permute-done.30.refs_1_, bf16[464,256]{1,0:T(8,128)(2,1)S(1)} %collective-permute-done.31.refs_2_, ...), custom_call_target="tpu_custom_call" | custom-call | flops 3892314112 | bytes 10000000 | tf_op jit(solution)/shard_map/pallas_call | solution.py:283
  122.2 4.0 %shard_map.83 = (f32[147,2048]{1,0:T(8,128)}, f32[147,2048]{1,0:T(8,128)}) custom-call(s32[2]{0:T(128)S(1)} %copy-done.8, s32[2,256]{1,0:T(2,128)S(1)} %copy-done.7, f32[147,2048]{1,0:T(8,128)S(1)} %get-tuple-element.21.residual_ref, f32[147,2048]{1,0:T(8,128)S(1)} %get-tuple-element.22.coeffs_ref, bf16[2048,2048]{1,0:T(8,128)(2,1)S(1)} %shard_map.81.refs_0_, ...), custom_call_target="tpu_custom_call" | custom-call | flops 1342177280 | bytes 8388608 | tf_op jit(solution)/shard_map/pallas_call | solution.py:352
  (110 shorter events, 1.9 us)
Async XLA Ops:
  0.6 6.4 %copy-start.8 = (s32[2]{0:T(128)S(1)}, s32[2]{0:T(128)}, u32[]{:S(2)}) copy-start(s32[2]{0:T(128)} %owners_ref.7) | copy-start | bytes 28
  0.6 1.3 %copy-start.2 = (f32[2048,147]{0,1:T(8,128)S(1)}, f32[2048,147]{0,1:T(8,128)}, u32[]{:S(2)}) copy-start(f32[2048,147]{0,1:T(8,128)} %param.7) | copy-start | bytes 3612676
  1.9 0.7 copy-start.6
  2.6 4.4 %copy-start.7 = (s32[2,256]{1,0:T(2,128)S(1)}, s32[2,256]{1,0:T(2,128)}, u32[]{:S(2)}) copy-start(s32[2,256]{1,0:T(2,128)} %index_ref.7) | copy-start | bytes 6148
  3.9 8.7 %collective-permute-start.9 = (f16[160,256]{1,0:T(8,128)(2,1)S(1)}, f16[160,256]{1,0:T(8,128)(2,1)S(1)}, u32[]{:S(2)}, u32[]{:S(2)}) collective-permute-start(f16[160,256]{1,0:T(8,128)(2,1)S(1)} %convert_element_type.24), channel_id=1, source_target_pairs={{0,8},{1,9},{2,10},{3,11},{4,12},{5,13},{6,14},{7,15},{8,0},{9,1},... | collective-permute-start | bytes 245768 | tf_op jit(solution)/shard_map/ppermute | solution.py:386
  7.0 1.5 %copy-start = (bf16[2048,440]{0,1:T(8,128)(2,1)S(1)}, bf16[2048,440]{0,1:T(8,128)(2,1)}, u32[]{:S(2)}) copy-start(bf16[2048,440]{0,1:T(8,128)(2,1)} %param.6) | copy-start | bytes 5406724
  8.5 6.8 %copy-start.5 = (f32[2,64,2048]{2,1,0:T(8,128)S(1)}, f32[2,64,2048]{2,1,0:T(8,128)}, u32[]{:S(2)}) copy-start(f32[2,64,2048]{2,1,0:T(8,128)} %inverse_ref.1) | copy-start | bytes 3145732
  10.2 17.3 %collective-permute-start = (bf16[464,256]{1,0:T(8,128)(2,1)S(1)}, bf16[464,256]{1,0:T(8,128)(2,1)S(1)}, u32[]{:S(2)}, u32[]{:S(2)}) collective-permute-start(bf16[464,256]{1,0:T(8,128)(2,1)S(1)} %get-tuple-element.18), channel_id=1, source_target_pairs={{0,8},{1,9},{2,10},{3,11},{4,12},{5,13},{6,14},{7,15},{8,0},{9,1},... | collective-permute-start | bytes 712712 | tf_op jit(solution)/shard_map/ppermute | solution.py:386
  10.4 23.8 %collective-permute-start.28 = (f16[624,256]{1,0:T(8,128)(2,1)S(1)}, f16[624,256]{1,0:T(8,128)(2,1)S(1)}, u32[]{:S(2)}, u32[]{:S(2)}) collective-permute-start(f16[624,256]{1,0:T(8,128)(2,1)S(1)} %pad_maximum_fusion), channel_id=1, source_target_pairs={{0,8},{1,9},{2,10},{3,11},{4,12},{5,13},{6,14},{7,15},{8,0},{9,1},... | collective-permute-start | bytes 958472 | tf_op jit(solution)/shard_map/ppermute | solution.py:386
  12.6 11.3 %collective-permute-start.10 = (f16[160,256]{1,0:T(8,128)(2,1)S(1)}, f16[160,256]{1,0:T(8,128)(2,1)S(1)}, u32[]{:S(2)}, u32[]{:S(2)}) collective-permute-start(f16[160,256]{1,0:T(8,128)(2,1)S(1)} %broadcast_select_fusion.4), channel_id=1, source_target_pairs={{0,16},{1,17},{2,18},{3,19},{4,20},{5,21},{6,22},{7,23},{8,24},{9,... | collective-permute-start | bytes 245768 | tf_op jit(solution)/shard_map/ppermute | solution.py:386
  24.0 6.0 %collective-permute-start.16 = (f16[160,256]{1,0:T(8,128)(2,1)S(1)}, f16[160,256]{1,0:T(8,128)(2,1)S(1)}, u32[]{:S(2)}, u32[]{:S(2)}) collective-permute-start(f16[160,256]{1,0:T(8,128)(2,1)S(1)} %get-tuple-element.33), channel_id=1, source_target_pairs={{0,6},{1,7},{2,4},{3,5},{4,2},{5,3},{6,0},{7,1},{8,14},{9,15},{10,... | collective-permute-start | bytes 245768 | tf_op jit(solution)/shard_map/ppermute | solution.py:386
  26.6 7.0 %collective-permute-start.14 = (f16[160,256]{1,0:T(8,128)(2,1)S(1)}, f16[160,256]{1,0:T(8,128)(2,1)S(1)}, u32[]{:S(2)}, u32[]{:S(2)}) collective-permute-start(f16[160,256]{1,0:T(8,128)(2,1)S(1)} %get-tuple-element.33), channel_id=1, source_target_pairs={{0,4},{1,5},{2,6},{3,7},{4,0},{5,1},{6,2},{7,3},{8,12},{9,13},{10,... | collective-permute-start | bytes 245768 | tf_op jit(solution)/shard_map/ppermute | solution.py:386
  27.1 6.5 %collective-permute-start.12 = (f16[160,256]{1,0:T(8,128)(2,1)S(1)}, f16[160,256]{1,0:T(8,128)(2,1)S(1)}, u32[]{:S(2)}, u32[]{:S(2)}) collective-permute-start(f16[160,256]{1,0:T(8,128)(2,1)S(1)} %get-tuple-element.33), channel_id=1, source_target_pairs={{0,2},{1,3},{2,0},{3,1},{4,6},{5,7},{6,4},{7,5},{8,10},{9,11},{10,... | collective-permute-start | bytes 245768 | tf_op jit(solution)/shard_map/ppermute | solution.py:386
  27.5 6.6 %collective-permute-start.11 = (f16[160,256]{1,0:T(8,128)(2,1)S(1)}, f16[160,256]{1,0:T(8,128)(2,1)S(1)}, u32[]{:S(2)}, u32[]{:S(2)}) collective-permute-start(f16[160,256]{1,0:T(8,128)(2,1)S(1)} %get-tuple-element.33), channel_id=1, source_target_pairs={{0,1},{1,0},{2,3},{3,2},{4,5},{5,4},{6,7},{7,6},{8,9},{9,8},{10,11... | collective-permute-start | bytes 245768 | tf_op jit(solution)/shard_map/ppermute | solution.py:386
  29.9 22.3 %collective-permute-start.1 = (bf16[464,256]{1,0:T(8,128)(2,1)S(1)}, bf16[464,256]{1,0:T(8,128)(2,1)S(1)}, u32[]{:S(2)}, u32[]{:S(2)}) collective-permute-start(bf16[464,256]{1,0:T(8,128)(2,1)S(1)} %broadcast_select_fusion.2), channel_id=1, source_target_pairs={{0,16},{1,17},{2,18},{3,19},{4,20},{5,21},{6,22},{7,23},{8,24},{9,... | collective-permute-start | bytes 712712 | tf_op jit(solution)/shard_map/ppermute | solution.py:386
  33.6 2.2 %collective-permute-start.17 = (f16[160,256]{1,0:T(8,128)(2,1)S(1)}, f16[160,256]{1,0:T(8,128)(2,1)S(1)}, u32[]{:S(2)}, u32[]{:S(2)}) collective-permute-start(f16[160,256]{1,0:T(8,128)(2,1)S(1)} %collective-permute-done.16), channel_id=1, source_target_pairs={{0,1},{1,0},{2,3},{3,2},{4,5},{5,4},{6,7},{7,6},{8,9},{9,8},{10,11... | collective-permute-start | bytes 245768 | tf_op jit(solution)/shard_map/ppermute | solution.py:386
  33.6 2.2 %collective-permute-start.15 = (f16[160,256]{1,0:T(8,128)(2,1)S(1)}, f16[160,256]{1,0:T(8,128)(2,1)S(1)}, u32[]{:S(2)}, u32[]{:S(2)}) collective-permute-start(f16[160,256]{1,0:T(8,128)(2,1)S(1)} %collective-permute-done.14), channel_id=1, source_target_pairs={{0,1},{1,0},{2,3},{3,2},{4,5},{5,4},{6,7},{7,6},{8,9},{9,8},{10,11... | collective-permute-start | bytes 245768 | tf_op jit(solution)/shard_map/ppermute | solution.py:386
  34.1 1.6 %collective-permute-start.13 = (f16[160,256]{1,0:T(8,128)(2,1)S(1)}, f16[160,256]{1,0:T(8,128)(2,1)S(1)}, u32[]{:S(2)}, u32[]{:S(2)}) collective-permute-start(f16[160,256]{1,0:T(8,128)(2,1)S(1)} %collective-permute-done.12), channel_id=1, source_target_pairs={{0,1},{1,0},{2,3},{3,2},{4,5},{5,4},{6,7},{7,6},{8,9},{9,8},{10,11... | collective-permute-start | bytes 245768 | tf_op jit(solution)/shard_map/ppermute | solution.py:386
  34.4 30.8 %collective-permute-start.29 = (f16[624,256]{1,0:T(8,128)(2,1)S(1)}, f16[624,256]{1,0:T(8,128)(2,1)S(1)}, u32[]{:S(2)}, u32[]{:S(2)}) collective-permute-start(f16[624,256]{1,0:T(8,128)(2,1)S(1)} %broadcast_select_fusion), channel_id=1, source_target_pairs={{0,16},{1,17},{2,18},{3,19},{4,20},{5,21},{6,22},{7,23},{8,24},{9,... | collective-permute-start | bytes 958472 | tf_op jit(solution)/shard_map/ppermute | solution.py:386
  36.0 19.2 %copy-start.1 = (bf16[2048,440]{0,1:T(8,128)(2,1)S(1)}, bf16[2048,440]{0,1:T(8,128)(2,1)}, u32[]{:S(2)}) copy-start(bf16[2048,440]{0,1:T(8,128)(2,1)} %param.6) | copy-start | bytes 5406724
  36.6 18.0 %collective-permute-start.20 = (bf16[80,128]{1,0:T(8,128)(2,1)S(1)}, bf16[80,128]{1,0:T(8,128)(2,1)S(1)}, u32[]{:S(2)}, u32[]{:S(2)}) collective-permute-start(bf16[80,128]{1,0:T(8,128)(2,1)S(1)} %shard_map.79), channel_id=1, source_target_pairs={{0,24},{1,25},{2,26},{3,27},{4,28},{5,29},{6,30},{7,31},{8,16},{9,... | collective-permute-start | bytes 61448 | tf_op jit(solution)/shard_map/ppermute | solution.py:386
  40.3 17.9 %collective-permute-start.19 = (bf16[80,128]{1,0:T(8,128)(2,1)S(1)}, bf16[80,128]{1,0:T(8,128)(2,1)S(1)}, u32[]{:S(2)}, u32[]{:S(2)}) collective-permute-start(bf16[80,128]{1,0:T(8,128)(2,1)S(1)} %shard_map.79), channel_id=1, source_target_pairs={{0,16},{1,17},{2,18},{3,19},{4,20},{5,21},{6,22},{7,23},{8,24},{9,... | collective-permute-start | bytes 61448 | tf_op jit(solution)/shard_map/ppermute | solution.py:386
  41.1 17.1 %collective-permute-start.18 = (bf16[80,128]{1,0:T(8,128)(2,1)S(1)}, bf16[80,128]{1,0:T(8,128)(2,1)S(1)}, u32[]{:S(2)}, u32[]{:S(2)}) collective-permute-start(bf16[80,128]{1,0:T(8,128)(2,1)S(1)} %shard_map.79), channel_id=1, source_target_pairs={{0,8},{1,9},{2,10},{3,11},{4,12},{5,13},{6,14},{7,15},{8,0},{9,1},... | collective-permute-start | bytes 61448 | tf_op jit(solution)/shard_map/ppermute | solution.py:386
  52.3 12.9 %collective-permute-start.7 = (bf16[464,256]{1,0:T(8,128)(2,1)S(1)}, bf16[464,256]{1,0:T(8,128)(2,1)S(1)}, u32[]{:S(2)}, u32[]{:S(2)}) collective-permute-start(bf16[464,256]{1,0:T(8,128)(2,1)S(1)} %broadcast_select_fusion.3.refs_0_), channel_id=1, source_target_pairs={{0,6},{1,7},{2,4},{3,5},{4,2},{5,3},{6,0},{7,1},{8,14},{9,15},{10,... | collective-permute-start | bytes 712712 | tf_op jit(solution)/shard_map/ppermute | solution.py:386
  54.6 11.0 %collective-permute-start.5 = (bf16[464,256]{1,0:T(8,128)(2,1)S(1)}, bf16[464,256]{1,0:T(8,128)(2,1)S(1)}, u32[]{:S(2)}, u32[]{:S(2)}) collective-permute-start(bf16[464,256]{1,0:T(8,128)(2,1)S(1)} %broadcast_select_fusion.3.refs_0_), channel_id=1, source_target_pairs={{0,4},{1,5},{2,6},{3,7},{4,0},{5,1},{6,2},{7,3},{8,12},{9,13},{10,... | collective-permute-start | bytes 712712 | tf_op jit(solution)/shard_map/ppermute | solution.py:386
  58.2 5.5 %collective-permute-start.26 = (bf16[320,128]{1,0:T(8,128)(2,1)S(1)}, bf16[320,128]{1,0:T(8,128)(2,1)S(1)}, u32[]{:S(2)}, u32[]{:S(2)}) collective-permute-start(bf16[320,128]{1,0:T(8,128)(2,1)S(1)} %pad_maximum_fusion.1.refs_2_.refs_0_), channel_id=1, source_target_pairs={{0,6},{1,7},{2,4},{3,5},{4,2},{5,3},{6,0},{7,1},{8,14},{9,15},{10,... | collective-permute-start | bytes 245768 | tf_op jit(solution)/shard_map/ppermute | solution.py:386
  60.7 5.2 %collective-permute-start.24 = (bf16[320,128]{1,0:T(8,128)(2,1)S(1)}, bf16[320,128]{1,0:T(8,128)(2,1)S(1)}, u32[]{:S(2)}, u32[]{:S(2)}) collective-permute-start(bf16[320,128]{1,0:T(8,128)(2,1)S(1)} %pad_maximum_fusion.1.refs_2_.refs_0_), channel_id=1, source_target_pairs={{0,4},{1,5},{2,6},{3,7},{4,0},{5,1},{6,2},{7,3},{8,12},{9,13},{10,... | collective-permute-start | bytes 245768 | tf_op jit(solution)/shard_map/ppermute | solution.py:386
  63.7 7.0 %collective-permute-start.3 = (bf16[464,256]{1,0:T(8,128)(2,1)S(1)}, bf16[464,256]{1,0:T(8,128)(2,1)S(1)}, u32[]{:S(2)}, u32[]{:S(2)}) collective-permute-start(bf16[464,256]{1,0:T(8,128)(2,1)S(1)} %broadcast_select_fusion.3.refs_0_), channel_id=1, source_target_pairs={{0,2},{1,3},{2,0},{3,1},{4,6},{5,7},{6,4},{7,5},{8,10},{9,11},{10,... | collective-permute-start | bytes 712712 | tf_op jit(solution)/shard_map/ppermute | solution.py:386
  65.2 6.5 %collective-permute-start.2 = (bf16[464,256]{1,0:T(8,128)(2,1)S(1)}, bf16[464,256]{1,0:T(8,128)(2,1)S(1)}, u32[]{:S(2)}, u32[]{:S(2)}) collective-permute-start(bf16[464,256]{1,0:T(8,128)(2,1)S(1)} %broadcast_select_fusion.3.refs_0_), channel_id=1, source_target_pairs={{0,1},{1,0},{2,3},{3,2},{4,5},{5,4},{6,7},{7,6},{8,9},{9,8},{10,11... | collective-permute-start | bytes 712712 | tf_op jit(solution)/shard_map/ppermute | solution.py:386
  65.2 7.0 %collective-permute-start.8 = (bf16[464,256]{1,0:T(8,128)(2,1)S(1)}, bf16[464,256]{1,0:T(8,128)(2,1)S(1)}, u32[]{:S(2)}, u32[]{:S(2)}) collective-permute-start(bf16[464,256]{1,0:T(8,128)(2,1)S(1)} %collective-permute-done.7.refs_2_.refs_6_), channel_id=1, source_target_pairs={{0,1},{1,0},{2,3},{3,2},{4,5},{5,4},{6,7},{7,6},{8,9},{9,8},{10,11... | collective-permute-start | bytes 712712 | tf_op jit(solution)/shard_map/ppermute | solution.py:386
  65.7 6.5 %collective-permute-start.6 = (bf16[464,256]{1,0:T(8,128)(2,1)S(1)}, bf16[464,256]{1,0:T(8,128)(2,1)S(1)}, u32[]{:S(2)}, u32[]{:S(2)}) collective-permute-start(bf16[464,256]{1,0:T(8,128)(2,1)S(1)} %collective-permute-done.5.refs_0_.refs_4_), channel_id=1, source_target_pairs={{0,1},{1,0},{2,3},{3,2},{4,5},{5,4},{6,7},{7,6},{8,9},{9,8},{10,11... | collective-permute-start | bytes 712712 | tf_op jit(solution)/shard_map/ppermute | solution.py:386
  65.8 5.8 %collective-permute-start.22 = (bf16[320,128]{1,0:T(8,128)(2,1)S(1)}, bf16[320,128]{1,0:T(8,128)(2,1)S(1)}, u32[]{:S(2)}, u32[]{:S(2)}) collective-permute-start(bf16[320,128]{1,0:T(8,128)(2,1)S(1)} %pad_maximum_fusion.1.refs_2_.refs_0_), channel_id=1, source_target_pairs={{0,2},{1,3},{2,0},{3,1},{4,6},{5,7},{6,4},{7,5},{8,10},{9,11},{10,... | collective-permute-start | bytes 245768 | tf_op jit(solution)/shard_map/ppermute | solution.py:386
  70.7 1.9 %collective-permute-start.4 = (bf16[464,256]{1,0:T(8,128)(2,1)S(1)}, bf16[464,256]{1,0:T(8,128)(2,1)S(1)}, u32[]{:S(2)}, u32[]{:S(2)}) collective-permute-start(bf16[464,256]{1,0:T(8,128)(2,1)S(1)} %collective-permute-done.3.refs_2_), channel_id=1, source_target_pairs={{0,1},{1,0},{2,3},{3,2},{4,5},{5,4},{6,7},{7,6},{8,9},{9,8},{10,11... | collective-permute-start | bytes 712712 | tf_op jit(solution)/shard_map/ppermute | solution.py:386
  71.6 4.9 %collective-permute-start.21 = (bf16[320,128]{1,0:T(8,128)(2,1)S(1)}, bf16[320,128]{1,0:T(8,128)(2,1)S(1)}, u32[]{:S(2)}, u32[]{:S(2)}) collective-permute-start(bf16[320,128]{1,0:T(8,128)(2,1)S(1)} %pad_maximum_fusion.1.refs_2_.refs_0_), channel_id=1, source_target_pairs={{0,1},{1,0},{2,3},{3,2},{4,5},{5,4},{6,7},{7,6},{8,9},{9,8},{10,11... | collective-permute-start | bytes 245768 | tf_op jit(solution)/shard_map/ppermute | solution.py:386
  71.6 5.5 %collective-permute-start.27 = (bf16[320,128]{1,0:T(8,128)(2,1)S(1)}, bf16[320,128]{1,0:T(8,128)(2,1)S(1)}, u32[]{:S(2)}, u32[]{:S(2)}) collective-permute-start(bf16[320,128]{1,0:T(8,128)(2,1)S(1)} %collective-permute-done.26.refs_8_.refs_6_), channel_id=1, source_target_pairs={{0,1},{1,0},{2,3},{3,2},{4,5},{5,4},{6,7},{7,6},{8,9},{9,8},{10,11... | collective-permute-start | bytes 245768 | tf_op jit(solution)/shard_map/ppermute | solution.py:386
  72.1 5.6 %collective-permute-start.25 = (bf16[320,128]{1,0:T(8,128)(2,1)S(1)}, bf16[320,128]{1,0:T(8,128)(2,1)S(1)}, u32[]{:S(2)}, u32[]{:S(2)}) collective-permute-start(bf16[320,128]{1,0:T(8,128)(2,1)S(1)} %collective-permute-done.24.refs_6_.refs_4_), channel_id=1, source_target_pairs={{0,1},{1,0},{2,3},{3,2},{4,5},{5,4},{6,7},{7,6},{8,9},{9,8},{10,11... | collective-permute-start | bytes 245768 | tf_op jit(solution)/shard_map/ppermute | solution.py:386
  72.2 5.5 %collective-permute-start.23 = (bf16[320,128]{1,0:T(8,128)(2,1)S(1)}, bf16[320,128]{1,0:T(8,128)(2,1)S(1)}, u32[]{:S(2)}, u32[]{:S(2)}) collective-permute-start(bf16[320,128]{1,0:T(8,128)(2,1)S(1)} %collective-permute-done.22.refs_4_.refs_2_), channel_id=1, source_target_pairs={{0,1},{1,0},{2,3},{3,2},{4,5},{5,4},{6,7},{7,6},{8,9},{9,8},{10,11... | collective-permute-start | bytes 245768 | tf_op jit(solution)/shard_map/ppermute | solution.py:386
  72.7 21.5 %collective-permute-start.35 = (bf16[464,256]{1,0:T(8,128)(2,1)S(1)}, bf16[464,256]{1,0:T(8,128)(2,1)S(1)}, u32[]{:S(2)}, u32[]{:S(2)}) collective-permute-start(bf16[464,256]{1,0:T(8,128)(2,1)S(1)} %slice_convert_fusion.refs_0_.second_ref), channel_id=1, source_target_pairs={{0,6},{1,7},{2,4},{3,5},{4,2},{5,3},{6,0},{7,1},{8,14},{9,15},{10,... | collective-permute-start | bytes 712712 | tf_op jit(solution)/shard_map/ppermute | solution.py:386
  76.5 28.2 %collective-permute-start.33 = (bf16[464,256]{1,0:T(8,128)(2,1)S(1)}, bf16[464,256]{1,0:T(8,128)(2,1)S(1)}, u32[]{:S(2)}, u32[]{:S(2)}) collective-permute-start(bf16[464,256]{1,0:T(8,128)(2,1)S(1)} %slice_convert_fusion.refs_0_.second_ref), channel_id=1, source_target_pairs={{0,4},{1,5},{2,6},{3,7},{4,0},{5,1},{6,2},{7,3},{8,12},{9,13},{10,... | collective-permute-start | bytes 712712 | tf_op jit(solution)/shard_map/ppermute | solution.py:386
  77.1 28.0 %collective-permute-start.31 = (bf16[464,256]{1,0:T(8,128)(2,1)S(1)}, bf16[464,256]{1,0:T(8,128)(2,1)S(1)}, u32[]{:S(2)}, u32[]{:S(2)}) collective-permute-start(bf16[464,256]{1,0:T(8,128)(2,1)S(1)} %slice_convert_fusion.refs_0_.second_ref), channel_id=1, source_target_pairs={{0,2},{1,3},{2,0},{3,1},{4,6},{5,7},{6,4},{7,5},{8,10},{9,11},{10,... | collective-permute-start | bytes 712712 | tf_op jit(solution)/shard_map/ppermute | solution.py:386
  78.4 9.8 %collective-permute-start.38 = (f16[160,256]{1,0:T(8,128)(2,1)S(1)}, f16[160,256]{1,0:T(8,128)(2,1)S(1)}, u32[]{:S(2)}, u32[]{:S(2)}) collective-permute-start(f16[160,256]{1,0:T(8,128)(2,1)S(1)} %get-tuple-element.31), channel_id=1, source_target_pairs={{0,2},{1,3},{2,0},{3,1},{4,6},{5,7},{6,4},{7,5},{8,10},{9,11},{10,... | collective-permute-start | bytes 245768 | tf_op jit(solution)/shard_map/ppermute | solution.py:386
  79.9 8.9 %collective-permute-start.37 = (f16[160,256]{1,0:T(8,128)(2,1)S(1)}, f16[160,256]{1,0:T(8,128)(2,1)S(1)}, u32[]{:S(2)}, u32[]{:S(2)}) collective-permute-start(f16[160,256]{1,0:T(8,128)(2,1)S(1)} %get-tuple-element.31), channel_id=1, source_target_pairs={{0,1},{1,0},{2,3},{3,2},{4,5},{5,4},{6,7},{7,6},{8,9},{9,8},{10,11... | collective-permute-start | bytes 245768 | tf_op jit(solution)/shard_map/ppermute | solution.py:386
  88.2 4.4 %collective-permute-start.40 = (f16[160,256]{1,0:T(8,128)(2,1)S(1)}, f16[160,256]{1,0:T(8,128)(2,1)S(1)}, u32[]{:S(2)}, u32[]{:S(2)}) collective-permute-start(f16[160,256]{1,0:T(8,128)(2,1)S(1)} %get-tuple-element.31), channel_id=1, source_target_pairs={{0,4},{1,5},{2,6},{3,7},{4,0},{5,1},{6,2},{7,3},{8,12},{9,13},{10,... | collective-permute-start | bytes 245768 | tf_op jit(solution)/shard_map/ppermute | solution.py:386
  88.8 5.3 %collective-permute-start.39 = (f16[160,256]{1,0:T(8,128)(2,1)S(1)}, f16[160,256]{1,0:T(8,128)(2,1)S(1)}, u32[]{:S(2)}, u32[]{:S(2)}) collective-permute-start(f16[160,256]{1,0:T(8,128)(2,1)S(1)} %collective-permute-done.38), channel_id=1, source_target_pairs={{0,1},{1,0},{2,3},{3,2},{4,5},{5,4},{6,7},{7,6},{8,9},{9,8},{10,11... | collective-permute-start | bytes 245768 | tf_op jit(solution)/shard_map/ppermute | solution.py:386
  92.7 5.3 %collective-permute-start.42 = (f16[160,256]{1,0:T(8,128)(2,1)S(1)}, f16[160,256]{1,0:T(8,128)(2,1)S(1)}, u32[]{:S(2)}, u32[]{:S(2)}) collective-permute-start(f16[160,256]{1,0:T(8,128)(2,1)S(1)} %get-tuple-element.31), channel_id=1, source_target_pairs={{0,6},{1,7},{2,4},{3,5},{4,2},{5,3},{6,0},{7,1},{8,14},{9,15},{10,... | collective-permute-start | bytes 245768 | tf_op jit(solution)/shard_map/ppermute | solution.py:386
  94.1 3.9 %collective-permute-start.41 = (f16[160,256]{1,0:T(8,128)(2,1)S(1)}, f16[160,256]{1,0:T(8,128)(2,1)S(1)}, u32[]{:S(2)}, u32[]{:S(2)}) collective-permute-start(f16[160,256]{1,0:T(8,128)(2,1)S(1)} %collective-permute-done.40), channel_id=1, source_target_pairs={{0,1},{1,0},{2,3},{3,2},{4,5},{5,4},{6,7},{7,6},{8,9},{9,8},{10,11... | collective-permute-start | bytes 245768 | tf_op jit(solution)/shard_map/ppermute | solution.py:386
  94.2 16.7 %collective-permute-start.30 = (bf16[464,256]{1,0:T(8,128)(2,1)S(1)}, bf16[464,256]{1,0:T(8,128)(2,1)S(1)}, u32[]{:S(2)}, u32[]{:S(2)}) collective-permute-start(bf16[464,256]{1,0:T(8,128)(2,1)S(1)} %slice_convert_fusion.refs_0_.second_ref), channel_id=1, source_target_pairs={{0,1},{1,0},{2,3},{3,2},{4,5},{5,4},{6,7},{7,6},{8,9},{9,8},{10,11... | collective-permute-start | bytes 712712 | tf_op jit(solution)/shard_map/ppermute | solution.py:386
  98.0 14.2 %collective-permute-start.36 = (bf16[464,256]{1,0:T(8,128)(2,1)S(1)}, bf16[464,256]{1,0:T(8,128)(2,1)S(1)}, u32[]{:S(2)}, u32[]{:S(2)}) collective-permute-start(bf16[464,256]{1,0:T(8,128)(2,1)S(1)} %collective-permute-done.35.refs_6_), channel_id=1, source_target_pairs={{0,1},{1,0},{2,3},{3,2},{4,5},{5,4},{6,7},{7,6},{8,9},{9,8},{10,11... | collective-permute-start | bytes 712712 | tf_op jit(solution)/shard_map/ppermute | solution.py:386
  98.0 1.6 %collective-permute-start.43 = (f16[160,256]{1,0:T(8,128)(2,1)S(1)}, f16[160,256]{1,0:T(8,128)(2,1)S(1)}, u32[]{:S(2)}, u32[]{:S(2)}) collective-permute-start(f16[160,256]{1,0:T(8,128)(2,1)S(1)} %collective-permute-done.42), channel_id=1, source_target_pairs={{0,1},{1,0},{2,3},{3,2},{4,5},{5,4},{6,7},{7,6},{8,9},{9,8},{10,11... | collective-permute-start | bytes 245768 | tf_op jit(solution)/shard_map/ppermute | solution.py:386
  100.4 12.5 %copy-start.3 = (f32[2048,147]{0,1:T(8,128)S(1)}, f32[2048,147]{0,1:T(8,128)}, u32[]{:S(2)}) copy-start(f32[2048,147]{0,1:T(8,128)} %param.7) | copy-start | bytes 3612676
  100.4 12.5 %copy-start.4 = (f32[2048,147]{0,1:T(8,128)S(1)}, f32[2048,147]{0,1:T(8,128)}, u32[]{:S(2)}) copy-start(f32[2048,147]{0,1:T(8,128)} %param.8) | copy-start | bytes 3612676
  100.4 7.8 %collective-permute-start.46 = (bf16[80,128]{1,0:T(8,128)(2,1)S(1)}, bf16[80,128]{1,0:T(8,128)(2,1)S(1)}, u32[]{:S(2)}, u32[]{:S(2)}) collective-permute-start(bf16[80,128]{1,0:T(8,128)(2,1)S(1)} %shard_map.82), channel_id=1, source_target_pairs={{0,24},{1,25},{2,26},{3,27},{4,28},{5,29},{6,30},{7,31},{8,16},{9,... | collective-permute-start | bytes 61448 | tf_op jit(solution)/shard_map/ppermute | solution.py:386
  104.7 4.7 %collective-permute-start.45 = (bf16[80,128]{1,0:T(8,128)(2,1)S(1)}, bf16[80,128]{1,0:T(8,128)(2,1)S(1)}, u32[]{:S(2)}, u32[]{:S(2)}) collective-permute-start(bf16[80,128]{1,0:T(8,128)(2,1)S(1)} %shard_map.82), channel_id=1, source_target_pairs={{0,16},{1,17},{2,18},{3,19},{4,20},{5,21},{6,22},{7,23},{8,24},{9,... | collective-permute-start | bytes 61448 | tf_op jit(solution)/shard_map/ppermute | solution.py:386
  105.1 4.3 %collective-permute-start.44 = (bf16[80,128]{1,0:T(8,128)(2,1)S(1)}, bf16[80,128]{1,0:T(8,128)(2,1)S(1)}, u32[]{:S(2)}, u32[]{:S(2)}) collective-permute-start(bf16[80,128]{1,0:T(8,128)(2,1)S(1)} %shard_map.82), channel_id=1, source_target_pairs={{0,8},{1,9},{2,10},{3,11},{4,12},{5,13},{6,14},{7,15},{8,0},{9,1},... | collective-permute-start | bytes 61448 | tf_op jit(solution)/shard_map/ppermute | solution.py:386
  108.3 7.8 %collective-permute-start.34 = (bf16[464,256]{1,0:T(8,128)(2,1)S(1)}, bf16[464,256]{1,0:T(8,128)(2,1)S(1)}, u32[]{:S(2)}, u32[]{:S(2)}) collective-permute-start(bf16[464,256]{1,0:T(8,128)(2,1)S(1)} %collective-permute-done.33.refs_4_), channel_id=1, source_target_pairs={{0,1},{1,0},{2,3},{3,2},{4,5},{5,4},{6,7},{7,6},{8,9},{9,8},{10,11... | collective-permute-start | bytes 712712 | tf_op jit(solution)/shard_map/ppermute | solution.py:386
  109.4 8.1 %collective-permute-start.32 = (bf16[464,256]{1,0:T(8,128)(2,1)S(1)}, bf16[464,256]{1,0:T(8,128)(2,1)S(1)}, u32[]{:S(2)}, u32[]{:S(2)}) collective-permute-start(bf16[464,256]{1,0:T(8,128)(2,1)S(1)} %collective-permute-done.31.refs_2_), channel_id=1, source_target_pairs={{0,1},{1,0},{2,3},{3,2},{4,5},{5,4},{6,7},{7,6},{8,9},{9,8},{10,11... | collective-permute-start | bytes 712712 | tf_op jit(solution)/shard_map/ppermute | solution.py:386
  109.4 6.8 %collective-permute-start.52 = (bf16[320,128]{1,0:T(8,128)(2,1)S(1)}, bf16[320,128]{1,0:T(8,128)(2,1)S(1)}, u32[]{:S(2)}, u32[]{:S(2)}) collective-permute-start(bf16[320,128]{1,0:T(8,128)(2,1)S(1)} %pad_maximum_fusion.2.refs_1_), channel_id=1, source_target_pairs={{0,6},{1,7},{2,4},{3,5},{4,2},{5,3},{6,0},{7,1},{8,14},{9,15},{10,... | collective-permute-start | bytes 245768 | tf_op jit(solution)/shard_map/ppermute | solution.py:386
  110.9 6.1 %collective-permute-start.50 = (bf16[320,128]{1,0:T(8,128)(2,1)S(1)}, bf16[320,128]{1,0:T(8,128)(2,1)S(1)}, u32[]{:S(2)}, u32[]{:S(2)}) collective-permute-start(bf16[320,128]{1,0:T(8,128)(2,1)S(1)} %pad_maximum_fusion.2.refs_1_), channel_id=1, source_target_pairs={{0,4},{1,5},{2,6},{3,7},{4,0},{5,1},{6,2},{7,3},{8,12},{9,13},{10,... | collective-permute-start | bytes 245768 | tf_op jit(solution)/shard_map/ppermute | solution.py:386
  112.2 4.8 %collective-permute-start.48 = (bf16[320,128]{1,0:T(8,128)(2,1)S(1)}, bf16[320,128]{1,0:T(8,128)(2,1)S(1)}, u32[]{:S(2)}, u32[]{:S(2)}) collective-permute-start(bf16[320,128]{1,0:T(8,128)(2,1)S(1)} %pad_maximum_fusion.2.refs_1_), channel_id=1, source_target_pairs={{0,2},{1,3},{2,0},{3,1},{4,6},{5,7},{6,4},{7,5},{8,10},{9,11},{10,... | collective-permute-start | bytes 245768 | tf_op jit(solution)/shard_map/ppermute | solution.py:386
  116.1 6.0 %collective-permute-start.47 = (bf16[320,128]{1,0:T(8,128)(2,1)S(1)}, bf16[320,128]{1,0:T(8,128)(2,1)S(1)}, u32[]{:S(2)}, u32[]{:S(2)}) collective-permute-start(bf16[320,128]{1,0:T(8,128)(2,1)S(1)} %pad_maximum_fusion.2.refs_1_), channel_id=1, source_target_pairs={{0,1},{1,0},{2,3},{3,2},{4,5},{5,4},{6,7},{7,6},{8,9},{9,8},{10,11... | collective-permute-start | bytes 245768 | tf_op jit(solution)/shard_map/ppermute | solution.py:386
  116.2 5.9 %collective-permute-start.53 = (bf16[320,128]{1,0:T(8,128)(2,1)S(1)}, bf16[320,128]{1,0:T(8,128)(2,1)S(1)}, u32[]{:S(2)}, u32[]{:S(2)}) collective-permute-start(bf16[320,128]{1,0:T(8,128)(2,1)S(1)} %collective-permute-done.52.refs_7_), channel_id=1, source_target_pairs={{0,1},{1,0},{2,3},{3,2},{4,5},{5,4},{6,7},{7,6},{8,9},{9,8},{10,11... | collective-permute-start | bytes 245768 | tf_op jit(solution)/shard_map/ppermute | solution.py:386
  117.0 5.2 %collective-permute-start.51 = (bf16[320,128]{1,0:T(8,128)(2,1)S(1)}, bf16[320,128]{1,0:T(8,128)(2,1)S(1)}, u32[]{:S(2)}, u32[]{:S(2)}) collective-permute-start(bf16[320,128]{1,0:T(8,128)(2,1)S(1)} %collective-permute-done.50.refs_5_), channel_id=1, source_target_pairs={{0,1},{1,0},{2,3},{3,2},{4,5},{5,4},{6,7},{7,6},{8,9},{9,8},{10,11... | collective-permute-start | bytes 245768 | tf_op jit(solution)/shard_map/ppermute | solution.py:386
  117.0 5.2 %collective-permute-start.49 = (bf16[320,128]{1,0:T(8,128)(2,1)S(1)}, bf16[320,128]{1,0:T(8,128)(2,1)S(1)}, u32[]{:S(2)}, u32[]{:S(2)}) collective-permute-start(bf16[320,128]{1,0:T(8,128)(2,1)S(1)} %collective-permute-done.48.refs_3_), channel_id=1, source_target_pairs={{0,1},{1,0},{2,3},{3,2},{4,5},{5,4},{6,7},{7,6},{8,9},{9,8},{10,11... | collective-permute-start | bytes 245768 | tf_op jit(solution)/shard_map/ppermute | solution.py:386

commit v4 on v3

--- a/solution.py
+++ b/solution.py
@@ -322,46 +322,46 @@
     picks = index.shape[1]
     count = len(pieces)
     rows = up(outputs, 16)
-    tile = min(1024, frames)
+    tile = min(512, frames)
+    tiles = frames // tile
 
     def body(owners_ref, index_ref, residual_ref, coeffs_ref, *refs):
         kernels_ref, refs = refs[: len(kernels)], refs[len(kernels) :]
         pieces_ref = refs[:count]
-        new_residual_ref, new_coeffs_ref, canon, own, places = refs[count:]
-        here = pl.program_id(0)
-
-        @pl.when(here == 0)
-        def _():
-            unfold(pieces_ref, pieces[0].shape[0] * 2 // rows, picks, canon)
-            mine = canon[:, 0:picks]
-            own[...] = jnp.where(lax.axis_index("rows") == owners_ref[step], mine, jnp.zeros_like(mine))
-            places[...] = turn(index_ref[step : step + 1, :])
-
-        change, first = 0.0, 0
-        for kernel_ref in kernels_ref:
-            last = first + kernel_ref.shape[0]
-            change = change + matmul(canon[:, first:last], kernel_ref[:, lane_start(here, tile)])
-            first = last
-        frame = lax.broadcasted_iota(jnp.int32, (picks, tile), 1) + here * tile
-        hot = jnp.where(frame == places[...], 1.0, 0.0).astype(bf16)
-        put = matmul(own[...], hot)
-        new_residual_ref[...] = residual_ref[:, lane_start(here, tile)] - (change + penalty * put)[:outputs]
-        new_coeffs_ref[...] = coeffs_ref[:, lane_start(here, tile)] + put[:outputs]
-
-    strip = pl.BlockSpec((outputs, tile), lambda i: (0, i))
-    return pl.pallas_call(
-        body,
-        grid=(frames // tile,),
+        out_residual, out_coeffs, canon, new_residual, new_coeffs, sems = refs[count:]
+        unfold(pieces_ref, pieces[0].shape[0] * 2 // rows, picks, canon)
+        mine = canon[:, 0:picks]
+        own = jnp.where(lax.axis_index("rows") == owners_ref[step], mine, jnp.zeros_like(mine))
+        places = turn(index_ref[step : step + 1, :])
+        copies = []
+        for n in range(tiles):
+            here = slice(n * tile, (n + 1) * tile)
+            change, first = 0.0, 0
+            for kernel_ref in kernels_ref:
+                last = first + kernel_ref.shape[0]
+                change = change + matmul(canon[:, first:last], kernel_ref[:, here])
+                first = last
+            frame = lax.broadcasted_iota(jnp.int32, (picks, tile), 1) + n * tile
+            put = matmul(own, jnp.where(frame == places, 1.0, 0.0).astype(bf16))
+            new_residual[:, here] = residual_ref[:, here] - (change + penalty * put)[:outputs]
+            new_coeffs[:, here] = coeffs_ref[:, here] + put[:outputs]
+            for k, (new, out) in enumerate(((new_residual, out_residual), (new_coeffs, out_coeffs))):
+                copy = pltpu.make_async_copy(new.at[:, here], out.at[:, here], sems.at[2 * n + k])
+                copy.start()
+                copies.append(copy)
+        for copy in copies:
+            copy.wait()
+
+    return pl.pallas_call(
+        body,
         in_specs=[smem, vmem, vmem, vmem] + [vmem] * (len(kernels) + count),
-        out_specs=(strip, strip),
-        out_shape=(
-            jax.ShapeDtypeStruct((outputs, frames), f32),
-            jax.ShapeDtypeStruct((outputs, frames), f32),
-        ),
+        out_specs=(pl.BlockSpec(memory_space=pl.ANY),) * 2,
+        out_shape=(jax.ShapeDtypeStruct((outputs, frames), f32),) * 2,
         scratch_shapes=[
             pltpu.VMEM((rows, block), bf16),
-            pltpu.VMEM((rows, picks), bf16),
-            pltpu.VMEM((picks, 1), jnp.int32),
+            pltpu.VMEM((outputs, frames), f32),
+            pltpu.VMEM((outputs, frames), f32),
+            pltpu.SemaphoreType.DMA((2 * tiles,)),
         ],
         cost_estimate=pl.CostEstimate(
             flops=2 * rows * block * frames, transcendentals=0, bytes_accessed=2 * block * frames
@@ -533,7 +533,7 @@
             and block_index.shape[0] == 2
             and block_index.shape[1] % LANES == 0
             and 2 * block_inverse.shape[1] == LANES
-            and features.shape[0] % 1024 == 0
+            and features.shape[0] % 512 == 0
         )
 
     small = power_of_two(rows) and power_of_two(cols) and 2 <= rows <= 8 and 4 <= cols <= 16

time: 126 us -> 126 us (level)
  transfers between devices with their start and end apart: 54 -> 54, of which waited for: 13 -> 12; matrix products, arithmetic and copies ran while one was open for 1% -> 1% of each run, Pallas kernels for 14% -> 15%
where the time goes in v4:
time: 126 us
  starting transfers between devices  49.3 us (39%)
  waiting for transfers between devices  47.5 us (38%)
  Pallas kernels  23.4 us (19%)
  local copies, waits for them, and re-layouts  3.74 us (3%)
  between operations  1.27 us (1%)
    ppermute x54, starting transfers between devices, send(): return lax.ppermute(value, ('rows', 'cols'), pairs)  49.3 us
    ppermute x54, waiting for transfers between devices, send(): return lax.ppermute(value, ('rows', 'cols'), pairs)  47.5 us
    pallas_call x3, Pallas kernels, block_kernel(): pl.pallas_call(body, in_specs=[vmem] * (1 + count), out_specs=vmem, out_s...  9.67 us
    pallas_call x2, Pallas kernels, apply_update(): pl.pallas_call(body, in_specs=[smem, vmem, vmem, vmem] + [vmem] * (len(ke...  7.17 us
    unnamed x30, local copies, waits for them, and re-layouts  3.71 us
  transfers between devices with their start and end apart: 54, of which 12 were waited for; matrix products, arithmetic and copies ran while one was open for 1% of the time, Pallas kernels for 15%

profile of v4, /device:TPU:0, one launch (start us, length us, event | category | flops | bytes accessed | tf_op | source)
XLA Modules:
  0.0 126.1 jit_solution(12657487426725647171)
XLA Ops:
  0.7 1.3 %copy-done.2 = f32[2048,147]{0,1:T(8,128)S(1)} copy-done((f32[2048,147]{0,1:T(8,128)S(1)}, f32[2048,147]{0,1:T(8,128)}, u32[]{:S(2)}) %copy-start.2) | copy-done | bytes 1204248
  1.9 0.7 copy-done.6
  2.6 1.2 pick_residual.1
  3.9 3.1 %collective-permute-start.9 = (f16[160,256]{1,0:T(8,128)(2,1)S(1)}, f16[160,256]{1,0:T(8,128)(2,1)S(1)}, u32[]{:S(2)}, u32[]{:S(2)}) collective-permute-start(f16[160,256]{1,0:T(8,128)(2,1)S(1)} %convert_element_type.24), channel_id=1, source_target_pairs={{0,8},{1,9},{2,10},{3,11},{4,12},{5,13},{6,14},{7,15},{8,0},{9,1},... | collective-permute-start | bytes 245768 | tf_op jit(solution)/shard_map/ppermute | solution.py:386
  7.0 1.5 %copy-done = bf16[2048,440]{0,1:T(8,128)(2,1)S(1)} copy-done((bf16[2048,440]{0,1:T(8,128)(2,1)S(1)}, bf16[2048,440]{0,1:T(8,128)(2,1)}, u32[]{:S(2)}) %copy-start) | copy-done | bytes 1802264
  8.5 1.7 %pick_features.1 = (bf16[464,256]{1,0:T(8,128)(2,1)S(1)}, bf16[464,256]{1,0:T(8,128)(2,1)S(1)}, f32[1,256]{1,0:T(1,128)S(1)}, f32[1,256]{1,0:T(1,128)S(1)}, f32[1,256]{1,0:T(1,128)S(1)}, /*index=5*/f32[1,256]{1,0:T(1,128)S(1)}) custom-call(s32[2]{0:T(128)S(1)} %copy-done.8, s32[2,256]{1,0:T(2,128)S(1)} %copy-done.7, bf16[440,2048]{1,0:T(8,128)(2,1)S(1)} %bitcast.5), custom_call_target="tpu_custom_call" | custom-call | tf_op jit(solution)/shard_map/pick_features/pallas_call | solution.py:135
  10.4 2.1 %collective-permute-start.28 = (f16[624,256]{1,0:T(8,128)(2,1)S(1)}, f16[624,256]{1,0:T(8,128)(2,1)S(1)}, u32[]{:S(2)}, u32[]{:S(2)}) collective-permute-start(f16[624,256]{1,0:T(8,128)(2,1)S(1)} %pad_maximum_fusion), channel_id=1, source_target_pairs={{0,8},{1,9},{2,10},{3,11},{4,12},{5,13},{6,14},{7,15},{8,0},{9,1},... | collective-permute-start | bytes 958472 | tf_op jit(solution)/shard_map/ppermute | solution.py:386
  12.6 2.7 %collective-permute-start.10 = (f16[160,256]{1,0:T(8,128)(2,1)S(1)}, f16[160,256]{1,0:T(8,128)(2,1)S(1)}, u32[]{:S(2)}, u32[]{:S(2)}) collective-permute-start(f16[160,256]{1,0:T(8,128)(2,1)S(1)} %broadcast_select_fusion.4), channel_id=1, source_target_pairs={{0,16},{1,17},{2,18},{3,19},{4,20},{5,21},{6,22},{7,23},{8,24},{9,... | collective-permute-start | bytes 245768 | tf_op jit(solution)/shard_map/ppermute | solution.py:386
  15.2 0.1 prepare.1
  15.4 8.5 %collective-permute-done.10 = f16[160,256]{1,0:T(8,128)(2,1)S(1)} collective-permute-done((f16[160,256]{1,0:T(8,128)(2,1)S(1)}, f16[160,256]{1,0:T(8,128)(2,1)S(1)}, u32[]{:S(2)}, u32[]{:S(2)}) %collective-permute-start.10) | collective-permute-done | bytes 81952 | tf_op jit(solution)/shard_map/ppermute | solution.py:386
  24.0 2.7 %collective-permute-start.16 = (f16[160,256]{1,0:T(8,128)(2,1)S(1)}, f16[160,256]{1,0:T(8,128)(2,1)S(1)}, u32[]{:S(2)}, u32[]{:S(2)}) collective-permute-start(f16[160,256]{1,0:T(8,128)(2,1)S(1)} %get-tuple-element.33), channel_id=1, source_target_pairs={{0,6},{1,7},{2,4},{3,5},{4,2},{5,3},{6,0},{7,1},{8,14},{9,15},{10,... | collective-permute-start | bytes 245768 | tf_op jit(solution)/shard_map/ppermute | solution.py:386
  26.6 0.5 collective-permute-start.14
  27.1 0.4 collective-permute-start.12
  27.6 2.4 %collective-permute-done.16 = f16[160,256]{1,0:T(8,128)(2,1)S(1)} collective-permute-done((f16[160,256]{1,0:T(8,128)(2,1)S(1)}, f16[160,256]{1,0:T(8,128)(2,1)S(1)}, u32[]{:S(2)}, u32[]{:S(2)}) %collective-permute-start.16) | collective-permute-done | bytes 81952 | tf_op jit(solution)/shard_map/ppermute | solution.py:386
  29.9 3.7 %collective-permute-start.1 = (bf16[464,256]{1,0:T(8,128)(2,1)S(1)}, bf16[464,256]{1,0:T(8,128)(2,1)S(1)}, u32[]{:S(2)}, u32[]{:S(2)}) collective-permute-start(bf16[464,256]{1,0:T(8,128)(2,1)S(1)} %broadcast_select_fusion.2), channel_id=1, source_target_pairs={{0,16},{1,17},{2,18},{3,19},{4,20},{5,21},{6,22},{7,23},{8,24},{9,... | collective-permute-start | bytes 712712 | tf_op jit(solution)/shard_map/ppermute | solution.py:386
  33.6 0.5 collective-permute-start.15
  34.4 1.3 %collective-permute-start.29 = (f16[624,256]{1,0:T(8,128)(2,1)S(1)}, f16[624,256]{1,0:T(8,128)(2,1)S(1)}, u32[]{:S(2)}, u32[]{:S(2)}) collective-permute-start(f16[624,256]{1,0:T(8,128)(2,1)S(1)} %broadcast_select_fusion), channel_id=1, source_target_pairs={{0,16},{1,17},{2,18},{3,19},{4,20},{5,21},{6,22},{7,23},{8,24},{9,... | collective-permute-start | bytes 958472 | tf_op jit(solution)/shard_map/ppermute | solution.py:386
  36.0 0.6 shard_map.79
  36.6 3.7 %collective-permute-start.20 = (bf16[80,128]{1,0:T(8,128)(2,1)S(1)}, bf16[80,128]{1,0:T(8,128)(2,1)S(1)}, u32[]{:S(2)}, u32[]{:S(2)}) collective-permute-start(bf16[80,128]{1,0:T(8,128)(2,1)S(1)} %shard_map.79), channel_id=1, source_target_pairs={{0,24},{1,25},{2,26},{3,27},{4,28},{5,29},{6,30},{7,31},{8,16},{9,... | collective-permute-start | bytes 61448 | tf_op jit(solution)/shard_map/ppermute | solution.py:386
  40.3 0.8 collective-permute-start.19
  41.1 11.1 %collective-permute-done.1 = bf16[464,256]{1,0:T(8,128)(2,1)S(1)} collective-permute-done((bf16[464,256]{1,0:T(8,128)(2,1)S(1)}, bf16[464,256]{1,0:T(8,128)(2,1)S(1)}, u32[]{:S(2)}, u32[]{:S(2)}) %collective-permute-start.1) | collective-permute-done | bytes 237600 | tf_op jit(solution)/shard_map/ppermute | solution.py:386
  52.3 2.3 %collective-permute-start.7 = (bf16[464,256]{1,0:T(8,128)(2,1)S(1)}, bf16[464,256]{1,0:T(8,128)(2,1)S(1)}, u32[]{:S(2)}, u32[]{:S(2)}) collective-permute-start(bf16[464,256]{1,0:T(8,128)(2,1)S(1)} %broadcast_select_fusion.3.refs_0_), channel_id=1, source_target_pairs={{0,6},{1,7},{2,4},{3,5},{4,2},{5,3},{6,0},{7,1},{8,14},{9,15},{10,... | collective-permute-start | bytes 712712 | tf_op jit(solution)/shard_map/ppermute | solution.py:386
  54.6 0.5 collective-permute-start.5
  55.1 0.2 localize.1.local_ref
  55.3 2.9 %collective-permute-done.19 = bf16[80,128]{1,0:T(8,128)(2,1)S(1)} collective-permute-done((bf16[80,128]{1,0:T(8,128)(2,1)S(1)}, bf16[80,128]{1,0:T(8,128)(2,1)S(1)}, u32[]{:S(2)}, u32[]{:S(2)}) %collective-permute-start.19) | collective-permute-done | bytes 20512 | tf_op jit(solution)/shard_map/ppermute | solution.py:386
  58.2 2.4 %collective-permute-start.26 = (bf16[320,128]{1,0:T(8,128)(2,1)S(1)}, bf16[320,128]{1,0:T(8,128)(2,1)S(1)}, u32[]{:S(2)}, u32[]{:S(2)}) collective-permute-start(bf16[320,128]{1,0:T(8,128)(2,1)S(1)} %pad_maximum_fusion.1.refs_2_.refs_0_), channel_id=1, source_target_pairs={{0,6},{1,7},{2,4},{3,5},{4,2},{5,3},{6,0},{7,1},{8,14},{9,15},{10,... | collective-permute-start | bytes 245768 | tf_op jit(solution)/shard_map/ppermute | solution.py:386
  60.7 0.6 collective-permute-start.24
  61.2 2.5 %collective-permute-done.26.refs_8_.refs_6_ = bf16[320,128]{1,0:T(8,128)(2,1)S(1)} collective-permute-done((bf16[320,128]{1,0:T(8,128)(2,1)S(1)}, bf16[320,128]{1,0:T(8,128)(2,1)S(1)}, u32[]{:S(2)}, u32[]{:S(2)}) %collective-permute-start.26) | collective-permute-done | bytes 81952 | tf_op jit(solution)/shard_map/ppermute | solution.py:386
  63.7 1.4 %collective-permute-start.3 = (bf16[464,256]{1,0:T(8,128)(2,1)S(1)}, bf16[464,256]{1,0:T(8,128)(2,1)S(1)}, u32[]{:S(2)}, u32[]{:S(2)}) collective-permute-start(bf16[464,256]{1,0:T(8,128)(2,1)S(1)} %broadcast_select_fusion.3.refs_0_), channel_id=1, source_target_pairs={{0,2},{1,3},{2,0},{3,1},{4,6},{5,7},{6,4},{7,5},{8,10},{9,11},{10,... | collective-permute-start | bytes 712712 | tf_op jit(solution)/shard_map/ppermute | solution.py:386
  65.2 0.5 collective-permute-start.8
  65.8 0.9 collective-permute-start.22
  66.7 4.0 %collective-permute-done.3.refs_2_ = bf16[464,256]{1,0:T(8,128)(2,1)S(1)} collective-permute-done((bf16[464,256]{1,0:T(8,128)(2,1)S(1)}, bf16[464,256]{1,0:T(8,128)(2,1)S(1)}, u32[]{:S(2)}, u32[]{:S(2)}) %collective-permute-start.3) | collective-permute-done | bytes 237600 | tf_op jit(solution)/shard_map/ppermute | solution.py:386
  70.8 0.8 collective-permute-done.22.refs_4_.refs_2_
  71.6 0.5 collective-permute-start.27
  72.2 0.4 collective-permute-start.23
  72.7 2.4 %collective-permute-start.35 = (bf16[464,256]{1,0:T(8,128)(2,1)S(1)}, bf16[464,256]{1,0:T(8,128)(2,1)S(1)}, u32[]{:S(2)}, u32[]{:S(2)}) collective-permute-start(bf16[464,256]{1,0:T(8,128)(2,1)S(1)} %slice_convert_fusion.refs_0_.second_ref), channel_id=1, source_target_pairs={{0,6},{1,7},{2,4},{3,5},{4,2},{5,3},{6,0},{7,1},{8,14},{9,15},{10,... | collective-permute-start | bytes 712712 | tf_op jit(solution)/shard_map/ppermute | solution.py:386
  75.1 1.4 %meeting_kernel.1.kernel_ref = bf16[2048,256]{1,0:T(8,128)(2,1)S(1)} custom-call(s32[2]{0:T(128)S(1)} %copy-done.8, s32[2,256]{1,0:T(2,128)S(1)} %copy-done.7, bf16[464,256]{1,0:T(8,128)(2,1)S(1)} %slice_convert_fusion.refs_0_.second_ref, bf16[464,256]{1,0:T(8,128)(2,1)S(1)} %broadcast_select_fusion.3.refs_0_, ...), custom_call_target="tpu_custom_call" | custom-call | flops 486539264 | bytes 1000000 | tf_op jit(solution)/shard_map/meeting_kernel/pallas_call | solution.py:234
  76.5 0.6 collective-permute-start.33
  77.1 0.6 collective-permute-start.31
  77.7 0.7 advance.1
  78.4 1.5 %collective-permute-start.38 = (f16[160,256]{1,0:T(8,128)(2,1)S(1)}, f16[160,256]{1,0:T(8,128)(2,1)S(1)}, u32[]{:S(2)}, u32[]{:S(2)}) collective-permute-start(f16[160,256]{1,0:T(8,128)(2,1)S(1)} %get-tuple-element.31), channel_id=1, source_target_pairs={{0,2},{1,3},{2,0},{3,1},{4,6},{5,7},{6,4},{7,5},{8,10},{9,11},{10,... | collective-permute-start | bytes 245768 | tf_op jit(solution)/shard_map/ppermute | solution.py:386
  79.9 2.4 %shard_map.78.refs_1_ = bf16[1024,2048]{1,0:T(8,128)(2,1)S(1)} custom-call(bf16[464,2048]{1,0:T(8,128)(2,1)S(1)} %localize.1.local_ref, bf16[464,256]{1,0:T(8,128)(2,1)S(1)} %collective-permute-done.5.refs_0_.refs_4_, bf16[464,256]{1,0:T(8,128)(2,1)S(1)} %collective-permute-done.6.refs_1_.refs_5_, ...), custom_call_target="tpu_custom_call" | custom-call | flops 1946157056 | bytes 10000000 | tf_op jit(solution)/shard_map/pallas_call | solution.py:283
  82.3 5.9 %collective-permute-done.38 = f16[160,256]{1,0:T(8,128)(2,1)S(1)} collective-permute-done((f16[160,256]{1,0:T(8,128)(2,1)S(1)}, f16[160,256]{1,0:T(8,128)(2,1)S(1)}, u32[]{:S(2)}, u32[]{:S(2)}) %collective-permute-start.38) | collective-permute-done | bytes 81952 | tf_op jit(solution)/shard_map/ppermute | solution.py:386
  88.2 0.6 collective-permute-start.40
  88.9 3.8 %collective-permute-done.40 = f16[160,256]{1,0:T(8,128)(2,1)S(1)} collective-permute-done((f16[160,256]{1,0:T(8,128)(2,1)S(1)}, f16[160,256]{1,0:T(8,128)(2,1)S(1)}, u32[]{:S(2)}, u32[]{:S(2)}) %collective-permute-start.40) | collective-permute-done | bytes 81952 | tf_op jit(solution)/shard_map/ppermute | solution.py:386
  92.7 1.4 %collective-permute-start.42 = (f16[160,256]{1,0:T(8,128)(2,1)S(1)}, f16[160,256]{1,0:T(8,128)(2,1)S(1)}, u32[]{:S(2)}, u32[]{:S(2)}) collective-permute-start(f16[160,256]{1,0:T(8,128)(2,1)S(1)} %get-tuple-element.31), channel_id=1, source_target_pairs={{0,6},{1,7},{2,4},{3,5},{4,2},{5,3},{6,0},{7,1},{8,14},{9,15},{10,... | collective-permute-start | bytes 245768 | tf_op jit(solution)/shard_map/ppermute | solution.py:386
  94.2 0.6 collective-permute-start.30
  94.8 3.3 %collective-permute-done.42 = f16[160,256]{1,0:T(8,128)(2,1)S(1)} collective-permute-done((f16[160,256]{1,0:T(8,128)(2,1)S(1)}, f16[160,256]{1,0:T(8,128)(2,1)S(1)}, u32[]{:S(2)}, u32[]{:S(2)}) %collective-permute-start.42) | collective-permute-done | bytes 81952 | tf_op jit(solution)/shard_map/ppermute | solution.py:386
  98.0 0.5 collective-permute-start.43
  98.6 1.1 collective-permute-done.43
  99.8 0.7 shard_map.82
  100.4 4.2 %collective-permute-start.46 = (bf16[80,128]{1,0:T(8,128)(2,1)S(1)}, bf16[80,128]{1,0:T(8,128)(2,1)S(1)}, u32[]{:S(2)}, u32[]{:S(2)}) collective-permute-start(bf16[80,128]{1,0:T(8,128)(2,1)S(1)} %shard_map.82), channel_id=1, source_target_pairs={{0,24},{1,25},{2,26},{3,27},{4,28},{5,29},{6,30},{7,31},{8,16},{9,... | collective-permute-start | bytes 61448 | tf_op jit(solution)/shard_map/ppermute | solution.py:386
  104.7 0.4 collective-permute-start.45
  105.1 0.5 collective-permute-start.44
  105.6 2.6 %shard_map.77.refs_0_ = bf16[1024,2048]{1,0:T(8,128)(2,1)S(1)} custom-call(bf16[464,2048]{1,0:T(8,128)(2,1)S(1)} %localize.1.local_ref, bf16[464,256]{1,0:T(8,128)(2,1)S(1)} %broadcast_select_fusion.3.refs_0_, bf16[464,256]{1,0:T(8,128)(2,1)S(1)} %collective-permute-done.2.refs_1_, bf16[464,256]{1,0:T(8,128)(2,1)S(1)} %collective-permute-done.3.refs_2_, ...), custom_call_target="tpu_custom_call" | custom-call | flops 1946157056 | bytes 10000000 | tf_op jit(solution)/shard_map/pallas_call | solution.py:283
  108.3 1.0 collective-permute-done.45
  109.4 1.5 %collective-permute-start.52 = (bf16[320,128]{1,0:T(8,128)(2,1)S(1)}, bf16[320,128]{1,0:T(8,128)(2,1)S(1)}, u32[]{:S(2)}, u32[]{:S(2)}) collective-permute-start(bf16[320,128]{1,0:T(8,128)(2,1)S(1)} %pad_maximum_fusion.2.refs_1_), channel_id=1, source_target_pairs={{0,6},{1,7},{2,4},{3,5},{4,2},{5,3},{6,0},{7,1},{8,14},{9,15},{10,... | collective-permute-start | bytes 245768 | tf_op jit(solution)/shard_map/ppermute | solution.py:386
  110.9 1.3 %collective-permute-start.50 = (bf16[320,128]{1,0:T(8,128)(2,1)S(1)}, bf16[320,128]{1,0:T(8,128)(2,1)S(1)}, u32[]{:S(2)}, u32[]{:S(2)}) collective-permute-start(bf16[320,128]{1,0:T(8,128)(2,1)S(1)} %pad_maximum_fusion.2.refs_1_), channel_id=1, source_target_pairs={{0,4},{1,5},{2,6},{3,7},{4,0},{5,1},{6,2},{7,3},{8,12},{9,13},{10,... | collective-permute-start | bytes 245768 | tf_op jit(solution)/shard_map/ppermute | solution.py:386
  112.2 0.7 collective-permute-start.48
  113.0 3.5 %shard_map.80 = (f32[147,2048]{1,0:T(8,128)S(1)}, f32[147,2048]{1,0:T(8,128)S(1)}) custom-call(s32[2]{0:T(128)S(1)} %copy-done.8, s32[2,256]{1,0:T(2,128)S(1)} %copy-done.7, f32[147,2048]{1,0:T(8,128)S(1)} %bitcast.8, f32[147,2048]{1,0:T(8,128)S(1)} %bitcast.9, bf16[1024,2048]{1,0:T(8,128)(2,1)S(1)} %shard_map.77.refs_0_, ...), custom_call_target="tpu_custom_call" | custom-call | flops 1342177280 | bytes 8388608 | tf_op jit(solution)/shard_map/pallas_call | solution.py:355
  116.5 0.5 collective-permute-start.53
  117.1 0.4 collective-permute-start.49
  117.6 4.6 %shard_map.81.refs_0_ = bf16[2048,2048]{1,0:T(8,128)(2,1)S(1)} custom-call(bf16[464,2048]{1,0:T(8,128)(2,1)S(1)} %localize.1.local_ref, bf16[464,256]{1,0:T(8,128)(2,1)S(1)} %slice_convert_fusion.refs_0_.second_ref, bf16[464,256]{1,0:T(8,128)(2,1)S(1)} %collective-permute-done.30.refs_1_, bf16[464,256]{1,0:T(8,128)(2,1)S(1)} %collective-permute-done.31.refs_2_, ...), custom_call_target="tpu_custom_call" | custom-call | flops 3892314112 | bytes 10000000 | tf_op jit(solution)/shard_map/pallas_call | solution.py:283
  122.2 3.7 %shard_map.83 = (f32[147,2048]{1,0:T(8,128)}, f32[147,2048]{1,0:T(8,128)}) custom-call(s32[2]{0:T(128)S(1)} %copy-done.8, s32[2,256]{1,0:T(2,128)S(1)} %copy-done.7, f32[147,2048]{1,0:T(8,128)S(1)} %get-tuple-element.21.residual_ref, f32[147,2048]{1,0:T(8,128)S(1)} %get-tuple-element.22.coeffs_ref, bf16[2048,2048]{1,0:T(8,128)(2,1)S(1)} %shard_map.81.refs_0_, ...), custom_call_target="tpu_custom_call" | custom-call | flops 1342177280 | bytes 8388608 | tf_op jit(solution)/shard_map/pallas_call | solution.py:355
  (110 shorter events, 1.8 us)
Async XLA Ops:
  0.6 6.4 %copy-start.8 = (s32[2]{0:T(128)S(1)}, s32[2]{0:T(128)}, u32[]{:S(2)}) copy-start(s32[2]{0:T(128)} %owners_ref.7) | copy-start | bytes 28
  0.6 1.3 %copy-start.2 = (f32[2048,147]{0,1:T(8,128)S(1)}, f32[2048,147]{0,1:T(8,128)}, u32[]{:S(2)}) copy-start(f32[2048,147]{0,1:T(8,128)} %param.7) | copy-start | bytes 3612676
  1.9 0.7 copy-start.6
  2.6 4.4 %copy-start.7 = (s32[2,256]{1,0:T(2,128)S(1)}, s32[2,256]{1,0:T(2,128)}, u32[]{:S(2)}) copy-start(s32[2,256]{1,0:T(2,128)} %index_ref.7) | copy-start | bytes 6148
  3.9 8.7 %collective-permute-start.9 = (f16[160,256]{1,0:T(8,128)(2,1)S(1)}, f16[160,256]{1,0:T(8,128)(2,1)S(1)}, u32[]{:S(2)}, u32[]{:S(2)}) collective-permute-start(f16[160,256]{1,0:T(8,128)(2,1)S(1)} %convert_element_type.24), channel_id=1, source_target_pairs={{0,8},{1,9},{2,10},{3,11},{4,12},{5,13},{6,14},{7,15},{8,0},{9,1},... | collective-permute-start | bytes 245768 | tf_op jit(solution)/shard_map/ppermute | solution.py:386
  7.0 1.5 %copy-start = (bf16[2048,440]{0,1:T(8,128)(2,1)S(1)}, bf16[2048,440]{0,1:T(8,128)(2,1)}, u32[]{:S(2)}) copy-start(bf16[2048,440]{0,1:T(8,128)(2,1)} %param.6) | copy-start | bytes 5406724
  8.5 6.8 %copy-start.5 = (f32[2,64,2048]{2,1,0:T(8,128)S(1)}, f32[2,64,2048]{2,1,0:T(8,128)}, u32[]{:S(2)}) copy-start(f32[2,64,2048]{2,1,0:T(8,128)} %inverse_ref.1) | copy-start | bytes 3145732
  10.2 17.3 %collective-permute-start = (bf16[464,256]{1,0:T(8,128)(2,1)S(1)}, bf16[464,256]{1,0:T(8,128)(2,1)S(1)}, u32[]{:S(2)}, u32[]{:S(2)}) collective-permute-start(bf16[464,256]{1,0:T(8,128)(2,1)S(1)} %get-tuple-element.18), channel_id=1, source_target_pairs={{0,8},{1,9},{2,10},{3,11},{4,12},{5,13},{6,14},{7,15},{8,0},{9,1},... | collective-permute-start | bytes 712712 | tf_op jit(solution)/shard_map/ppermute | solution.py:386
  10.4 23.8 %collective-permute-start.28 = (f16[624,256]{1,0:T(8,128)(2,1)S(1)}, f16[624,256]{1,0:T(8,128)(2,1)S(1)}, u32[]{:S(2)}, u32[]{:S(2)}) collective-permute-start(f16[624,256]{1,0:T(8,128)(2,1)S(1)} %pad_maximum_fusion), channel_id=1, source_target_pairs={{0,8},{1,9},{2,10},{3,11},{4,12},{5,13},{6,14},{7,15},{8,0},{9,1},... | collective-permute-start | bytes 958472 | tf_op jit(solution)/shard_map/ppermute | solution.py:386
  12.6 11.3 %collective-permute-start.10 = (f16[160,256]{1,0:T(8,128)(2,1)S(1)}, f16[160,256]{1,0:T(8,128)(2,1)S(1)}, u32[]{:S(2)}, u32[]{:S(2)}) collective-permute-start(f16[160,256]{1,0:T(8,128)(2,1)S(1)} %broadcast_select_fusion.4), channel_id=1, source_target_pairs={{0,16},{1,17},{2,18},{3,19},{4,20},{5,21},{6,22},{7,23},{8,24},{9,... | collective-permute-start | bytes 245768 | tf_op jit(solution)/shard_map/ppermute | solution.py:386
  24.0 6.0 %collective-permute-start.16 = (f16[160,256]{1,0:T(8,128)(2,1)S(1)}, f16[160,256]{1,0:T(8,128)(2,1)S(1)}, u32[]{:S(2)}, u32[]{:S(2)}) collective-permute-start(f16[160,256]{1,0:T(8,128)(2,1)S(1)} %get-tuple-element.33), channel_id=1, source_target_pairs={{0,6},{1,7},{2,4},{3,5},{4,2},{5,3},{6,0},{7,1},{8,14},{9,15},{10,... | collective-permute-start | bytes 245768 | tf_op jit(solution)/shard_map/ppermute | solution.py:386
  26.6 7.0 %collective-permute-start.14 = (f16[160,256]{1,0:T(8,128)(2,1)S(1)}, f16[160,256]{1,0:T(8,128)(2,1)S(1)}, u32[]{:S(2)}, u32[]{:S(2)}) collective-permute-start(f16[160,256]{1,0:T(8,128)(2,1)S(1)} %get-tuple-element.33), channel_id=1, source_target_pairs={{0,4},{1,5},{2,6},{3,7},{4,0},{5,1},{6,2},{7,3},{8,12},{9,13},{10,... | collective-permute-start | bytes 245768 | tf_op jit(solution)/shard_map/ppermute | solution.py:386
  27.1 6.5 %collective-permute-start.12 = (f16[160,256]{1,0:T(8,128)(2,1)S(1)}, f16[160,256]{1,0:T(8,128)(2,1)S(1)}, u32[]{:S(2)}, u32[]{:S(2)}) collective-permute-start(f16[160,256]{1,0:T(8,128)(2,1)S(1)} %get-tuple-element.33), channel_id=1, source_target_pairs={{0,2},{1,3},{2,0},{3,1},{4,6},{5,7},{6,4},{7,5},{8,10},{9,11},{10,... | collective-permute-start | bytes 245768 | tf_op jit(solution)/shard_map/ppermute | solution.py:386
  27.5 6.6 %collective-permute-start.11 = (f16[160,256]{1,0:T(8,128)(2,1)S(1)}, f16[160,256]{1,0:T(8,128)(2,1)S(1)}, u32[]{:S(2)}, u32[]{:S(2)}) collective-permute-start(f16[160,256]{1,0:T(8,128)(2,1)S(1)} %get-tuple-element.33), channel_id=1, source_target_pairs={{0,1},{1,0},{2,3},{3,2},{4,5},{5,4},{6,7},{7,6},{8,9},{9,8},{10,11... | collective-permute-start | bytes 245768 | tf_op jit(solution)/shard_map/ppermute | solution.py:386
  29.9 22.3 %collective-permute-start.1 = (bf16[464,256]{1,0:T(8,128)(2,1)S(1)}, bf16[464,256]{1,0:T(8,128)(2,1)S(1)}, u32[]{:S(2)}, u32[]{:S(2)}) collective-permute-start(bf16[464,256]{1,0:T(8,128)(2,1)S(1)} %broadcast_select_fusion.2), channel_id=1, source_target_pairs={{0,16},{1,17},{2,18},{3,19},{4,20},{5,21},{6,22},{7,23},{8,24},{9,... | collective-permute-start | bytes 712712 | tf_op jit(solution)/shard_map/ppermute | solution.py:386
  33.6 2.2 %collective-permute-start.17 = (f16[160,256]{1,0:T(8,128)(2,1)S(1)}, f16[160,256]{1,0:T(8,128)(2,1)S(1)}, u32[]{:S(2)}, u32[]{:S(2)}) collective-permute-start(f16[160,256]{1,0:T(8,128)(2,1)S(1)} %collective-permute-done.16), channel_id=1, source_target_pairs={{0,1},{1,0},{2,3},{3,2},{4,5},{5,4},{6,7},{7,6},{8,9},{9,8},{10,11... | collective-permute-start | bytes 245768 | tf_op jit(solution)/shard_map/ppermute | solution.py:386
  33.6 2.2 %collective-permute-start.15 = (f16[160,256]{1,0:T(8,128)(2,1)S(1)}, f16[160,256]{1,0:T(8,128)(2,1)S(1)}, u32[]{:S(2)}, u32[]{:S(2)}) collective-permute-start(f16[160,256]{1,0:T(8,128)(2,1)S(1)} %collective-permute-done.14), channel_id=1, source_target_pairs={{0,1},{1,0},{2,3},{3,2},{4,5},{5,4},{6,7},{7,6},{8,9},{9,8},{10,11... | collective-permute-start | bytes 245768 | tf_op jit(solution)/shard_map/ppermute | solution.py:386
  34.1 1.6 %collective-permute-start.13 = (f16[160,256]{1,0:T(8,128)(2,1)S(1)}, f16[160,256]{1,0:T(8,128)(2,1)S(1)}, u32[]{:S(2)}, u32[]{:S(2)}) collective-permute-start(f16[160,256]{1,0:T(8,128)(2,1)S(1)} %collective-permute-done.12), channel_id=1, source_target_pairs={{0,1},{1,0},{2,3},{3,2},{4,5},{5,4},{6,7},{7,6},{8,9},{9,8},{10,11... | collective-permute-start | bytes 245768 | tf_op jit(solution)/shard_map/ppermute | solution.py:386
  34.4 30.8 %collective-permute-start.29 = (f16[624,256]{1,0:T(8,128)(2,1)S(1)}, f16[624,256]{1,0:T(8,128)(2,1)S(1)}, u32[]{:S(2)}, u32[]{:S(2)}) collective-permute-start(f16[624,256]{1,0:T(8,128)(2,1)S(1)} %broadcast_select_fusion), channel_id=1, source_target_pairs={{0,16},{1,17},{2,18},{3,19},{4,20},{5,21},{6,22},{7,23},{8,24},{9,... | collective-permute-start | bytes 958472 | tf_op jit(solution)/shard_map/ppermute | solution.py:386
  36.0 19.2 %copy-start.1 = (bf16[2048,440]{0,1:T(8,128)(2,1)S(1)}, bf16[2048,440]{0,1:T(8,128)(2,1)}, u32[]{:S(2)}) copy-start(bf16[2048,440]{0,1:T(8,128)(2,1)} %param.6) | copy-start | bytes 5406724
  36.6 18.0 %collective-permute-start.20 = (bf16[80,128]{1,0:T(8,128)(2,1)S(1)}, bf16[80,128]{1,0:T(8,128)(2,1)S(1)}, u32[]{:S(2)}, u32[]{:S(2)}) collective-permute-start(bf16[80,128]{1,0:T(8,128)(2,1)S(1)} %shard_map.79), channel_id=1, source_target_pairs={{0,24},{1,25},{2,26},{3,27},{4,28},{5,29},{6,30},{7,31},{8,16},{9,... | collective-permute-start | bytes 61448 | tf_op jit(solution)/shard_map/ppermute | solution.py:386
  40.3 17.9 %collective-permute-start.19 = (bf16[80,128]{1,0:T(8,128)(2,1)S(1)}, bf16[80,128]{1,0:T(8,128)(2,1)S(1)}, u32[]{:S(2)}, u32[]{:S(2)}) collective-permute-start(bf16[80,128]{1,0:T(8,128)(2,1)S(1)} %shard_map.79), channel_id=1, source_target_pairs={{0,16},{1,17},{2,18},{3,19},{4,20},{5,21},{6,22},{7,23},{8,24},{9,... | collective-permute-start | bytes 61448 | tf_op jit(solution)/shard_map/ppermute | solution.py:386
  41.1 17.1 %collective-permute-start.18 = (bf16[80,128]{1,0:T(8,128)(2,1)S(1)}, bf16[80,128]{1,0:T(8,128)(2,1)S(1)}, u32[]{:S(2)}, u32[]{:S(2)}) collective-permute-start(bf16[80,128]{1,0:T(8,128)(2,1)S(1)} %shard_map.79), channel_id=1, source_target_pairs={{0,8},{1,9},{2,10},{3,11},{4,12},{5,13},{6,14},{7,15},{8,0},{9,1},... | collective-permute-start | bytes 61448 | tf_op jit(solution)/shard_map/ppermute | solution.py:386
  52.3 12.9 %collective-permute-start.7 = (bf16[464,256]{1,0:T(8,128)(2,1)S(1)}, bf16[464,256]{1,0:T(8,128)(2,1)S(1)}, u32[]{:S(2)}, u32[]{:S(2)}) collective-permute-start(bf16[464,256]{1,0:T(8,128)(2,1)S(1)} %broadcast_select_fusion.3.refs_0_), channel_id=1, source_target_pairs={{0,6},{1,7},{2,4},{3,5},{4,2},{5,3},{6,0},{7,1},{8,14},{9,15},{10,... | collective-permute-start | bytes 712712 | tf_op jit(solution)/shard_map/ppermute | solution.py:386
  54.6 11.0 %collective-permute-start.5 = (bf16[464,256]{1,0:T(8,128)(2,1)S(1)}, bf16[464,256]{1,0:T(8,128)(2,1)S(1)}, u32[]{:S(2)}, u32[]{:S(2)}) collective-permute-start(bf16[464,256]{1,0:T(8,128)(2,1)S(1)} %broadcast_select_fusion.3.refs_0_), channel_id=1, source_target_pairs={{0,4},{1,5},{2,6},{3,7},{4,0},{5,1},{6,2},{7,3},{8,12},{9,13},{10,... | collective-permute-start | bytes 712712 | tf_op jit(solution)/shard_map/ppermute | solution.py:386
  58.2 5.5 %collective-permute-start.26 = (bf16[320,128]{1,0:T(8,128)(2,1)S(1)}, bf16[320,128]{1,0:T(8,128)(2,1)S(1)}, u32[]{:S(2)}, u32[]{:S(2)}) collective-permute-start(bf16[320,128]{1,0:T(8,128)(2,1)S(1)} %pad_maximum_fusion.1.refs_2_.refs_0_), channel_id=1, source_target_pairs={{0,6},{1,7},{2,4},{3,5},{4,2},{5,3},{6,0},{7,1},{8,14},{9,15},{10,... | collective-permute-start | bytes 245768 | tf_op jit(solution)/shard_map/ppermute | solution.py:386
  60.7 5.2 %collective-permute-start.24 = (bf16[320,128]{1,0:T(8,128)(2,1)S(1)}, bf16[320,128]{1,0:T(8,128)(2,1)S(1)}, u32[]{:S(2)}, u32[]{:S(2)}) collective-permute-start(bf16[320,128]{1,0:T(8,128)(2,1)S(1)} %pad_maximum_fusion.1.refs_2_.refs_0_), channel_id=1, source_target_pairs={{0,4},{1,5},{2,6},{3,7},{4,0},{5,1},{6,2},{7,3},{8,12},{9,13},{10,... | collective-permute-start | bytes 245768 | tf_op jit(solution)/shard_map/ppermute | solution.py:386
  63.7 7.0 %collective-permute-start.3 = (bf16[464,256]{1,0:T(8,128)(2,1)S(1)}, bf16[464,256]{1,0:T(8,128)(2,1)S(1)}, u32[]{:S(2)}, u32[]{:S(2)}) collective-permute-start(bf16[464,256]{1,0:T(8,128)(2,1)S(1)} %broadcast_select_fusion.3.refs_0_), channel_id=1, source_target_pairs={{0,2},{1,3},{2,0},{3,1},{4,6},{5,7},{6,4},{7,5},{8,10},{9,11},{10,... | collective-permute-start | bytes 712712 | tf_op jit(solution)/shard_map/ppermute | solution.py:386
  65.2 6.5 %collective-permute-start.2 = (bf16[464,256]{1,0:T(8,128)(2,1)S(1)}, bf16[464,256]{1,0:T(8,128)(2,1)S(1)}, u32[]{:S(2)}, u32[]{:S(2)}) collective-permute-start(bf16[464,256]{1,0:T(8,128)(2,1)S(1)} %broadcast_select_fusion.3.refs_0_), channel_id=1, source_target_pairs={{0,1},{1,0},{2,3},{3,2},{4,5},{5,4},{6,7},{7,6},{8,9},{9,8},{10,11... | collective-permute-start | bytes 712712 | tf_op jit(solution)/shard_map/ppermute | solution.py:386
  65.2 7.0 %collective-permute-start.8 = (bf16[464,256]{1,0:T(8,128)(2,1)S(1)}, bf16[464,256]{1,0:T(8,128)(2,1)S(1)}, u32[]{:S(2)}, u32[]{:S(2)}) collective-permute-start(bf16[464,256]{1,0:T(8,128)(2,1)S(1)} %collective-permute-done.7.refs_2_.refs_6_), channel_id=1, source_target_pairs={{0,1},{1,0},{2,3},{3,2},{4,5},{5,4},{6,7},{7,6},{8,9},{9,8},{10,11... | collective-permute-start | bytes 712712 | tf_op jit(solution)/shard_map/ppermute | solution.py:386
  65.7 6.5 %collective-permute-start.6 = (bf16[464,256]{1,0:T(8,128)(2,1)S(1)}, bf16[464,256]{1,0:T(8,128)(2,1)S(1)}, u32[]{:S(2)}, u32[]{:S(2)}) collective-permute-start(bf16[464,256]{1,0:T(8,128)(2,1)S(1)} %collective-permute-done.5.refs_0_.refs_4_), channel_id=1, source_target_pairs={{0,1},{1,0},{2,3},{3,2},{4,5},{5,4},{6,7},{7,6},{8,9},{9,8},{10,11... | collective-permute-start | bytes 712712 | tf_op jit(solution)/shard_map/ppermute | solution.py:386
  65.8 5.8 %collective-permute-start.22 = (bf16[320,128]{1,0:T(8,128)(2,1)S(1)}, bf16[320,128]{1,0:T(8,128)(2,1)S(1)}, u32[]{:S(2)}, u32[]{:S(2)}) collective-permute-start(bf16[320,128]{1,0:T(8,128)(2,1)S(1)} %pad_maximum_fusion.1.refs_2_.refs_0_), channel_id=1, source_target_pairs={{0,2},{1,3},{2,0},{3,1},{4,6},{5,7},{6,4},{7,5},{8,10},{9,11},{10,... | collective-permute-start | bytes 245768 | tf_op jit(solution)/shard_map/ppermute | solution.py:386
  70.7 1.9 %collective-permute-start.4 = (bf16[464,256]{1,0:T(8,128)(2,1)S(1)}, bf16[464,256]{1,0:T(8,128)(2,1)S(1)}, u32[]{:S(2)}, u32[]{:S(2)}) collective-permute-start(bf16[464,256]{1,0:T(8,128)(2,1)S(1)} %collective-permute-done.3.refs_2_), channel_id=1, source_target_pairs={{0,1},{1,0},{2,3},{3,2},{4,5},{5,4},{6,7},{7,6},{8,9},{9,8},{10,11... | collective-permute-start | bytes 712712 | tf_op jit(solution)/shard_map/ppermute | solution.py:386
  71.6 4.9 %collective-permute-start.21 = (bf16[320,128]{1,0:T(8,128)(2,1)S(1)}, bf16[320,128]{1,0:T(8,128)(2,1)S(1)}, u32[]{:S(2)}, u32[]{:S(2)}) collective-permute-start(bf16[320,128]{1,0:T(8,128)(2,1)S(1)} %pad_maximum_fusion.1.refs_2_.refs_0_), channel_id=1, source_target_pairs={{0,1},{1,0},{2,3},{3,2},{4,5},{5,4},{6,7},{7,6},{8,9},{9,8},{10,11... | collective-permute-start | bytes 245768 | tf_op jit(solution)/shard_map/ppermute | solution.py:386
  71.6 5.5 %collective-permute-start.27 = (bf16[320,128]{1,0:T(8,128)(2,1)S(1)}, bf16[320,128]{1,0:T(8,128)(2,1)S(1)}, u32[]{:S(2)}, u32[]{:S(2)}) collective-permute-start(bf16[320,128]{1,0:T(8,128)(2,1)S(1)} %collective-permute-done.26.refs_8_.refs_6_), channel_id=1, source_target_pairs={{0,1},{1,0},{2,3},{3,2},{4,5},{5,4},{6,7},{7,6},{8,9},{9,8},{10,11... | collective-permute-start | bytes 245768 | tf_op jit(solution)/shard_map/ppermute | solution.py:386
  72.1 5.6 %collective-permute-start.25 = (bf16[320,128]{1,0:T(8,128)(2,1)S(1)}, bf16[320,128]{1,0:T(8,128)(2,1)S(1)}, u32[]{:S(2)}, u32[]{:S(2)}) collective-permute-start(bf16[320,128]{1,0:T(8,128)(2,1)S(1)} %collective-permute-done.24.refs_6_.refs_4_), channel_id=1, source_target_pairs={{0,1},{1,0},{2,3},{3,2},{4,5},{5,4},{6,7},{7,6},{8,9},{9,8},{10,11... | collective-permute-start | bytes 245768 | tf_op jit(solution)/shard_map/ppermute | solution.py:386
  72.2 5.5 %collective-permute-start.23 = (bf16[320,128]{1,0:T(8,128)(2,1)S(1)}, bf16[320,128]{1,0:T(8,128)(2,1)S(1)}, u32[]{:S(2)}, u32[]{:S(2)}) collective-permute-start(bf16[320,128]{1,0:T(8,128)(2,1)S(1)} %collective-permute-done.22.refs_4_.refs_2_), channel_id=1, source_target_pairs={{0,1},{1,0},{2,3},{3,2},{4,5},{5,4},{6,7},{7,6},{8,9},{9,8},{10,11... | collective-permute-start | bytes 245768 | tf_op jit(solution)/shard_map/ppermute | solution.py:386
  72.7 21.5 %collective-permute-start.35 = (bf16[464,256]{1,0:T(8,128)(2,1)S(1)}, bf16[464,256]{1,0:T(8,128)(2,1)S(1)}, u32[]{:S(2)}, u32[]{:S(2)}) collective-permute-start(bf16[464,256]{1,0:T(8,128)(2,1)S(1)} %slice_convert_fusion.refs_0_.second_ref), channel_id=1, source_target_pairs={{0,6},{1,7},{2,4},{3,5},{4,2},{5,3},{6,0},{7,1},{8,14},{9,15},{10,... | collective-permute-start | bytes 712712 | tf_op jit(solution)/shard_map/ppermute | solution.py:386
  76.5 28.2 %collective-permute-start.33 = (bf16[464,256]{1,0:T(8,128)(2,1)S(1)}, bf16[464,256]{1,0:T(8,128)(2,1)S(1)}, u32[]{:S(2)}, u32[]{:S(2)}) collective-permute-start(bf16[464,256]{1,0:T(8,128)(2,1)S(1)} %slice_convert_fusion.refs_0_.second_ref), channel_id=1, source_target_pairs={{0,4},{1,5},{2,6},{3,7},{4,0},{5,1},{6,2},{7,3},{8,12},{9,13},{10,... | collective-permute-start | bytes 712712 | tf_op jit(solution)/shard_map/ppermute | solution.py:386
  77.1 28.0 %collective-permute-start.31 = (bf16[464,256]{1,0:T(8,128)(2,1)S(1)}, bf16[464,256]{1,0:T(8,128)(2,1)S(1)}, u32[]{:S(2)}, u32[]{:S(2)}) collective-permute-start(bf16[464,256]{1,0:T(8,128)(2,1)S(1)} %slice_convert_fusion.refs_0_.second_ref), channel_id=1, source_target_pairs={{0,2},{1,3},{2,0},{3,1},{4,6},{5,7},{6,4},{7,5},{8,10},{9,11},{10,... | collective-permute-start | bytes 712712 | tf_op jit(solution)/shard_map/ppermute | solution.py:386
  78.4 9.8 %collective-permute-start.38 = (f16[160,256]{1,0:T(8,128)(2,1)S(1)}, f16[160,256]{1,0:T(8,128)(2,1)S(1)}, u32[]{:S(2)}, u32[]{:S(2)}) collective-permute-start(f16[160,256]{1,0:T(8,128)(2,1)S(1)} %get-tuple-element.31), channel_id=1, source_target_pairs={{0,2},{1,3},{2,0},{3,1},{4,6},{5,7},{6,4},{7,5},{8,10},{9,11},{10,... | collective-permute-start | bytes 245768 | tf_op jit(solution)/shard_map/ppermute | solution.py:386
  79.9 8.9 %collective-permute-start.37 = (f16[160,256]{1,0:T(8,128)(2,1)S(1)}, f16[160,256]{1,0:T(8,128)(2,1)S(1)}, u32[]{:S(2)}, u32[]{:S(2)}) collective-permute-start(f16[160,256]{1,0:T(8,128)(2,1)S(1)} %get-tuple-element.31), channel_id=1, source_target_pairs={{0,1},{1,0},{2,3},{3,2},{4,5},{5,4},{6,7},{7,6},{8,9},{9,8},{10,11... | collective-permute-start | bytes 245768 | tf_op jit(solution)/shard_map/ppermute | solution.py:386
  88.2 4.4 %collective-permute-start.40 = (f16[160,256]{1,0:T(8,128)(2,1)S(1)}, f16[160,256]{1,0:T(8,128)(2,1)S(1)}, u32[]{:S(2)}, u32[]{:S(2)}) collective-permute-start(f16[160,256]{1,0:T(8,128)(2,1)S(1)} %get-tuple-element.31), channel_id=1, source_target_pairs={{0,4},{1,5},{2,6},{3,7},{4,0},{5,1},{6,2},{7,3},{8,12},{9,13},{10,... | collective-permute-start | bytes 245768 | tf_op jit(solution)/shard_map/ppermute | solution.py:386
  88.8 5.3 %collective-permute-start.39 = (f16[160,256]{1,0:T(8,128)(2,1)S(1)}, f16[160,256]{1,0:T(8,128)(2,1)S(1)}, u32[]{:S(2)}, u32[]{:S(2)}) collective-permute-start(f16[160,256]{1,0:T(8,128)(2,1)S(1)} %collective-permute-done.38), channel_id=1, source_target_pairs={{0,1},{1,0},{2,3},{3,2},{4,5},{5,4},{6,7},{7,6},{8,9},{9,8},{10,11... | collective-permute-start | bytes 245768 | tf_op jit(solution)/shard_map/ppermute | solution.py:386
  92.7 5.3 %collective-permute-start.42 = (f16[160,256]{1,0:T(8,128)(2,1)S(1)}, f16[160,256]{1,0:T(8,128)(2,1)S(1)}, u32[]{:S(2)}, u32[]{:S(2)}) collective-permute-start(f16[160,256]{1,0:T(8,128)(2,1)S(1)} %get-tuple-element.31), channel_id=1, source_target_pairs={{0,6},{1,7},{2,4},{3,5},{4,2},{5,3},{6,0},{7,1},{8,14},{9,15},{10,... | collective-permute-start | bytes 245768 | tf_op jit(solution)/shard_map/ppermute | solution.py:386
  94.1 3.9 %collective-permute-start.41 = (f16[160,256]{1,0:T(8,128)(2,1)S(1)}, f16[160,256]{1,0:T(8,128)(2,1)S(1)}, u32[]{:S(2)}, u32[]{:S(2)}) collective-permute-start(f16[160,256]{1,0:T(8,128)(2,1)S(1)} %collective-permute-done.40), channel_id=1, source_target_pairs={{0,1},{1,0},{2,3},{3,2},{4,5},{5,4},{6,7},{7,6},{8,9},{9,8},{10,11... | collective-permute-start | bytes 245768 | tf_op jit(solution)/shard_map/ppermute | solution.py:386
  94.2 16.7 %collective-permute-start.30 = (bf16[464,256]{1,0:T(8,128)(2,1)S(1)}, bf16[464,256]{1,0:T(8,128)(2,1)S(1)}, u32[]{:S(2)}, u32[]{:S(2)}) collective-permute-start(bf16[464,256]{1,0:T(8,128)(2,1)S(1)} %slice_convert_fusion.refs_0_.second_ref), channel_id=1, source_target_pairs={{0,1},{1,0},{2,3},{3,2},{4,5},{5,4},{6,7},{7,6},{8,9},{9,8},{10,11... | collective-permute-start | bytes 712712 | tf_op jit(solution)/shard_map/ppermute | solution.py:386
  98.0 14.2 %collective-permute-start.36 = (bf16[464,256]{1,0:T(8,128)(2,1)S(1)}, bf16[464,256]{1,0:T(8,128)(2,1)S(1)}, u32[]{:S(2)}, u32[]{:S(2)}) collective-permute-start(bf16[464,256]{1,0:T(8,128)(2,1)S(1)} %collective-permute-done.35.refs_6_), channel_id=1, source_target_pairs={{0,1},{1,0},{2,3},{3,2},{4,5},{5,4},{6,7},{7,6},{8,9},{9,8},{10,11... | collective-permute-start | bytes 712712 | tf_op jit(solution)/shard_map/ppermute | solution.py:386
  98.0 1.6 %collective-permute-start.43 = (f16[160,256]{1,0:T(8,128)(2,1)S(1)}, f16[160,256]{1,0:T(8,128)(2,1)S(1)}, u32[]{:S(2)}, u32[]{:S(2)}) collective-permute-start(f16[160,256]{1,0:T(8,128)(2,1)S(1)} %collective-permute-done.42), channel_id=1, source_target_pairs={{0,1},{1,0},{2,3},{3,2},{4,5},{5,4},{6,7},{7,6},{8,9},{9,8},{10,11... | collective-permute-start | bytes 245768 | tf_op jit(solution)/shard_map/ppermute | solution.py:386
  100.4 12.5 %copy-start.3 = (f32[2048,147]{0,1:T(8,128)S(1)}, f32[2048,147]{0,1:T(8,128)}, u32[]{:S(2)}) copy-start(f32[2048,147]{0,1:T(8,128)} %param.7) | copy-start | bytes 3612676
  100.4 12.5 %copy-start.4 = (f32[2048,147]{0,1:T(8,128)S(1)}, f32[2048,147]{0,1:T(8,128)}, u32[]{:S(2)}) copy-start(f32[2048,147]{0,1:T(8,128)} %param.8) | copy-start | bytes 3612676
  100.4 7.8 %collective-permute-start.46 = (bf16[80,128]{1,0:T(8,128)(2,1)S(1)}, bf16[80,128]{1,0:T(8,128)(2,1)S(1)}, u32[]{:S(2)}, u32[]{:S(2)}) collective-permute-start(bf16[80,128]{1,0:T(8,128)(2,1)S(1)} %shard_map.82), channel_id=1, source_target_pairs={{0,24},{1,25},{2,26},{3,27},{4,28},{5,29},{6,30},{7,31},{8,16},{9,... | collective-permute-start | bytes 61448 | tf_op jit(solution)/shard_map/ppermute | solution.py:386
  104.7 4.7 %collective-permute-start.45 = (bf16[80,128]{1,0:T(8,128)(2,1)S(1)}, bf16[80,128]{1,0:T(8,128)(2,1)S(1)}, u32[]{:S(2)}, u32[]{:S(2)}) collective-permute-start(bf16[80,128]{1,0:T(8,128)(2,1)S(1)} %shard_map.82), channel_id=1, source_target_pairs={{0,16},{1,17},{2,18},{3,19},{4,20},{5,21},{6,22},{7,23},{8,24},{9,... | collective-permute-start | bytes 61448 | tf_op jit(solution)/shard_map/ppermute | solution.py:386
  105.1 4.3 %collective-permute-start.44 = (bf16[80,128]{1,0:T(8,128)(2,1)S(1)}, bf16[80,128]{1,0:T(8,128)(2,1)S(1)}, u32[]{:S(2)}, u32[]{:S(2)}) collective-permute-start(bf16[80,128]{1,0:T(8,128)(2,1)S(1)} %shard_map.82), channel_id=1, source_target_pairs={{0,8},{1,9},{2,10},{3,11},{4,12},{5,13},{6,14},{7,15},{8,0},{9,1},... | collective-permute-start | bytes 61448 | tf_op jit(solution)/shard_map/ppermute | solution.py:386
  108.3 8.2 %collective-permute-start.34 = (bf16[464,256]{1,0:T(8,128)(2,1)S(1)}, bf16[464,256]{1,0:T(8,128)(2,1)S(1)}, u32[]{:S(2)}, u32[]{:S(2)}) collective-permute-start(bf16[464,256]{1,0:T(8,128)(2,1)S(1)} %collective-permute-done.33.refs_4_), channel_id=1, source_target_pairs={{0,1},{1,0},{2,3},{3,2},{4,5},{5,4},{6,7},{7,6},{8,9},{9,8},{10,11... | collective-permute-start | bytes 712712 | tf_op jit(solution)/shard_map/ppermute | solution.py:386
  109.4 8.2 %collective-permute-start.32 = (bf16[464,256]{1,0:T(8,128)(2,1)S(1)}, bf16[464,256]{1,0:T(8,128)(2,1)S(1)}, u32[]{:S(2)}, u32[]{:S(2)}) collective-permute-start(bf16[464,256]{1,0:T(8,128)(2,1)S(1)} %collective-permute-done.31.refs_2_), channel_id=1, source_target_pairs={{0,1},{1,0},{2,3},{3,2},{4,5},{5,4},{6,7},{7,6},{8,9},{9,8},{10,11... | collective-permute-start | bytes 712712 | tf_op jit(solution)/shard_map/ppermute | solution.py:386
  109.4 7.1 %collective-permute-start.52 = (bf16[320,128]{1,0:T(8,128)(2,1)S(1)}, bf16[320,128]{1,0:T(8,128)(2,1)S(1)}, u32[]{:S(2)}, u32[]{:S(2)}) collective-permute-start(bf16[320,128]{1,0:T(8,128)(2,1)S(1)} %pad_maximum_fusion.2.refs_1_), channel_id=1, source_target_pairs={{0,6},{1,7},{2,4},{3,5},{4,2},{5,3},{6,0},{7,1},{8,14},{9,15},{10,... | collective-permute-start | bytes 245768 | tf_op jit(solution)/shard_map/ppermute | solution.py:386
  110.9 6.2 %collective-permute-start.50 = (bf16[320,128]{1,0:T(8,128)(2,1)S(1)}, bf16[320,128]{1,0:T(8,128)(2,1)S(1)}, u32[]{:S(2)}, u32[]{:S(2)}) collective-permute-start(bf16[320,128]{1,0:T(8,128)(2,1)S(1)} %pad_maximum_fusion.2.refs_1_), channel_id=1, source_target_pairs={{0,4},{1,5},{2,6},{3,7},{4,0},{5,1},{6,2},{7,3},{8,12},{9,13},{10,... | collective-permute-start | bytes 245768 | tf_op jit(solution)/shard_map/ppermute | solution.py:386
  112.2 4.9 %collective-permute-start.48 = (bf16[320,128]{1,0:T(8,128)(2,1)S(1)}, bf16[320,128]{1,0:T(8,128)(2,1)S(1)}, u32[]{:S(2)}, u32[]{:S(2)}) collective-permute-start(bf16[320,128]{1,0:T(8,128)(2,1)S(1)} %pad_maximum_fusion.2.refs_1_), channel_id=1, source_target_pairs={{0,2},{1,3},{2,0},{3,1},{4,6},{5,7},{6,4},{7,5},{8,10},{9,11},{10,... | collective-permute-start | bytes 245768 | tf_op jit(solution)/shard_map/ppermute | solution.py:386
  116.5 5.8 %collective-permute-start.47 = (bf16[320,128]{1,0:T(8,128)(2,1)S(1)}, bf16[320,128]{1,0:T(8,128)(2,1)S(1)}, u32[]{:S(2)}, u32[]{:S(2)}) collective-permute-start(bf16[320,128]{1,0:T(8,128)(2,1)S(1)} %pad_maximum_fusion.2.refs_1_), channel_id=1, source_target_pairs={{0,1},{1,0},{2,3},{3,2},{4,5},{5,4},{6,7},{7,6},{8,9},{9,8},{10,11... | collective-permute-start | bytes 245768 | tf_op jit(solution)/shard_map/ppermute | solution.py:386
  116.5 5.7 %collective-permute-start.53 = (bf16[320,128]{1,0:T(8,128)(2,1)S(1)}, bf16[320,128]{1,0:T(8,128)(2,1)S(1)}, u32[]{:S(2)}, u32[]{:S(2)}) collective-permute-start(bf16[320,128]{1,0:T(8,128)(2,1)S(1)} %collective-permute-done.52.refs_7_), channel_id=1, source_target_pairs={{0,1},{1,0},{2,3},{3,2},{4,5},{5,4},{6,7},{7,6},{8,9},{9,8},{10,11... | collective-permute-start | bytes 245768 | tf_op jit(solution)/shard_map/ppermute | solution.py:386
  117.0 5.2 %collective-permute-start.51 = (bf16[320,128]{1,0:T(8,128)(2,1)S(1)}, bf16[320,128]{1,0:T(8,128)(2,1)S(1)}, u32[]{:S(2)}, u32[]{:S(2)}) collective-permute-start(bf16[320,128]{1,0:T(8,128)(2,1)S(1)} %collective-permute-done.50.refs_5_), channel_id=1, source_target_pairs={{0,1},{1,0},{2,3},{3,2},{4,5},{5,4},{6,7},{7,6},{8,9},{9,8},{10,11... | collective-permute-start | bytes 245768 | tf_op jit(solution)/shard_map/ppermute | solution.py:386
  117.1 5.1 %collective-permute-start.49 = (bf16[320,128]{1,0:T(8,128)(2,1)S(1)}, bf16[320,128]{1,0:T(8,128)(2,1)S(1)}, u32[]{:S(2)}, u32[]{:S(2)}) collective-permute-start(bf16[320,128]{1,0:T(8,128)(2,1)S(1)} %collective-permute-done.48.refs_3_), channel_id=1, source_target_pairs={{0,1},{1,0},{2,3},{3,2},{4,5},{5,4},{6,7},{7,6},{8,9},{9,8},{10,11... | collective-permute-start | bytes 245768 | tf_op jit(solution)/shard_map/ppermute | solution.py:386
